TPU v7x, 8 devices: a whole 2x2x1 slice. The times are simulated.
8 devices in a mesh: fsdp: 8 (over z, y, x, core).
Axes of the slice: x: 2, y: 2, z: 1, core: 2. Of those that a mesh axis runs over, the one named last changes fastest.
Arguments:
- x_saved: bfloat16 [2, 2, 8, 2048, 1024], P(None, None, 'fsdp')
- grad_out: bfloat16 [2, 8, 2048, 1024], P(None, 'fsdp')
- x_next: bfloat16 [2, 8, 2048, 1024], P(None, 'fsdp')
- w_up: bfloat16 [2, 2, 1024, 4096], replicated
- w_down: bfloat16 [2, 2, 4096, 1024], replicated
- acc_up: float32 [2, 2, 1024, 4096], P(None, None, 'fsdp')
- acc_down: float32 [2, 2, 4096, 1024], P(None, None, 'fsdp')
- master_up: float32 [2, 2, 1024, 4096], P(None, None, 'fsdp')
- master_down: float32 [2, 2, 4096, 1024], P(None, None, 'fsdp')
- moment1_up: float32 [2, 2, 1024, 4096], P(None, None, 'fsdp')
- moment1_down: float32 [2, 2, 4096, 1024], P(None, None, 'fsdp')
- moment2_up: float32 [2, 2, 1024, 4096], P(None, None, 'fsdp')
- moment2_down: float32 [2, 2, 4096, 1024], P(None, None, 'fsdp')
Outputs:
- output 1: float32 [2, 2, 1024, 4096], P(None, None, 'fsdp')
- output 2: float32 [2, 2, 4096, 1024], P(None, None, 'fsdp')
- output 3: float32 [2, 2, 1024, 4096], P(None, None, 'fsdp')
- output 4: float32 [2, 2, 4096, 1024], P(None, None, 'fsdp')
- output 5: float32 [2, 2, 1024, 4096], P(None, None, 'fsdp')
- output 6: float32 [2, 2, 4096, 1024], P(None, None, 'fsdp')
- output 7: bfloat16 [2, 8, 2048, 1024], P(None, 'fsdp')
All inputs are finite; a program needn't handle non-finite values.
Results may differ from a plain program's by a relative error of at most 0.00723387.
Values are sent between devices in bfloat16 or wider.
A program may use at most 1 GiB of HBM per device.

v0:
```python
import functools
import math

import jax
import jax.numpy as jnp
from jax import lax
from jax.experimental import pallas as pl
from jax.experimental.pallas import tpu as pltpu
from jax.sharding import PartitionSpec as P


LEARN_RATE = 0.005
BETA_ONE = 0.9
BETA_TWO = 0.95
ADAM_EPS = 1e-8
WEIGHT_DECAY = 0.1
MICROBATCHES = 2
ADAM_STEP = 2
CORR_ONE = 1.0 - BETA_ONE ** ADAM_STEP
CORR_TWO = 1.0 - BETA_TWO ** ADAM_STEP
GELU_C = math.sqrt(2.0 / math.pi)
GELU_K = 0.044715

D = 1024
FF = 4096
TOK = 2048
TM = 512
NB = TOK // TM
HALVES = 2
FC = FF // 2 // HALVES
BW = FC // 4
ROWS = D // 8
DROWS = FF // 8

F32 = jnp.float32
BF16 = jnp.bfloat16

ANY = pl.BlockSpec(memory_space=pl.ANY)


def dot(a, b, ca, cb):
    return lax.dot_general(a, b, (((ca,), (cb,)), ((), ())), preferred_element_type=F32)


def gelu_pair(h):
    hh = h * h
    t = jnp.tanh(h * (GELU_C + (GELU_C * GELU_K) * hh))
    cdf = 0.5 * t + 0.5
    grad = cdf + h * ((0.5 - 0.5 * (t * t)) * (GELU_C + (3.0 * GELU_C * GELU_K) * hh))
    return h * cdf, grad


def gelu(h):
    t = jnp.tanh(h * (GELU_C + (GELU_C * GELU_K) * (h * h)))
    return h * (0.5 * t + 0.5)


def bwd_kernel(stage, layer, half, mode, part, info, *refs):
    it = iter(refs)
    take = lambda k: [next(it) for _ in range(k)]
    xo, xp, do, dp, w_up, w_down = take(6)
    n_extra = {1: 0, 2: 1, 3: 2}[mode]
    extra_own, extra_par = take(n_extra), take(n_extra)
    sums_in = take(2) if part == "par" else None
    if part == "own":
        sums_out = take(2)
    else:
        outs_even, outs_odd = take(4), take(4)
    if mode != 3:
        dxo = next(it) if part != "par" else None
        dxp = next(it) if part != "own" else None
    xb, db, w1s, w2s, acc1, acc2, act, dhs, insem, wsem, ssem = take(11)
    eb, esem = take(2) if n_extra else (None, None)
    dxb, outsem = take(2) if mode != 3 else (None, None)
    i = pl.program_id(0)
    n = 2 * NB if part == "all" else NB
    base = NB if part == "par" else 0
    slot = lax.rem(i, 2)
    me = info[0]
    core = lax.rem(me, 2)
    chip = lax.div(me, 2)

    def in_copies(own, j, slot):
        rows = pl.ds(pl.multiple_of(j * TM, TM), TM)
        xs, ds, es = (xo, do, extra_own) if own else (xp, dp, extra_par)
        out = [pltpu.make_async_copy(xs.at[stage, layer, 0, rows], xb.at[slot], insem.at[0, slot]),
               pltpu.make_async_copy(ds.at[stage, 0, rows], db.at[slot], insem.at[1, slot])]
        for k, e in enumerate(es):
            out.append(pltpu.make_async_copy(e.at[rows], eb.at[k, slot], esem.at[k, slot]))
        return out

    def fetch(j, slot):
        @pl.when(j < NB)
        def _():
            for c in in_copies(True, j, slot):
                c.start()

        @pl.when(j >= NB)
        def _():
            for c in in_copies(False, j - NB, slot):
                c.start()

    def w_copies():
        out = []
        for j in range(4):
            f0 = pl.multiple_of(j * 1024 + core * 512 + half * BW, BW)
            out.append(pltpu.make_async_copy(w_up.at[stage, layer, :, pl.ds(f0, BW)], w1s.at[:, pl.ds(j * BW, BW)], wsem.at[0, j]))
            out.append(pltpu.make_async_copy(w_down.at[stage, layer, pl.ds(f0, BW), :], w2s.at[pl.ds(j * BW, BW), :], wsem.at[1, j]))
        return out

    @pl.when(i == 0)
    def _():
        fetch(base, 0)
        for c in w_copies():
            c.start()
        if part == "par":
            loads = [pltpu.make_async_copy(a, b, ssem.at[k]) for k, (a, b) in enumerate(zip(sums_in, (acc1, acc2)))]
            for c in loads:
                c.start()
            for c in loads:
                c.wait()
        else:
            acc1[...] = jnp.zeros_like(acc1)
            acc2[...] = jnp.zeros_like(acc2)
        for c in w_copies():
            c.wait()

    @pl.when(i + 1 < n)
    def _():
        fetch(base + i + 1, 1 - slot)

    for c in in_copies(True, 0, slot):
        c.wait()

    def dx_copy(own, j, slot):
        rows = pl.ds(pl.multiple_of(j * TM, TM), TM)
        return pltpu.make_async_copy(dxb.at[slot], (dxo if own else dxp).at[rows], outsem.at[slot])

    if mode != 3:
        @pl.when(i >= 2)
        def _():
            dx_copy(part != "par", 0, slot).wait()

    CH = 256
    n_ch = FC // CH
    x = xb[slot]
    dy = db[slot]
    if mode == 3:
        dy = (dy.astype(F32) + (eb[0, slot] + eb[1, slot])).astype(BF16)

    def front(c):
        cs = slice(c * CH, (c + 1) * CH)
        h = dot(x, w1s[:, cs], 1, 0)
        da = dot(dy, w2s[cs, :], 1, 1)
        g, grad = gelu_pair(h)
        act[:, cs] = g.astype(BF16)
        dhs[:, cs] = (da * grad).astype(BF16)

    def back(c):
        cs = slice(c * CH, (c + 1) * CH)
        acc1[:, cs] += dot(x, dhs[:, cs], 0, 0)
        acc2[cs, :] += dot(act[:, cs], dy, 0, 0)

    for c in range(n_ch):
        front(c)
    for c in range(n_ch):
        back(c)
    if mode != 3:
        dx = dot(dhs[...], w1s[...], 1, 1)
        if mode == 2:
            dx = dx + eb[0, slot]
        dxb[slot] = dx
        if part != "par":
            @pl.when(i < NB)
            def _():
                dx_copy(True, i, slot).start()

        if part != "own":
            @pl.when(i + base >= NB)
            def _():
                dx_copy(False, i + base - NB, slot).start()

    @pl.when(i == n - 1)
    def _():
        if part == "own":
            saves = [pltpu.make_async_copy(a, b, ssem.at[k]) for k, (a, b) in enumerate(zip((acc1, acc2), sums_out))]
            for c in saves:
                c.start()
            for c in saves:
                c.wait()
        else:
            for q in range(4):
                dev = jnp.bitwise_xor(me, 2 * q)
                oc = jnp.bitwise_xor(chip, q)
                outs_even[q][0:ROWS, :] = acc1[pl.ds(pl.multiple_of(dev * ROWS, ROWS), ROWS), :].astype(BF16)
                outs_even[q][ROWS:ROWS + BW, :] = acc2[pl.ds(pl.multiple_of(oc * BW, BW), BW), :].astype(BF16)
                dev = jnp.bitwise_xor(me, 2 * q + 1)
                outs_odd[q][...] = acc1[pl.ds(pl.multiple_of(dev * ROWS, ROWS), ROWS), :].astype(BF16)
        if mode != 3:
            dx_copy(part != "par", 0, 0).wait()
            dx_copy(part != "par", 0, 1).wait()


def bwd_call(stage, layer, half, mode, part, info, base_args, extra_own=(), extra_par=(), sums=()):
    sum_shapes = [jax.ShapeDtypeStruct((D, FC), F32), jax.ShapeDtypeStruct((FC, D), F32)]
    if part == "own":
        out_shape, out_specs = list(sum_shapes), [ANY] * 2
    else:
        out_shape = [jax.ShapeDtypeStruct((ROWS + BW, FC), BF16)] * 4 + [jax.ShapeDtypeStruct((ROWS, FC), BF16)] * 4
        out_specs = [pl.BlockSpec((ROWS + BW, FC), lambda i, s: (0, 0))] * 4 + [pl.BlockSpec((ROWS, FC), lambda i, s: (0, 0))] * 4
    scratch = [
        pltpu.VMEM((2, TM, D), BF16), pltpu.VMEM((2, TM, D), BF16),
        pltpu.VMEM((D, FC), BF16), pltpu.VMEM((FC, D), BF16),
        pltpu.VMEM((D, FC), F32), pltpu.VMEM((FC, D), F32),
        pltpu.VMEM((TM, FC), BF16), pltpu.VMEM((TM, FC), BF16),
        pltpu.SemaphoreType.DMA((2, 2)), pltpu.SemaphoreType.DMA((2, 4)), pltpu.SemaphoreType.DMA((2,)),
    ]
    args = list(base_args) + list(extra_own) + list(extra_par) + list(sums)
    n_extra = len(extra_own)
    if n_extra:
        scratch += [pltpu.VMEM((n_extra, 2, TM, D), F32), pltpu.SemaphoreType.DMA((n_extra, 2))]
    n_tok = 2 * TOK if part == "all" else TOK
    if mode != 3:
        k = 2 if part == "all" else 1
        out_shape += [jax.ShapeDtypeStruct((TOK, D), F32)] * k
        out_specs += [ANY] * k
        scratch += [pltpu.VMEM((2, TM, D), F32), pltpu.SemaphoreType.DMA((2,))]
    return pl.pallas_call(
        functools.partial(bwd_kernel, stage, layer, half, mode, part),
        out_shape=out_shape,
        grid_spec=pltpu.PrefetchScalarGridSpec(
            num_scalar_prefetch=1, grid=(n_tok // TM,), in_specs=[ANY] * len(args), out_specs=out_specs, scratch_shapes=scratch),
        compiler_params=pltpu.CompilerParams(dimension_semantics=("arbitrary",), vmem_limit_bytes=60 * 2 ** 20),
        cost_estimate=pl.CostEstimate(flops=2 * (4 if mode == 3 else 5) * n_tok * D * FC, bytes_accessed=n_tok * 10 * 2 ** 10, transcendentals=n_tok * FC),
    )(info, *args)


def adam(grad_new, acc, master, m1, m2):
    g = (acc + grad_new) / MICROBATCHES
    m1 = BETA_ONE * m1 + (1.0 - BETA_ONE) * g
    m2 = BETA_TWO * m2 + (1.0 - BETA_TWO) * g * g
    step_dir = (m1 * (1.0 / CORR_ONE)) / (jnp.sqrt(m2 * (1.0 / CORR_TWO)) + ADAM_EPS)
    master = master - LEARN_RATE * (step_dir + WEIGHT_DECAY * master)
    return master, m1, m2


def adam_kernel(n_alias, info, *refs):
    up = refs[:16]
    down = refs[16:24]
    au, mu, m1u, m2u, ad, md, m1d, m2d = refs[24:32]
    omu, om1u, om2u, omd, om1d, om2d, w_out = refs[32 + n_alias:]
    core = lax.rem(info[0], 2)
    j = pl.program_id(0)
    up_rows = pl.ds(pl.multiple_of(j * ROWS, ROWS), ROWS)
    for half in range(HALVES):
        for g in range(2):
            total = None
            for q in range(4):
                v = up[half * 8 + 2 * q + g][...].astype(F32)
                total = v if total is None else total + v
            col = jnp.bitwise_xor(core, g) * 512 + half * BW
            cs = pl.ds(pl.multiple_of(col, BW), BW)
            new = adam(total, au[0, 0, :, cs], mu[0, 0, :, cs], m1u[0, 0, :, cs], m2u[0, 0, :, cs])
            omu[0, 0, :, cs] = new[0]
            om1u[0, 0, :, cs] = new[1]
            om2u[0, 0, :, cs] = new[2]
            w_out[up_rows, cs] = new[0].astype(BF16)
        total = None
        for q in range(4):
            v = down[half * 4 + q][...].astype(F32)
            total = v if total is None else total + v
        new = adam(total, ad[0, 0, half], md[0, 0, half], m1d[0, 0, half], m2d[0, 0, half])
        omd[0, 0, half] = new[0]
        om1d[0, 0, half] = new[1]
        om2d[0, 0, half] = new[2]
        w_out[pl.ds(pl.multiple_of(DROWS + half * BW + j * (BW // 4), BW // 4), BW // 4), :] = new[0].astype(BF16)


def adam_call(stage, layer, info, recv, states, prev):
    nj = 4
    dr = BW // nj
    up_spec = pl.BlockSpec((ROWS, BW), lambda j, s: (0, j))
    down_spec = pl.BlockSpec((dr, D), lambda j, s: (ROWS // dr + j, 0))
    st_up = pl.BlockSpec((1, 1, ROWS, FF // nj), lambda j, s: (stage, layer, 0, j))
    st_down = pl.BlockSpec((1, 1, HALVES, dr, D), lambda j, s: (stage, layer, 0, j, 0))
    args, specs = [], []
    for half in range(HALVES):
        for r in range(8):
            args.append(recv[half][r])
            specs.append(up_spec)
    for half in range(HALVES):
        for q in range(4):
            args.append(recv[half][2 * q])
            specs.append(down_spec)
    args += list(states)
    specs += [st_up] * 4 + [st_down] * 4
    n_alias = len(prev)
    args += list(prev)
    specs += [ANY] * n_alias
    up_shape = jax.ShapeDtypeStruct(states[0].shape, F32)
    down_shape = jax.ShapeDtypeStruct(states[4].shape, F32)
    n_in = 1 + len(args) - n_alias
    return pl.pallas_call(
        functools.partial(adam_kernel, n_alias),
        out_shape=[up_shape] * 3 + [down_shape] * 3 + [jax.ShapeDtypeStruct((2 * DROWS, D), BF16)],
        grid_spec=pltpu.PrefetchScalarGridSpec(
            num_scalar_prefetch=1, grid=(nj,), in_specs=specs,
            out_specs=[st_up] * 3 + [st_down] * 3 + [pl.BlockSpec((2 * DROWS, D), lambda j, s: (0, 0))]),
        input_output_aliases={n_in + k: k for k in range(n_alias)},
        compiler_params=pltpu.CompilerParams(dimension_semantics=("arbitrary",), vmem_limit_bytes=60 * 2 ** 20),
        cost_estimate=pl.CostEstimate(flops=20 * 2 ** 20 * 40, bytes_accessed=40 * 2 ** 20, transcendentals=2 ** 20),
    )(info, *args)


def fwd_kernel(has_alias, *refs):
    x_ref, w = refs[:2]
    o_ref, w1s, w2s, sem = refs[2 + has_alias:]
    i = pl.program_id(0)
    CH = DROWS
    n_ch = FF // CH

    def copies(c):
        out = []
        for d in range(8):
            src = w.at[pl.ds(2 * DROWS * d + (c // 2) * ROWS, ROWS), pl.ds((c % 2) * CH, CH)]
            out.append(pltpu.make_async_copy(src, w1s.at[pl.ds(d * ROWS, ROWS), pl.ds(c * CH, CH)], sem.at[0, c]))
        out.append(pltpu.make_async_copy(w.at[pl.ds(2 * DROWS * c + DROWS, CH), :], w2s.at[pl.ds(c * CH, CH), :], sem.at[1, c]))
        return out

    def run(wait):
        x = x_ref[...].reshape(TM, D)
        acc = None
        for c in range(n_ch):
            if wait:
                for cp in copies(c):
                    cp.wait()
            cs = pl.ds(c * CH, CH)
            a = gelu(dot(x, w1s[:, cs], 1, 0)).astype(BF16)
            part = dot(a, w2s[cs, :], 1, 0)
            acc = part if acc is None else acc + part
        o_ref[...] = (x.astype(F32) + acc).astype(BF16).reshape(o_ref.shape)

    @pl.when(i == 0)
    def _():
        for c in range(n_ch):
            for cp in copies(c):
                cp.start()
        run(True)

    @pl.when(i > 0)
    def _():
        run(False)


def fwd_call(stage, layer, x, w, y_prev):
    if layer == 0:
        x_spec = pl.BlockSpec((1, 1, TM, D), lambda i: (stage, 0, i, 0))
        out_shape = jax.ShapeDtypeStruct((TOK, D), BF16)
        o_spec = pl.BlockSpec((TM, D), lambda i: (i, 0))
    else:
        x_spec = pl.BlockSpec((TM, D), lambda i: (i, 0))
        out_shape = jax.ShapeDtypeStruct((2, 1, TOK, D), BF16)
        o_spec = pl.BlockSpec((1, 1, TM, D), lambda i: (stage, 0, i, 0))
    args = [x, w]
    specs = [x_spec, ANY]
    aliases = {}
    if y_prev is not None:
        args.append(y_prev)
        specs.append(ANY)
        aliases = {2: 0}
    return pl.pallas_call(
        functools.partial(fwd_kernel, len(args) - 2),
        out_shape=out_shape,
        grid_spec=pltpu.PrefetchScalarGridSpec(
            num_scalar_prefetch=0, grid=(NB,), in_specs=specs, out_specs=o_spec,
            scratch_shapes=[pltpu.VMEM((D, FF), BF16), pltpu.VMEM((FF, D), BF16), pltpu.SemaphoreType.DMA((2, FF // DROWS))]),
        input_output_aliases=aliases,
        compiler_params=pltpu.CompilerParams(dimension_semantics=("arbitrary",), vmem_limit_bytes=60 * 2 ** 20),
        cost_estimate=pl.CostEstimate(flops=4 * TOK * D * FF, bytes_accessed=26 * 2 ** 20, transcendentals=TOK * FF),
    )(*args)


SEQ = ("bwd_010a", "bwd_010b", "bwd_011", "bwd_110", "adam_01", "bwd_000", "bwd_111", "bwd_001", "bwd_100", "adam_00", "bwd_101", "adam_11", "fwd_00", "adam_10", "fwd_01", "fwd_10", "fwd_11")


def solution(mesh):
    tok_spec = P(None, 'fsdp')
    layer_spec = P(None, None, 'fsdp')
    n_dev = mesh.shape['fsdp']

    def swap(a, r):
        return lax.ppermute(a, 'fsdp', [(d, d ^ r) for d in range(n_dev)])

    def gather(a):
        return lax.all_gather(a, 'fsdp', axis=0, tiled=True)

    def device_step(x_saved, grad_out, x_next, w_up, w_down, acc_up, acc_down, master_up, master_down, moment1_up, moment1_down, moment2_up, moment2_down):
        me = lax.axis_index('fsdp').astype(jnp.int32)
        info = me.reshape(1)

        g_par = swap(grad_out, 1)
        x_par = swap(x_saved, 1)
        base_own = (x_saved, x_saved, grad_out, grad_out, w_up, w_down)
        base = (x_saved, x_par, grad_out, g_par, w_up, w_down)

        down5 = lambda a: a.reshape(2, 2, HALVES, BW, D)
        states = (acc_up, master_up, moment1_up, moment2_up, down5(acc_down), down5(master_down), down5(moment1_down), down5(moment2_down))

        recv = {}
        dx = {}
        outs6 = ()
        full = {}
        hid = {}
        y = None

        for name in SEQ:
            s, l = int(name.split("_")[1][0]), int(name.split("_")[1][1])
            if name.startswith("adam"):
                res = adam_call(s, l, info, recv[s, l], states, outs6)
                outs6 = tuple(res[:6])
                full[s, l] = gather(res[6])
                continue
            if name.startswith("fwd"):
                if l == 0:
                    hid[s] = fwd_call(s, 0, x_next, full[s, 0], None)
                else:
                    y = fwd_call(s, 1, hid[s], full[s, 1], y)
                continue
            half = int(name[6])
            if name == "bwd_010a":
                sum1, sum2, dx_own = bwd_call(s, l, half, 1, "own", info, base_own)
                continue
            if name == "bwd_010b":
                outs = bwd_call(s, l, half, 1, "par", info, base, sums=(sum1, sum2))
                dx[s] = (dx_own, outs[8])
            elif l == 0:
                (own, par), (got_own, got_par) = dx[s]
                outs = bwd_call(s, l, half, 3, "all", info, base, (own, got_own), (par, got_par))
            elif half == 0:
                outs = bwd_call(s, l, half, 1, "all", info, base)
                dx[s] = tuple(outs[8:])
            else:
                own, par = dx[s]
                outs = bwd_call(s, l, half, 2, "all", info, base, (own,), (par,))
                own, par = outs[8:]
                dx[s] = ((own, par), (swap(par, 1), swap(own, 1)))
            msgs = [outs[0], outs[4], outs[1], outs[5], outs[2], outs[6], outs[3], outs[7]]
            recv.setdefault((s, l), []).append([msgs[0]] + [swap(msgs[r], r) for r in range(1, 8)])

        up4 = lambda a: a.reshape(2, 2, DROWS, D)
        return (outs6[0], up4(outs6[3]), outs6[1], up4(outs6[4]), outs6[2], up4(outs6[5]), y)

    return jax.shard_map(device_step, mesh=mesh, in_specs=(layer_spec, tok_spec, tok_spec, P(), P()) + (layer_spec,) * 8, out_specs=(layer_spec,) * 6 + (tok_spec,), check_vma=False)
```

profile of v0, /device:TPU:0, one launch (start us, length us, event | category | flops | bytes accessed | tf_op | source)
XLA Modules:
  0.0 1159.8 jit_solution(16239367808193128309)
XLA Ops:
  8.1 30.2 %shard_map.184 = (f32[1024,1024]{1,0:T(8,128)}, f32[1024,1024]{1,0:T(8,128)}, f32[2048,1024]{1,0:T(8,128)}) custom-call(s32[1]{0:T(128)} %bitcast.info, bf16[2,2,1,2048,1024]{4,3,2,1,0:T(8,128)(2,1)} %refs_0_.19, bf16[2,2,1,2048,1024]{4,3,2,1,0:T(8,128)(2,1)} %refs_0_.19, bf16[2,1,2048,1024]{3,2,1,0:T(8,128)(2,1)} %refs_2_.17, ...), custom_call_target="tpu_custom_call" | custom-call | flops 21474836480 | bytes 20971520 | tf_op jit(solution)/shard_map/pallas_call | solution.py:228
  45.2 33.5 %shard_map.185 = (bf16[384,1024]{1,0:T(8,128)(2,1)}, bf16[384,1024]{1,0:T(8,128)(2,1)}, bf16[384,1024]{1,0:T(8,128)(2,1)}, bf16[384,1024]{1,0:T(8,128)(2,1)}, bf...) custom-call(s32[1]{0:T(128)} %bitcast.info, ...), custom_call_target="tpu_custom_call" | custom-call | flops 21474836480 | bytes 20971520 | tf_op jit(solution)/shard_map/pallas_call | solution.py:228
  82.9 56.0 %shard_map.186 = (bf16[384,1024]{1,0:T(8,128)(2,1)}, bf16[384,1024]{1,0:T(8,128)(2,1)}, bf16[384,1024]{1,0:T(8,128)(2,1)}, bf16[384,1024]{1,0:T(8,128)(2,1)}, bf...) custom-call(s32[1]{0:T(128)} %bitcast.info, ...), custom_call_target="tpu_custom_call" | custom-call | flops 42949672960 | bytes 41943040 | tf_op jit(solution)/shard_map/pallas_call | solution.py:228
  141.5 55.4 %shard_map.180 = (bf16[384,1024]{1,0:T(8,128)(2,1)}, bf16[384,1024]{1,0:T(8,128)(2,1)}, bf16[384,1024]{1,0:T(8,128)(2,1)}, bf16[384,1024]{1,0:T(8,128)(2,1)}, bf...) custom-call(s32[1]{0:T(128)} %bitcast.info, ...), custom_call_target="tpu_custom_call" | custom-call | flops 42949672960 | bytes 41943040 | tf_op jit(solution)/shard_map/pallas_call | solution.py:228
  198.7 12.2 %collective-permute-done.59.refs_13_ = bf16[128,1024]{1,0:T(8,128)(2,1)S(1)} collective-permute-done((bf16[128,1024]{1,0:T(8,128)(2,1)S(1)}, bf16[128,1024]{1,0:T(8,128)(2,1)S(1)}, u32[]{:S(2)}, u32[]{:S(2)}) %collective-permute-start.59) | collective-permute-done | bytes 262176 | tf_op jit(solution)/shard_map/ppermute | solution.py:392
  214.6 56.5 %shard_map.181 = (bf16[384,1024]{1,0:T(8,128)(2,1)}, bf16[384,1024]{1,0:T(8,128)(2,1)}, bf16[384,1024]{1,0:T(8,128)(2,1)}, bf16[384,1024]{1,0:T(8,128)(2,1)}, bf...) custom-call(s32[1]{0:T(128)} %bitcast.info, ...), custom_call_target="tpu_custom_call" | custom-call | flops 42949672960 | bytes 41943040 | tf_op jit(solution)/shard_map/pallas_call | solution.py:228
  283.0 20.6 %collective-permute-done.31.refs_15_ = bf16[128,1024]{1,0:T(8,128)(2,1)S(1)} collective-permute-done((bf16[128,1024]{1,0:T(8,128)(2,1)}, bf16[128,1024]{1,0:T(8,128)(2,1)S(1)}, u32[]{:S(2)}, u32[]{:S(2)}) %collective-permute-start.31) | collective-permute-done | bytes 262176 | tf_op jit(solution)/shard_map/ppermute | solution.py:392
  307.4 17.6 %collective-permute-done.53.refs_6_.refs_19_ = bf16[384,1024]{1,0:T(8,128)(2,1)} collective-permute-done((bf16[384,1024]{1,0:T(8,128)(2,1)S(1)}, bf16[384,1024]{1,0:T(8,128)(2,1)}, u32[]{:S(2)}, u32[]{:S(2)}) %collective-permute-start.53) | collective-permute-done | bytes 786464 | tf_op jit(solution)/shard_map/ppermute | solution.py:392
  325.1 15.8 %collective-permute-done.56.refs_10_.refs_21_ = bf16[384,1024]{1,0:T(8,128)(2,1)S(1)} collective-permute-done((bf16[384,1024]{1,0:T(8,128)(2,1)}, bf16[384,1024]{1,0:T(8,128)(2,1)S(1)}, u32[]{:S(2)}, u32[]{:S(2)}) %collective-permute-start.56) | collective-permute-done | bytes 786464 | tf_op jit(solution)/shard_map/ppermute | solution.py:392
  341.7 16.1 %collective-permute-done.60.refs_14_.refs_23_ = bf16[384,1024]{1,0:T(8,128)(2,1)S(1)} collective-permute-done((bf16[384,1024]{1,0:T(8,128)(2,1)S(1)}, bf16[384,1024]{1,0:T(8,128)(2,1)S(1)}, u32[]{:S(2)}, u32[]{:S(2)}) %collective-permute-start.60) | collective-permute-done | bytes 786464 | tf_op jit(solution)/shard_map/ppermute | solution.py:392
  358.4 18.5 %collective-permute-done.19.refs_2_.refs_17_ = bf16[384,1024]{1,0:T(8,128)(2,1)} collective-permute-done((bf16[384,1024]{1,0:T(8,128)(2,1)}, bf16[384,1024]{1,0:T(8,128)(2,1)}, u32[]{:S(2)}, u32[]{:S(2)}) %collective-permute-start.19) | collective-permute-done | bytes 786464 | tf_op jit(solution)/shard_map/ppermute | solution.py:392
  377.4 17.7 %collective-permute-done.21.refs_4_.refs_18_ = bf16[384,1024]{1,0:T(8,128)(2,1)} collective-permute-done((bf16[384,1024]{1,0:T(8,128)(2,1)}, bf16[384,1024]{1,0:T(8,128)(2,1)}, u32[]{:S(2)}, u32[]{:S(2)}) %collective-permute-start.21) | collective-permute-done | bytes 786464 | tf_op jit(solution)/shard_map/ppermute | solution.py:392
  398.6 46.5 %shard_map.188 = (bf16[384,1024]{1,0:T(8,128)(2,1)}, bf16[384,1024]{1,0:T(8,128)(2,1)}, bf16[384,1024]{1,0:T(8,128)(2,1)}, bf16[384,1024]{1,0:T(8,128)(2,1)}, bf...) custom-call(s32[1]{0:T(128)} %bitcast.info, ...), custom_call_target="tpu_custom_call" | custom-call | flops 34359738368 | bytes 41943040 | tf_op jit(solution)/shard_map/pallas_call | solution.py:228
  447.3 46.3 %shard_map.187 = (bf16[384,1024]{1,0:T(8,128)(2,1)}, bf16[384,1024]{1,0:T(8,128)(2,1)}, bf16[384,1024]{1,0:T(8,128)(2,1)}, bf16[384,1024]{1,0:T(8,128)(2,1)}, bf...) custom-call(s32[1]{0:T(128)} %bitcast.info, ...), custom_call_target="tpu_custom_call" | custom-call | flops 34359738368 | bytes 41943040 | tf_op jit(solution)/shard_map/pallas_call | solution.py:228
  498.2 46.8 %shard_map.183 = (bf16[384,1024]{1,0:T(8,128)(2,1)}, bf16[384,1024]{1,0:T(8,128)(2,1)}, bf16[384,1024]{1,0:T(8,128)(2,1)}, bf16[384,1024]{1,0:T(8,128)(2,1)}, bf...) custom-call(s32[1]{0:T(128)} %bitcast.info, ...), custom_call_target="tpu_custom_call" | custom-call | flops 34359738368 | bytes 41943040 | tf_op jit(solution)/shard_map/pallas_call | solution.py:228
  552.2 46.3 %shard_map.182 = (bf16[384,1024]{1,0:T(8,128)(2,1)}, bf16[384,1024]{1,0:T(8,128)(2,1)}, bf16[384,1024]{1,0:T(8,128)(2,1)}, bf16[384,1024]{1,0:T(8,128)(2,1)}, bf...) custom-call(s32[1]{0:T(128)} %bitcast.info, ...), custom_call_target="tpu_custom_call" | custom-call | flops 34359738368 | bytes 41943040 | tf_op jit(solution)/shard_map/pallas_call | solution.py:228
  622.8 21.9 %collective-permute-done.8.refs_5_ = bf16[128,1024]{1,0:T(8,128)(2,1)S(1)} collective-permute-done((bf16[128,1024]{1,0:T(8,128)(2,1)}, bf16[128,1024]{1,0:T(8,128)(2,1)S(1)}, u32[]{:S(2)}, u32[]{:S(2)}) %collective-permute-start.8) | collective-permute-done | bytes 262176 | tf_op jit(solution)/shard_map/ppermute | solution.py:392
  650.3 15.5 %collective-permute-done.35.refs_2_.refs_17_ = bf16[384,1024]{1,0:T(8,128)(2,1)S(1)} collective-permute-done((bf16[384,1024]{1,0:T(8,128)(2,1)S(1)}, bf16[384,1024]{1,0:T(8,128)(2,1)S(1)}, u32[]{:S(2)}, u32[]{:S(2)}) %collective-permute-start.35) | collective-permute-done | bytes 786464 | tf_op jit(solution)/shard_map/ppermute | solution.py:392
  665.9 17.8 %collective-permute-done.37.refs_4_.refs_18_ = bf16[384,1024]{1,0:T(8,128)(2,1)S(1)} collective-permute-done((bf16[384,1024]{1,0:T(8,128)(2,1)}, bf16[384,1024]{1,0:T(8,128)(2,1)S(1)}, u32[]{:S(2)}, u32[]{:S(2)}) %collective-permute-start.37) | collective-permute-done | bytes 786464 | tf_op jit(solution)/shard_map/ppermute | solution.py:392
  685.9 13.7 %collective-permute-done.12.refs_10_.refs_21_ = bf16[384,1024]{1,0:T(8,128)(2,1)S(1)} collective-permute-done((bf16[384,1024]{1,0:T(8,128)(2,1)}, bf16[384,1024]{1,0:T(8,128)(2,1)S(1)}, u32[]{:S(2)}, u32[]{:S(2)}) %collective-permute-start.12) | collective-permute-done | bytes 786464 | tf_op jit(solution)/shard_map/ppermute | solution.py:392
  699.7 14.3 %shard_map.189 = (f32[2,2,128,4096]{3,2,1,0:T(8,128)}, f32[2,2,128,4096]{3,2,1,0:T(8,128)}, f32[2,2,128,4096]{3,2,1,0:T(8,128)}, f32[2,2,2,256,1024]{4,3,2,1,0:T...) custom-call(s32[1]{0:T(128)} %bitcast.info, ...), custom_call_target="tpu_custom_call" | custom-call | flops 838860800 | bytes 41943040 | tf_op jit(solution)/shard_map/pallas_call | solution.py:303
  713.9 14.2 %shard_map.190 = (f32[2,2,128,4096]{3,2,1,0:T(8,128)}, f32[2,2,128,4096]{3,2,1,0:T(8,128)}, f32[2,2,128,4096]{3,2,1,0:T(8,128)}, f32[2,2,2,256,1024]{4,3,2,1,0:T...) custom-call(s32[1]{0:T(128)} %bitcast.info, ...), custom_call_target="tpu_custom_call", output_to_operand_aliasing={{0}: (33, {}), {1}: (34, {}), {2}: (35, {}), {3}: (36, {}),... | custom-call | flops 838860800 | bytes 41943040 | tf_op jit(solution)/shard_map/pallas_call | solution.py:303
  728.1 14.2 %shard_map.191 = (f32[2,2,128,4096]{3,2,1,0:T(8,128)}, f32[2,2,128,4096]{3,2,1,0:T(8,128)}, f32[2,2,128,4096]{3,2,1,0:T(8,128)}, f32[2,2,2,256,1024]{4,3,2,1,0:T...) custom-call(s32[1]{0:T(128)} %bitcast.info, ...), custom_call_target="tpu_custom_call", output_to_operand_aliasing={{0}: (33, {}), {1}: (34, {}), {2}: (35, {}), {3}: (36, {}),... | custom-call | flops 838860800 | bytes 41943040 | tf_op jit(solution)/shard_map/pallas_call | solution.py:303
  750.9 14.2 %shard_map.192 = (f32[2,2,128,4096]{3,2,1,0:T(8,128)}, f32[2,2,128,4096]{3,2,1,0:T(8,128)}, f32[2,2,128,4096]{3,2,1,0:T(8,128)}, f32[2,2,2,256,1024]{4,3,2,1,0:T...) custom-call(s32[1]{0:T(128)} %bitcast.info, ...), custom_call_target="tpu_custom_call", output_to_operand_aliasing={{0}: (33, {}), {1}: (34, {}), {2}: (35, {}), {3}: (36, {}),... | custom-call | flops 838860800 | bytes 41943040 | tf_op jit(solution)/shard_map/pallas_call | solution.py:303
  767.2 82.3 %all-gather.5.cloned.1.call-done.refs_1_ = bf16[8192,1024]{1,0:T(8,128)(2,1)} async-done(((bf16[1024,1024]{1,0:T(8,128)(2,1)}), bf16[8192,1024]{1,0:T(8,128)(2,1)}) %all-gather.5.cloned.1.call-update) | async-done | bytes 16777232 | tf_op jit(solution)/shard_map/all_gather | solution.py:395
  849.4 45.0 %shard_map.193.refs_0_ = bf16[2048,1024]{1,0:T(8,128)(2,1)} custom-call(bf16[2,1,2048,1024]{3,2,1,0:T(8,128)(2,1)} %refs_0_.21, bf16[8192,1024]{1,0:T(8,128)(2,1)} %all-gather.5.cloned.1.call-done.refs_1_), custom_call_target="tpu_custom_call" | custom-call | flops 34359738368 | bytes 27262976 | tf_op jit(solution)/shard_map/pallas_call | solution.py:371
  894.4 41.0 %all-gather.9.cloned.1.call-done.refs_1_ = bf16[8192,1024]{1,0:T(8,128)(2,1)} async-done(((bf16[1024,1024]{1,0:T(8,128)(2,1)}), bf16[8192,1024]{1,0:T(8,128)(2,1)}) %all-gather.9.cloned.1.call-update) | async-done | bytes 16777232 | tf_op jit(solution)/shard_map/all_gather | solution.py:395
  935.5 45.1 %shard_map.194.refs_0_ = bf16[2048,1024]{1,0:T(8,128)(2,1)} custom-call(bf16[2,1,2048,1024]{3,2,1,0:T(8,128)(2,1)} %refs_0_.21, bf16[8192,1024]{1,0:T(8,128)(2,1)} %all-gather.9.cloned.1.call-done.refs_1_), custom_call_target="tpu_custom_call" | custom-call | flops 34359738368 | bytes 27262976 | tf_op jit(solution)/shard_map/pallas_call | solution.py:371
  980.6 41.5 %all-gather.11.cloned.1.call-done.refs_1_ = bf16[8192,1024]{1,0:T(8,128)(2,1)} async-done(((bf16[1024,1024]{1,0:T(8,128)(2,1)}), bf16[8192,1024]{1,0:T(8,128)(2,1)}) %all-gather.11.cloned.1.call-update) | async-done | bytes 16777232 | tf_op jit(solution)/shard_map/all_gather | solution.py:395
  1022.1 44.9 %shard_map.195.refs_2_ = bf16[2,1,2048,1024]{3,2,1,0:T(8,128)(2,1)} custom-call(bf16[2048,1024]{1,0:T(8,128)(2,1)} %shard_map.194.refs_0_, bf16[8192,1024]{1,0:T(8,128)(2,1)} %all-gather.11.cloned.1.call-done.refs_1_), custom_call_target="tpu_custom_call" | custom-call | flops 34359738368 | bytes 27262976 | tf_op jit(solution)/shard_map/pallas_call | solution.py:371
  1067.0 41.0 %all-gather.7.cloned.1.call-done.refs_1_ = bf16[8192,1024]{1,0:T(8,128)(2,1)} async-done(((bf16[1024,1024]{1,0:T(8,128)(2,1)}), bf16[8192,1024]{1,0:T(8,128)(2,1)}) %all-gather.7.cloned.1.call-update) | async-done | bytes 16777232 | tf_op jit(solution)/shard_map/all_gather | solution.py:395
  1107.9 45.0 %shard_map.196 = bf16[2,1,2048,1024]{3,2,1,0:T(8,128)(2,1)} custom-call(bf16[2048,1024]{1,0:T(8,128)(2,1)} %shard_map.193.refs_0_, bf16[8192,1024]{1,0:T(8,128)(2,1)} %all-gather.7.cloned.1.call-done.refs_1_, bf16[2,1,2048,1024]{3,2,1,0:T(8,128)(2,1)} %shard_map.195.refs_2_), custom_call_target="tpu_custom_call", output_to_operand_aliasing={{}: (2, {})} | custom-call | flops 34359738368 | bytes 27262976 | tf_op jit(solution)/shard_map/pallas_call | solution.py:371
  (231 shorter events, 97.4 us)
Async XLA Ops:
  7.2 842.3 %all-gather.5.cloned.1.call-start = ((), (), s32[]{:S(2)}) async-start(), calls=%async_computation | async-start | bytes 18874368 | tf_op jit(solution)/shard_map/all_gather | solution.py:395
  78.7 60.6 %collective-permute-start.48 = (bf16[128,1024]{1,0:T(8,128)(2,1)}, bf16[128,1024]{1,0:T(8,128)(2,1)S(1)}, u32[]{:S(2)}, u32[]{:S(2)}) collective-permute-start(bf16[128,1024]{1,0:T(8,128)(2,1)} %get-tuple-element.168), channel_id=1, source_target_pairs={{0,1},{1,0},{2,3},{3,2},{4,5},{5,4},{6,7},{7,6}} | collective-permute-start | bytes 786440 | tf_op jit(solution)/shard_map/ppermute | solution.py:392
  79.1 61.9 %collective-permute-start.50 = (bf16[128,1024]{1,0:T(8,128)(2,1)}, bf16[128,1024]{1,0:T(8,128)(2,1)S(1)}, u32[]{:S(2)}, u32[]{:S(2)}) collective-permute-start(bf16[128,1024]{1,0:T(8,128)(2,1)} %get-tuple-element.170), channel_id=1, source_target_pairs={{0,3},{1,2},{2,1},{3,0},{4,7},{5,6},{6,5},{7,4}} | collective-permute-start | bytes 786440 | tf_op jit(solution)/shard_map/ppermute | solution.py:392
  81.7 59.5 %collective-permute-start.52 = (bf16[128,1024]{1,0:T(8,128)(2,1)}, bf16[128,1024]{1,0:T(8,128)(2,1)S(1)}, u32[]{:S(2)}, u32[]{:S(2)}) collective-permute-start(bf16[128,1024]{1,0:T(8,128)(2,1)} %get-tuple-element.172), channel_id=1, source_target_pairs={{0,5},{1,4},{2,7},{3,6},{4,1},{5,0},{6,3},{7,2}} | collective-permute-start | bytes 786440 | tf_op jit(solution)/shard_map/ppermute | solution.py:392
  82.9 114.0 %collective-permute-start.54 = (bf16[128,1024]{1,0:T(8,128)(2,1)}, bf16[128,1024]{1,0:T(8,128)(2,1)S(1)}, u32[]{:S(2)}, u32[]{:S(2)}) collective-permute-start(bf16[128,1024]{1,0:T(8,128)(2,1)} %get-tuple-element.174), channel_id=1, source_target_pairs={{0,7},{1,6},{2,5},{3,4},{4,3},{5,2},{6,1},{7,0}} | collective-permute-start | bytes 786440 | tf_op jit(solution)/shard_map/ppermute | solution.py:392
  138.9 59.4 %collective-permute-start.55 = (bf16[128,1024]{1,0:T(8,128)(2,1)}, bf16[128,1024]{1,0:T(8,128)(2,1)S(1)}, u32[]{:S(2)}, u32[]{:S(2)}) collective-permute-start(bf16[128,1024]{1,0:T(8,128)(2,1)} %get-tuple-element.176), channel_id=1, source_target_pairs={{0,1},{1,0},{2,3},{3,2},{4,5},{5,4},{6,7},{7,6}} | collective-permute-start | bytes 786440 | tf_op jit(solution)/shard_map/ppermute | solution.py:392
  139.3 59.0 %collective-permute-start.57 = (bf16[128,1024]{1,0:T(8,128)(2,1)}, bf16[128,1024]{1,0:T(8,128)(2,1)S(1)}, u32[]{:S(2)}, u32[]{:S(2)}) collective-permute-start(bf16[128,1024]{1,0:T(8,128)(2,1)} %get-tuple-element.178), channel_id=1, source_target_pairs={{0,3},{1,2},{2,1},{3,0},{4,7},{5,6},{6,5},{7,4}} | collective-permute-start | bytes 786440 | tf_op jit(solution)/shard_map/ppermute | solution.py:392
  141.0 255.0 %collective-permute-start.33 = (f32[2048,1024]{1,0:T(8,128)}, f32[2048,1024]{1,0:T(8,128)}, u32[]{:S(2)}, u32[]{:S(2)}) collective-permute-start(f32[2048,1024]{1,0:T(8,128)} %get-tuple-element.149.refs_6_), channel_id=1, source_target_pairs={{0,1},{1,0},{2,3},{3,2},{4,5},{5,4},{6,7},{7,6}} | collective-permute-start | bytes 25165832 | tf_op jit(solution)/shard_map/ppermute | solution.py:392
  141.1 256.0 %collective-permute-start.32 = (f32[2048,1024]{1,0:T(8,128)}, f32[2048,1024]{1,0:T(8,128)}, u32[]{:S(2)}, u32[]{:S(2)}) collective-permute-start(f32[2048,1024]{1,0:T(8,128)} %get-tuple-element.150.refs_8_), channel_id=1, source_target_pairs={{0,1},{1,0},{2,3},{3,2},{4,5},{5,4},{6,7},{7,6}} | collective-permute-start | bytes 25165832 | tf_op jit(solution)/shard_map/ppermute | solution.py:392
  210.9 60.3 %collective-permute-start.20 = (bf16[128,1024]{1,0:T(8,128)(2,1)}, bf16[128,1024]{1,0:T(8,128)(2,1)S(1)}, u32[]{:S(2)}, u32[]{:S(2)}) collective-permute-start(bf16[128,1024]{1,0:T(8,128)(2,1)} %get-tuple-element.132), channel_id=1, source_target_pairs={{0,3},{1,2},{2,1},{3,0},{4,7},{5,6},{6,5},{7,4}} | collective-permute-start | bytes 786440 | tf_op jit(solution)/shard_map/ppermute | solution.py:392
  211.7 59.9 %collective-permute-start.22 = (bf16[128,1024]{1,0:T(8,128)(2,1)}, bf16[128,1024]{1,0:T(8,128)(2,1)S(1)}, u32[]{:S(2)}, u32[]{:S(2)}) collective-permute-start(bf16[128,1024]{1,0:T(8,128)(2,1)} %get-tuple-element.134), channel_id=1, source_target_pairs={{0,5},{1,4},{2,7},{3,6},{4,1},{5,0},{6,3},{7,2}} | collective-permute-start | bytes 786440 | tf_op jit(solution)/shard_map/ppermute | solution.py:392
  213.4 58.2 %collective-permute-start.24 = (bf16[128,1024]{1,0:T(8,128)(2,1)}, bf16[128,1024]{1,0:T(8,128)(2,1)S(1)}, u32[]{:S(2)}, u32[]{:S(2)}) collective-permute-start(bf16[128,1024]{1,0:T(8,128)(2,1)} %get-tuple-element.136), channel_id=1, source_target_pairs={{0,7},{1,6},{2,5},{3,4},{4,3},{5,2},{6,1},{7,0}} | collective-permute-start | bytes 786440 | tf_op jit(solution)/shard_map/ppermute | solution.py:392
  340.9 154.0 %collective-permute-start.3 = (f32[2048,1024]{1,0:T(8,128)}, f32[2048,1024]{1,0:T(8,128)}, u32[]{:S(2)}, u32[]{:S(2)}) collective-permute-start(f32[2048,1024]{1,0:T(8,128)} %get-tuple-element.111.refs_6_), channel_id=1, source_target_pairs={{0,1},{1,0},{2,3},{3,2},{4,5},{5,4},{6,7},{7,6}} | collective-permute-start | bytes 25165832 | tf_op jit(solution)/shard_map/ppermute | solution.py:392
  341.7 154.0 %collective-permute-start.2 = (f32[2048,1024]{1,0:T(8,128)}, f32[2048,1024]{1,0:T(8,128)}, u32[]{:S(2)}, u32[]{:S(2)}) collective-permute-start(f32[2048,1024]{1,0:T(8,128)} %get-tuple-element.112.refs_8_), channel_id=1, source_target_pairs={{0,1},{1,0},{2,3},{3,2},{4,5},{5,4},{6,7},{7,6}} | collective-permute-start | bytes 25165832 | tf_op jit(solution)/shard_map/ppermute | solution.py:392
  396.0 50.0 %collective-permute-start.26 = (bf16[384,1024]{1,0:T(8,128)(2,1)}, bf16[384,1024]{1,0:T(8,128)(2,1)S(1)}, u32[]{:S(2)}, u32[]{:S(2)}) collective-permute-start(bf16[384,1024]{1,0:T(8,128)(2,1)} %get-tuple-element.139), channel_id=1, source_target_pairs={{0,2},{1,3},{2,0},{3,1},{4,6},{5,7},{6,4},{7,5}} | collective-permute-start | bytes 2359304 | tf_op jit(solution)/shard_map/ppermute | solution.py:392
  446.0 51.0 %collective-permute-start.43 = (bf16[128,1024]{1,0:T(8,128)(2,1)}, bf16[128,1024]{1,0:T(8,128)(2,1)S(1)}, u32[]{:S(2)}, u32[]{:S(2)}) collective-permute-start(bf16[128,1024]{1,0:T(8,128)(2,1)} %get-tuple-element.162), channel_id=1, source_target_pairs={{0,3},{1,2},{2,1},{3,0},{4,7},{5,6},{6,5},{7,4}} | collective-permute-start | bytes 786440 | tf_op jit(solution)/shard_map/ppermute | solution.py:392
  493.7 51.4 %collective-permute-start.45 = (bf16[128,1024]{1,0:T(8,128)(2,1)}, bf16[128,1024]{1,0:T(8,128)(2,1)S(1)}, u32[]{:S(2)}, u32[]{:S(2)}) collective-permute-start(bf16[128,1024]{1,0:T(8,128)(2,1)} %get-tuple-element.164), channel_id=1, source_target_pairs={{0,5},{1,4},{2,7},{3,6},{4,1},{5,0},{6,3},{7,2}} | collective-permute-start | bytes 786440 | tf_op jit(solution)/shard_map/ppermute | solution.py:392
  494.9 51.1 %collective-permute-start.47 = (bf16[128,1024]{1,0:T(8,128)(2,1)S(1)}, bf16[128,1024]{1,0:T(8,128)(2,1)S(1)}, u32[]{:S(2)}, u32[]{:S(2)}) collective-permute-start(bf16[128,1024]{1,0:T(8,128)(2,1)S(1)} %copy-done.52), channel_id=1, source_target_pairs={{0,7},{1,6},{2,5},{3,4},{4,3},{5,2},{6,1},{7,0}} | collective-permute-start | bytes 786440 | tf_op jit(solution)/shard_map/ppermute | solution.py:392
  495.8 52.1 %collective-permute-start.34 = (bf16[128,1024]{1,0:T(8,128)(2,1)}, bf16[128,1024]{1,0:T(8,128)(2,1)S(1)}, u32[]{:S(2)}, u32[]{:S(2)}) collective-permute-start(bf16[128,1024]{1,0:T(8,128)(2,1)} %get-tuple-element.152), channel_id=1, source_target_pairs={{0,1},{1,0},{2,3},{3,2},{4,5},{5,4},{6,7},{7,6}} | collective-permute-start | bytes 786440 | tf_op jit(solution)/shard_map/ppermute | solution.py:392
  495.8 54.3 %collective-permute-start.36 = (bf16[128,1024]{1,0:T(8,128)(2,1)}, bf16[128,1024]{1,0:T(8,128)(2,1)S(1)}, u32[]{:S(2)}, u32[]{:S(2)}) collective-permute-start(bf16[128,1024]{1,0:T(8,128)(2,1)} %get-tuple-element.154), channel_id=1, source_target_pairs={{0,3},{1,2},{2,1},{3,0},{4,7},{5,6},{6,5},{7,4}} | collective-permute-start | bytes 786440 | tf_op jit(solution)/shard_map/ppermute | solution.py:392
  497.1 53.8 %collective-permute-start.38 = (bf16[128,1024]{1,0:T(8,128)(2,1)}, bf16[128,1024]{1,0:T(8,128)(2,1)S(1)}, u32[]{:S(2)}, u32[]{:S(2)}) collective-permute-start(bf16[128,1024]{1,0:T(8,128)(2,1)} %get-tuple-element.156), channel_id=1, source_target_pairs={{0,5},{1,4},{2,7},{3,6},{4,1},{5,0},{6,3},{7,2}} | collective-permute-start | bytes 786440 | tf_op jit(solution)/shard_map/ppermute | solution.py:392
  545.1 53.4 %collective-permute-start.40 = (bf16[128,1024]{1,0:T(8,128)(2,1)}, bf16[128,1024]{1,0:T(8,128)(2,1)S(1)}, u32[]{:S(2)}, u32[]{:S(2)}) collective-permute-start(bf16[128,1024]{1,0:T(8,128)(2,1)} %get-tuple-element.158), channel_id=1, source_target_pairs={{0,7},{1,6},{2,5},{3,4},{4,3},{5,2},{6,1},{7,0}} | collective-permute-start | bytes 786440 | tf_op jit(solution)/shard_map/ppermute | solution.py:392
  546.7 99.7 %collective-permute-start.42 = (bf16[384,1024]{1,0:T(8,128)(2,1)}, bf16[384,1024]{1,0:T(8,128)(2,1)S(1)}, u32[]{:S(2)}, u32[]{:S(2)}) collective-permute-start(bf16[384,1024]{1,0:T(8,128)(2,1)} %get-tuple-element.161), channel_id=1, source_target_pairs={{0,2},{1,3},{2,0},{3,1},{4,6},{5,7},{6,4},{7,5}} | collective-permute-start | bytes 2359304 | tf_op jit(solution)/shard_map/ppermute | solution.py:392
  548.6 101.0 %collective-permute-start.44 = (bf16[384,1024]{1,0:T(8,128)(2,1)}, bf16[384,1024]{1,0:T(8,128)(2,1)S(1)}, u32[]{:S(2)}, u32[]{:S(2)}) collective-permute-start(bf16[384,1024]{1,0:T(8,128)(2,1)} %get-tuple-element.163), channel_id=1, source_target_pairs={{0,4},{1,5},{2,6},{3,7},{4,0},{5,1},{6,2},{7,3}} | collective-permute-start | bytes 2359304 | tf_op jit(solution)/shard_map/ppermute | solution.py:392
  649.7 92.6 %collective-permute-start.14 = (bf16[384,1024]{1,0:T(8,128)(2,1)}, bf16[384,1024]{1,0:T(8,128)(2,1)S(1)}, u32[]{:S(2)}, u32[]{:S(2)}) collective-permute-start(bf16[384,1024]{1,0:T(8,128)(2,1)} %get-tuple-element.125), channel_id=1, source_target_pairs={{0,4},{1,5},{2,6},{3,7},{4,0},{5,1},{6,2},{7,3}} | collective-permute-start | bytes 2359304 | tf_op jit(solution)/shard_map/ppermute | solution.py:392
  665.8 76.5 %collective-permute-start.16 = (bf16[384,1024]{1,0:T(8,128)(2,1)}, bf16[384,1024]{1,0:T(8,128)(2,1)S(1)}, u32[]{:S(2)}, u32[]{:S(2)}) collective-permute-start(bf16[384,1024]{1,0:T(8,128)(2,1)} %get-tuple-element.127), channel_id=1, source_target_pairs={{0,6},{1,7},{2,4},{3,5},{4,2},{5,3},{6,0},{7,1}} | collective-permute-start | bytes 2359304 | tf_op jit(solution)/shard_map/ppermute | solution.py:392
  683.6 58.7 %collective-permute-start.5 = (bf16[384,1024]{1,0:T(8,128)(2,1)}, bf16[384,1024]{1,0:T(8,128)(2,1)}, u32[]{:S(2)}, u32[]{:S(2)}) collective-permute-start(bf16[384,1024]{1,0:T(8,128)(2,1)} %get-tuple-element.115), channel_id=1, source_target_pairs={{0,2},{1,3},{2,0},{3,1},{4,6},{5,7},{6,4},{7,5}} | collective-permute-start | bytes 2359304 | tf_op jit(solution)/shard_map/ppermute | solution.py:392
  685.7 65.2 %collective-permute-start.7 = (bf16[384,1024]{1,0:T(8,128)(2,1)}, bf16[384,1024]{1,0:T(8,128)(2,1)}, u32[]{:S(2)}, u32[]{:S(2)}) collective-permute-start(bf16[384,1024]{1,0:T(8,128)(2,1)} %get-tuple-element.117), channel_id=1, source_target_pairs={{0,4},{1,5},{2,6},{3,7},{4,0},{5,1},{6,2},{7,3}} | collective-permute-start | bytes 2359304 | tf_op jit(solution)/shard_map/ppermute | solution.py:392
  699.6 51.2 %collective-permute-start.9 = (bf16[384,1024]{1,0:T(8,128)(2,1)}, bf16[384,1024]{1,0:T(8,128)(2,1)}, u32[]{:S(2)}, u32[]{:S(2)}) collective-permute-start(bf16[384,1024]{1,0:T(8,128)(2,1)} %get-tuple-element.119), channel_id=1, source_target_pairs={{0,6},{1,7},{2,4},{3,5},{4,2},{5,3},{6,0},{7,1}} | collective-permute-start | bytes 2359304 | tf_op jit(solution)/shard_map/ppermute | solution.py:392
  765.1 170.4 %all-gather.9.cloned.1.call-start = ((), (), s32[]{:S(2)}) async-start(), calls=%async_computation.2 | async-start | bytes 18874368 | tf_op jit(solution)/shard_map/all_gather | solution.py:395
  765.9 256.2 %all-gather.11.cloned.1.call-start = ((), (), s32[]{:S(2)}) async-start(), calls=%async_computation.3 | async-start | bytes 18874368 | tf_op jit(solution)/shard_map/all_gather | solution.py:395
  766.6 341.4 %all-gather.7.cloned.1.call-start = ((), (), s32[]{:S(2)}) async-start(), calls=%async_computation.1 | async-start | bytes 18874368 | tf_op jit(solution)/shard_map/all_gather | solution.py:395
  (89 other events, 3428.6 us)
Sparse Core Ops, SparseCore 0:
  765.2 84.1 all-gather.4
  851.3 84.1 all-gather.8
  937.9 84.1 all-gather.10
  1023.7 84.1 all-gather.6
where the time goes:
time: 1170 us; the launch traced here: 1160 us
  Pallas kernels  654 us (56%)
  waiting for transfers between devices  434 us (37%)
  starting transfers between devices  51.4 us (4%)
  between operations  14.9 us (1%)
    pallas_call x9, Pallas kernels, bwd_call(): pl.pallas_call(functools.partial(bwd_kernel, stage, layer, half, mode, pa...  418 us
    ppermute x62, waiting for transfers between devices, swap(): return lax.ppermute(a, 'fsdp', [(d, d ^ r) for d in range(n_dev)])  226 us
    all_gather x4, waiting for transfers between devices, gather(): return lax.all_gather(a, 'fsdp', axis=0, tiled=True)  206 us
    pallas_call x4, Pallas kernels, fwd_call(): pl.pallas_call(functools.partial(fwd_kernel, len(args) - 2), out_shape=ou...  180 us
    pallas_call x4, Pallas kernels, adam_call(): pl.pallas_call(functools.partial(adam_kernel, n_alias), out_shape=[up_sha...  56.9 us
    ppermute x62, starting transfers between devices, swap(): return lax.ppermute(a, 'fsdp', [(d, d ^ r) for d in range(n_dev)])  51.3 us
  transfers between devices with their start and end apart: 66, of which 22 were waited for; matrix products, arithmetic and copies ran while one was open for 0% of the time, Pallas kernels for 48%

commit v1 on v0

--- a/solution.py
+++ b/solution.py
@@ -59,7 +59,7 @@
     it = iter(refs)
     take = lambda k: [next(it) for _ in range(k)]
     xo, xp, do, dp, w_up, w_down = take(6)
-    n_extra = {1: 0, 2: 1, 3: 2}[mode]
+    n_extra = {1: 0, 3: 2}[mode]
     extra_own, extra_par = take(n_extra), take(n_extra)
     sums_in = take(2) if part == "par" else None
     if part == "own":
@@ -67,11 +67,11 @@
     else:
         outs_even, outs_odd = take(4), take(4)
     if mode != 3:
-        dxo = next(it) if part != "par" else None
-        dxp = next(it) if part != "own" else None
+        dho = next(it) if part != "par" else None
+        dhp = next(it) if part != "own" else None
     xb, db, w1s, w2s, acc1, acc2, act, dhs, insem, wsem, ssem = take(11)
     eb, esem = take(2) if n_extra else (None, None)
-    dxb, outsem = take(2) if mode != 3 else (None, None)
+    outsem = next(it) if mode != 3 else None
     i = pl.program_id(0)
     n = 2 * NB if part == "all" else NB
     base = NB if part == "par" else 0
@@ -132,14 +132,14 @@
     for c in in_copies(True, 0, slot):
         c.wait()
 
-    def dx_copy(own, j, slot):
+    def dh_copy(own, j, slot):
         rows = pl.ds(pl.multiple_of(j * TM, TM), TM)
-        return pltpu.make_async_copy(dxb.at[slot], (dxo if own else dxp).at[rows], outsem.at[slot])
+        return pltpu.make_async_copy(dhs.at[slot], (dho if own else dhp).at[rows], outsem.at[slot])
 
     if mode != 3:
         @pl.when(i >= 2)
         def _():
-            dx_copy(part != "par", 0, slot).wait()
+            dh_copy(part != "par", 0, slot).wait()
 
     CH = 256
     n_ch = FC // CH
@@ -154,11 +154,11 @@
         da = dot(dy, w2s[cs, :], 1, 1)
         g, grad = gelu_pair(h)
         act[:, cs] = g.astype(BF16)
-        dhs[:, cs] = (da * grad).astype(BF16)
+        dhs[slot, :, cs] = (da * grad).astype(BF16)
 
     def back(c):
         cs = slice(c * CH, (c + 1) * CH)
-        acc1[:, cs] += dot(x, dhs[:, cs], 0, 0)
+        acc1[:, cs] += dot(x, dhs[slot, :, cs], 0, 0)
         acc2[cs, :] += dot(act[:, cs], dy, 0, 0)
 
     for c in range(n_ch):
@@ -166,19 +166,15 @@
     for c in range(n_ch):
         back(c)
     if mode != 3:
-        dx = dot(dhs[...], w1s[...], 1, 1)
-        if mode == 2:
-            dx = dx + eb[0, slot]
-        dxb[slot] = dx
         if part != "par":
             @pl.when(i < NB)
             def _():
-                dx_copy(True, i, slot).start()
+                dh_copy(True, i, slot).start()
 
         if part != "own":
             @pl.when(i + base >= NB)
             def _():
-                dx_copy(False, i + base - NB, slot).start()
+                dh_copy(False, i + base - NB, slot).start()
 
     @pl.when(i == n - 1)
     def _():
@@ -197,8 +193,8 @@
                 dev = jnp.bitwise_xor(me, 2 * q + 1)
                 outs_odd[q][...] = acc1[pl.ds(pl.multiple_of(dev * ROWS, ROWS), ROWS), :].astype(BF16)
         if mode != 3:
-            dx_copy(part != "par", 0, 0).wait()
-            dx_copy(part != "par", 0, 1).wait()
+            dh_copy(part != "par", 0, 0).wait()
+            dh_copy(part != "par", 0, 1).wait()
 
 
 def bwd_call(stage, layer, half, mode, part, info, base_args, extra_own=(), extra_par=(), sums=()):
@@ -212,7 +208,7 @@
         pltpu.VMEM((2, TM, D), BF16), pltpu.VMEM((2, TM, D), BF16),
         pltpu.VMEM((D, FC), BF16), pltpu.VMEM((FC, D), BF16),
         pltpu.VMEM((D, FC), F32), pltpu.VMEM((FC, D), F32),
-        pltpu.VMEM((TM, FC), BF16), pltpu.VMEM((TM, FC), BF16),
+        pltpu.VMEM((TM, FC), BF16), pltpu.VMEM((2, TM, FC), BF16),
         pltpu.SemaphoreType.DMA((2, 2)), pltpu.SemaphoreType.DMA((2, 4)), pltpu.SemaphoreType.DMA((2,)),
     ]
     args = list(base_args) + list(extra_own) + list(extra_par) + list(sums)
@@ -222,16 +218,99 @@
     n_tok = 2 * TOK if part == "all" else TOK
     if mode != 3:
         k = 2 if part == "all" else 1
-        out_shape += [jax.ShapeDtypeStruct((TOK, D), F32)] * k
+        out_shape += [jax.ShapeDtypeStruct((TOK, FC), BF16)] * k
         out_specs += [ANY] * k
-        scratch += [pltpu.VMEM((2, TM, D), F32), pltpu.SemaphoreType.DMA((2,))]
+        scratch += [pltpu.SemaphoreType.DMA((2,))]
     return pl.pallas_call(
         functools.partial(bwd_kernel, stage, layer, half, mode, part),
         out_shape=out_shape,
         grid_spec=pltpu.PrefetchScalarGridSpec(
             num_scalar_prefetch=1, grid=(n_tok // TM,), in_specs=[ANY] * len(args), out_specs=out_specs, scratch_shapes=scratch),
         compiler_params=pltpu.CompilerParams(dimension_semantics=("arbitrary",), vmem_limit_bytes=60 * 2 ** 20),
-        cost_estimate=pl.CostEstimate(flops=2 * (4 if mode == 3 else 5) * n_tok * D * FC, bytes_accessed=n_tok * 10 * 2 ** 10, transcendentals=n_tok * FC),
+        cost_estimate=pl.CostEstimate(flops=8 * n_tok * D * FC, bytes_accessed=n_tok * 10 * 2 ** 10, transcendentals=n_tok * FC),
+    )(info, *args)
+
+
+def dx_kernel(stage, layer, info, h0o, h0p, h1o, h1p, w_up, dxo, dxp, dhb, w1s, dxb, insem, wsem, outsem):
+    i = pl.program_id(0)
+    n = 2 * NB
+    slot = lax.rem(i, 2)
+    core = lax.rem(info[0], 2)
+
+    def in_copies(own, j, slot):
+        rows = pl.ds(pl.multiple_of(j * TM, TM), TM)
+        pair = (h0o, h1o) if own else (h0p, h1p)
+        return [pltpu.make_async_copy(a.at[rows], dhb.at[slot, :, pl.ds(k * FC, FC)], insem.at[k, slot]) for k, a in enumerate(pair)]
+
+    def fetch(j, slot):
+        @pl.when(j < NB)
+        def _():
+            for c in in_copies(False, j, slot):
+                c.start()
+
+        @pl.when(j >= NB)
+        def _():
+            for c in in_copies(True, j - NB, slot):
+                c.start()
+
+    def w_copies():
+        out = []
+        for half in range(HALVES):
+            for j in range(4):
+                f0 = pl.multiple_of(j * 1024 + core * 512 + half * BW, BW)
+                out.append(pltpu.make_async_copy(w_up.at[stage, layer, :, pl.ds(f0, BW)], w1s.at[:, pl.ds(half * FC + j * BW, BW)], wsem.at[half, j]))
+        return out
+
+    def out_copy(own, j, slot):
+        rows = pl.ds(pl.multiple_of(j * TM, TM), TM)
+        return pltpu.make_async_copy(dxb.at[slot], (dxo if own else dxp).at[rows], outsem.at[slot])
+
+    @pl.when(i == 0)
+    def _():
+        fetch(0, 0)
+        for c in w_copies():
+            c.start()
+        for c in w_copies():
+            c.wait()
+
+    @pl.when(i + 1 < n)
+    def _():
+        fetch(i + 1, 1 - slot)
+
+    for c in in_copies(True, 0, slot):
+        c.wait()
+
+    @pl.when(i >= 2)
+    def _():
+        out_copy(True, 0, slot).wait()
+
+    dxb[slot] = dot(dhb[slot], w1s[...], 1, 1)
+
+    @pl.when(i < NB)
+    def _():
+        out_copy(False, i, slot).start()
+
+    @pl.when(i >= NB)
+    def _():
+        out_copy(True, i - NB, slot).start()
+
+    @pl.when(i == n - 1)
+    def _():
+        out_copy(True, 0, 0).wait()
+        out_copy(True, 0, 1).wait()
+
+
+def dx_call(stage, layer, info, dh0, dh1, w_up):
+    args = [dh0[0], dh0[1], dh1[0], dh1[1], w_up]
+    return pl.pallas_call(
+        functools.partial(dx_kernel, stage, layer),
+        out_shape=[jax.ShapeDtypeStruct((TOK, D), F32)] * 2,
+        grid_spec=pltpu.PrefetchScalarGridSpec(
+            num_scalar_prefetch=1, grid=(2 * NB,), in_specs=[ANY] * 5, out_specs=[ANY] * 2,
+            scratch_shapes=[pltpu.VMEM((2, TM, HALVES * FC), BF16), pltpu.VMEM((D, HALVES * FC), BF16), pltpu.VMEM((2, TM, D), F32),
+                            pltpu.SemaphoreType.DMA((2, 2)), pltpu.SemaphoreType.DMA((2, 4)), pltpu.SemaphoreType.DMA((2,))]),
+        compiler_params=pltpu.CompilerParams(dimension_semantics=("arbitrary",), vmem_limit_bytes=60 * 2 ** 20),
+        cost_estimate=pl.CostEstimate(flops=4 * TOK * D * HALVES * FC, bytes_accessed=38 * 2 ** 20, transcendentals=0),
     )(info, *args)
 
 
@@ -380,7 +459,7 @@
     )(*args)
 
 
-SEQ = ("bwd_010a", "bwd_010b", "bwd_011", "bwd_110", "adam_01", "bwd_000", "bwd_111", "bwd_001", "bwd_100", "adam_00", "bwd_101", "adam_11", "fwd_00", "adam_10", "fwd_01", "fwd_10", "fwd_11")
+SEQ = ("bwd_010a", "bwd_010b", "bwd_011", "bwd_110", "adam_01", "dx_01", "bwd_111", "bwd_000", "dx_11", "bwd_001", "bwd_100", "adam_00", "bwd_101", "adam_11", "adam_10", "fwd_00", "fwd_01", "fwd_10", "fwd_11")
 
 
 def solution(mesh):
@@ -408,8 +487,10 @@
 
         recv = {}
         dx = {}
+        dh = {}
         outs6 = ()
         full = {}
+        w_new = {}
         hid = {}
         y = None
 
@@ -418,7 +499,11 @@
             if name.startswith("adam"):
                 res = adam_call(s, l, info, recv[s, l], states, outs6)
                 outs6 = tuple(res[:6])
-                full[s, l] = gather(res[6])
+                w_new[s, l] = res[6]
+                if (s, l) != (1, 1):
+                    full[s, l] = gather(res[6])
+                if (s, l) == (1, 0):
+                    full[1, 1] = gather(lax.optimization_barrier((w_new[1, 1], res[6]))[0])
                 continue
             if name.startswith("fwd"):
                 if l == 0:
@@ -426,24 +511,22 @@
                 else:
                     y = fwd_call(s, 1, hid[s], full[s, 1], y)
                 continue
+            if name.startswith("dx"):
+                own, par = dx_call(s, l, info, dh[s, 0], dh[s, 1], w_up)
+                dx[s] = ((own, swap(par, 1)), (par, swap(own, 1)))
+                continue
             half = int(name[6])
             if name == "bwd_010a":
-                sum1, sum2, dx_own = bwd_call(s, l, half, 1, "own", info, base_own)
+                sum1, sum2, dh_own = bwd_call(s, l, half, 1, "own", info, base_own)
                 continue
             if name == "bwd_010b":
                 outs = bwd_call(s, l, half, 1, "par", info, base, sums=(sum1, sum2))
-                dx[s] = (dx_own, outs[8])
+                dh[s, half] = (dh_own, outs[8])
             elif l == 0:
-                (own, par), (got_own, got_par) = dx[s]
-                outs = bwd_call(s, l, half, 3, "all", info, base, (own, got_own), (par, got_par))
-            elif half == 0:
+                outs = bwd_call(s, l, half, 3, "all", info, base, *dx[s])
+            else:
                 outs = bwd_call(s, l, half, 1, "all", info, base)
-                dx[s] = tuple(outs[8:])
-            else:
-                own, par = dx[s]
-                outs = bwd_call(s, l, half, 2, "all", info, base, (own,), (par,))
-                own, par = outs[8:]
-                dx[s] = ((own, par), (swap(par, 1), swap(own, 1)))
+                dh[s, half] = tuple(outs[8:])
             msgs = [outs[0], outs[4], outs[1], outs[5], outs[2], outs[6], outs[3], outs[7]]
             recv.setdefault((s, l), []).append([msgs[0]] + [swap(msgs[r], r) for r in range(1, 8)])
 

time: 1170 us -> 1160 us (level)
  waiting for transfers between devices: 434 us -> 410 us
  Pallas kernels: 654 us -> 666 us
    pallas_call x0 -> x2, Pallas kernels: none -> 47.3 us  [dx_call(): pl.pallas_call(functools.partial(dx_kernel, stage, layer), out_shape=[jax...]
    pallas_call x9, Pallas kernels: 418 us -> 383 us  [bwd_call(): pl.pallas_call(functools.partial(bwd_kernel, stage, layer, half, mode, pa...]
    ppermute x62, waiting for transfers between devices: 226 us -> 202 us  [swap(): return lax.ppermute(a, 'fsdp', [(d, d ^ r) for d in range(n_dev)])]
  transfers between devices with their start and end apart: 66 -> 66, of which waited for: 22 -> 22; matrix products, arithmetic and copies ran while one was open for 0% -> 0% of each run, Pallas kernels for 48% -> 50%
where the time goes in v1:
time: 1160 us; the launch traced here: 1150 us
  Pallas kernels  666 us (57%)
  waiting for transfers between devices  410 us (35%)
  starting transfers between devices  60.8 us (5%)
  between operations  14.9 us (1%)
    pallas_call x9, Pallas kernels, bwd_call(): pl.pallas_call(functools.partial(bwd_kernel, stage, layer, half, mode, pa...  383 us
    all_gather x4, waiting for transfers between devices, gather(): return lax.all_gather(a, 'fsdp', axis=0, tiled=True)  206 us
    ppermute x62, waiting for transfers between devices, swap(): return lax.ppermute(a, 'fsdp', [(d, d ^ r) for d in range(n_dev)])  202 us
    pallas_call x4, Pallas kernels, fwd_call(): pl.pallas_call(functools.partial(fwd_kernel, len(args) - 2), out_shape=ou...  180 us
    ppermute x62, starting transfers between devices, swap(): return lax.ppermute(a, 'fsdp', [(d, d ^ r) for d in range(n_dev)])  60.6 us
    pallas_call x4, Pallas kernels, adam_call(): pl.pallas_call(functools.partial(adam_kernel, n_alias), out_shape=[up_sha...  56.6 us
    pallas_call x2, Pallas kernels, dx_call(): pl.pallas_call(functools.partial(dx_kernel, stage, layer), out_shape=[jax...  47.3 us
  transfers between devices with their start and end apart: 66, of which 22 were waited for; matrix products, arithmetic and copies ran while one was open for 0% of the time, Pallas kernels for 50%

profile of v1, /device:TPU:0, one launch (start us, length us, event | category | flops | bytes accessed | tf_op | source)
XLA Modules:
  0.0 1152.4 jit_solution(9174320828754547368)
XLA Ops:
  8.1 26.4 %shard_map.185 = (f32[1024,1024]{1,0:T(8,128)}, f32[1024,1024]{1,0:T(8,128)}, bf16[2048,1024]{1,0:T(8,128)(2,1)}) custom-call(s32[1]{0:T(128)} %bitcast.info, bf16[2,2,1,2048,1024]{4,3,2,1,0:T(8,128)(2,1)} %refs_0_.19, bf16[2,2,1,2048,1024]{4,3,2,1,0:T(8,128)(2,1)} %refs_0_.19, bf16[2,1,2048,1024]{3,2,1,0:T(8,128)(2,1)} %refs_2_.17, ...), custom_call_target="tpu_custom_call" | custom-call | flops 17179869184 | bytes 20971520 | tf_op jit(solution)/shard_map/pallas_call | solution.py:224
  45.2 28.1 %shard_map.186 = (bf16[384,1024]{1,0:T(8,128)(2,1)}, bf16[384,1024]{1,0:T(8,128)(2,1)}, bf16[384,1024]{1,0:T(8,128)(2,1)}, bf16[384,1024]{1,0:T(8,128)(2,1)}, bf...) custom-call(s32[1]{0:T(128)} %bitcast.info, ...), custom_call_target="tpu_custom_call" | custom-call | flops 17179869184 | bytes 20971520 | tf_op jit(solution)/shard_map/pallas_call | solution.py:224
  77.5 45.9 %shard_map.187 = (bf16[384,1024]{1,0:T(8,128)(2,1)}, bf16[384,1024]{1,0:T(8,128)(2,1)}, bf16[384,1024]{1,0:T(8,128)(2,1)}, bf16[384,1024]{1,0:T(8,128)(2,1)}, bf...) custom-call(s32[1]{0:T(128)} %bitcast.info, ...), custom_call_target="tpu_custom_call" | custom-call | flops 34359738368 | bytes 41943040 | tf_op jit(solution)/shard_map/pallas_call | solution.py:224
  123.8 23.6 %shard_map.188 = (f32[2048,1024]{1,0:T(8,128)}, f32[2048,1024]{1,0:T(8,128)}) custom-call(s32[1]{0:T(128)} %bitcast.info, bf16[2048,1024]{1,0:T(8,128)(2,1)} %get-tuple-element.152.h0o, bf16[2048,1024]{1,0:T(8,128)(2,1)} %get-tuple-element.155.h0p, bf16[2048,1024]{1,0:T(8,128)(2,1)} %get-tuple-element.156.h1o, bf16[2048,1024]{1,0:T(8,128)(2,1)} %get-tuple-element.157.h1p, ...), custom_call_target="tpu_custom_call" | custom-call | flops 17179869184 | bytes 39845888 | tf_op jit(solution)/shard_map/pallas_call | solution.py:305
  150.9 46.1 %shard_map.181 = (bf16[384,1024]{1,0:T(8,128)(2,1)}, bf16[384,1024]{1,0:T(8,128)(2,1)}, bf16[384,1024]{1,0:T(8,128)(2,1)}, bf16[384,1024]{1,0:T(8,128)(2,1)}, bf...) custom-call(s32[1]{0:T(128)} %bitcast.info, ...), custom_call_target="tpu_custom_call" | custom-call | flops 34359738368 | bytes 41943040 | tf_op jit(solution)/shard_map/pallas_call | solution.py:224
  199.3 45.7 %shard_map.180 = (bf16[384,1024]{1,0:T(8,128)(2,1)}, bf16[384,1024]{1,0:T(8,128)(2,1)}, bf16[384,1024]{1,0:T(8,128)(2,1)}, bf16[384,1024]{1,0:T(8,128)(2,1)}, bf...) custom-call(s32[1]{0:T(128)} %bitcast.info, ...), custom_call_target="tpu_custom_call" | custom-call | flops 34359738368 | bytes 41943040 | tf_op jit(solution)/shard_map/pallas_call | solution.py:224
  246.9 12.0 %collective-permute-done.29.refs_13_ = bf16[128,1024]{1,0:T(8,128)(2,1)S(1)} collective-permute-done((bf16[128,1024]{1,0:T(8,128)(2,1)S(1)}, bf16[128,1024]{1,0:T(8,128)(2,1)S(1)}, u32[]{:S(2)}, u32[]{:S(2)}) %collective-permute-start.29) | collective-permute-done | bytes 262176 | tf_op jit(solution)/shard_map/ppermute | solution.py:471
  275.8 14.9 %collective-permute-done.49.refs_2_.refs_17_ = bf16[384,1024]{1,0:T(8,128)(2,1)} collective-permute-done((bf16[384,1024]{1,0:T(8,128)(2,1)}, bf16[384,1024]{1,0:T(8,128)(2,1)}, u32[]{:S(2)}, u32[]{:S(2)}) %collective-permute-start.49) | collective-permute-done | bytes 786464 | tf_op jit(solution)/shard_map/ppermute | solution.py:471
  291.1 19.4 %collective-permute-done.51.refs_4_.refs_18_ = bf16[384,1024]{1,0:T(8,128)(2,1)} collective-permute-done((bf16[384,1024]{1,0:T(8,128)(2,1)}, bf16[384,1024]{1,0:T(8,128)(2,1)}, u32[]{:S(2)}, u32[]{:S(2)}) %collective-permute-start.51) | collective-permute-done | bytes 786464 | tf_op jit(solution)/shard_map/ppermute | solution.py:471
  313.3 23.7 %shard_map.182 = (f32[2048,1024]{1,0:T(8,128)}, f32[2048,1024]{1,0:T(8,128)}) custom-call(s32[1]{0:T(128)} %bitcast.info, bf16[2048,1024]{1,0:T(8,128)(2,1)} %get-tuple-element.114.h0o, bf16[2048,1024]{1,0:T(8,128)(2,1)} %get-tuple-element.115.h0p, bf16[2048,1024]{1,0:T(8,128)(2,1)} %get-tuple-element.116.h1o, bf16[2048,1024]{1,0:T(8,128)(2,1)} %get-tuple-element.117.h1p, ...), custom_call_target="tpu_custom_call" | custom-call | flops 17179869184 | bytes 39845888 | tf_op jit(solution)/shard_map/pallas_call | solution.py:305
  348.3 18.9 %collective-permute-done.26.refs_10_.refs_21_ = bf16[384,1024]{1,0:T(8,128)(2,1)} collective-permute-done((bf16[384,1024]{1,0:T(8,128)(2,1)}, bf16[384,1024]{1,0:T(8,128)(2,1)}, u32[]{:S(2)}, u32[]{:S(2)}) %collective-permute-start.26) | collective-permute-done | bytes 786464 | tf_op jit(solution)/shard_map/ppermute | solution.py:471
  368.5 17.9 %collective-permute-done.28.refs_12_.refs_22_ = bf16[384,1024]{1,0:T(8,128)(2,1)} collective-permute-done((bf16[384,1024]{1,0:T(8,128)(2,1)S(1)}, bf16[384,1024]{1,0:T(8,128)(2,1)}, u32[]{:S(2)}, u32[]{:S(2)}) %collective-permute-start.28) | collective-permute-done | bytes 786464 | tf_op jit(solution)/shard_map/ppermute | solution.py:471
  389.9 47.4 %shard_map.190 = (bf16[384,1024]{1,0:T(8,128)(2,1)}, bf16[384,1024]{1,0:T(8,128)(2,1)}, bf16[384,1024]{1,0:T(8,128)(2,1)}, bf16[384,1024]{1,0:T(8,128)(2,1)}, bf...) custom-call(s32[1]{0:T(128)} %bitcast.info, ...), custom_call_target="tpu_custom_call" | custom-call | flops 34359738368 | bytes 41943040 | tf_op jit(solution)/shard_map/pallas_call | solution.py:224
  440.5 47.7 %shard_map.189 = (bf16[384,1024]{1,0:T(8,128)(2,1)}, bf16[384,1024]{1,0:T(8,128)(2,1)}, bf16[384,1024]{1,0:T(8,128)(2,1)}, bf16[384,1024]{1,0:T(8,128)(2,1)}, bf...) custom-call(s32[1]{0:T(128)} %bitcast.info, ...), custom_call_target="tpu_custom_call" | custom-call | flops 34359738368 | bytes 41943040 | tf_op jit(solution)/shard_map/pallas_call | solution.py:224
  491.8 47.5 %shard_map.184 = (bf16[384,1024]{1,0:T(8,128)(2,1)}, bf16[384,1024]{1,0:T(8,128)(2,1)}, bf16[384,1024]{1,0:T(8,128)(2,1)}, bf16[384,1024]{1,0:T(8,128)(2,1)}, bf...) custom-call(s32[1]{0:T(128)} %bitcast.info, ...), custom_call_target="tpu_custom_call" | custom-call | flops 34359738368 | bytes 41943040 | tf_op jit(solution)/shard_map/pallas_call | solution.py:224
  544.4 47.8 %shard_map.183 = (bf16[384,1024]{1,0:T(8,128)(2,1)}, bf16[384,1024]{1,0:T(8,128)(2,1)}, bf16[384,1024]{1,0:T(8,128)(2,1)}, bf16[384,1024]{1,0:T(8,128)(2,1)}, bf...) custom-call(s32[1]{0:T(128)} %bitcast.info, ...), custom_call_target="tpu_custom_call" | custom-call | flops 34359738368 | bytes 41943040 | tf_op jit(solution)/shard_map/pallas_call | solution.py:224
  616.8 20.6 %collective-permute-done.8.refs_5_ = bf16[128,1024]{1,0:T(8,128)(2,1)S(1)} collective-permute-done((bf16[128,1024]{1,0:T(8,128)(2,1)}, bf16[128,1024]{1,0:T(8,128)(2,1)S(1)}, u32[]{:S(2)}, u32[]{:S(2)}) %collective-permute-start.8) | collective-permute-done | bytes 262176 | tf_op jit(solution)/shard_map/ppermute | solution.py:471
  644.3 13.8 %collective-permute-done.35.refs_2_.refs_17_ = bf16[384,1024]{1,0:T(8,128)(2,1)S(1)} collective-permute-done((bf16[384,1024]{1,0:T(8,128)(2,1)}, bf16[384,1024]{1,0:T(8,128)(2,1)S(1)}, u32[]{:S(2)}, u32[]{:S(2)}) %collective-permute-start.35) | collective-permute-done | bytes 786464 | tf_op jit(solution)/shard_map/ppermute | solution.py:471
  660.8 15.6 %collective-permute-done.37.refs_4_.refs_18_ = bf16[384,1024]{1,0:T(8,128)(2,1)S(1)} collective-permute-done((bf16[384,1024]{1,0:T(8,128)(2,1)}, bf16[384,1024]{1,0:T(8,128)(2,1)S(1)}, u32[]{:S(2)}, u32[]{:S(2)}) %collective-permute-start.37) | collective-permute-done | bytes 786464 | tf_op jit(solution)/shard_map/ppermute | solution.py:471
  678.8 13.1 %collective-permute-done.12.refs_10_.refs_21_ = bf16[384,1024]{1,0:T(8,128)(2,1)S(1)} collective-permute-done((bf16[384,1024]{1,0:T(8,128)(2,1)}, bf16[384,1024]{1,0:T(8,128)(2,1)S(1)}, u32[]{:S(2)}, u32[]{:S(2)}) %collective-permute-start.12) | collective-permute-done | bytes 786464 | tf_op jit(solution)/shard_map/ppermute | solution.py:471
  694.5 14.1 %shard_map.191 = (f32[2,2,128,4096]{3,2,1,0:T(8,128)}, f32[2,2,128,4096]{3,2,1,0:T(8,128)}, f32[2,2,128,4096]{3,2,1,0:T(8,128)}, f32[2,2,2,256,1024]{4,3,2,1,0:T...) custom-call(s32[1]{0:T(128)} %bitcast.info, ...), custom_call_target="tpu_custom_call" | custom-call | flops 838860800 | bytes 41943040 | tf_op jit(solution)/shard_map/pallas_call | solution.py:382
  708.7 14.2 %shard_map.192 = (f32[2,2,128,4096]{3,2,1,0:T(8,128)}, f32[2,2,128,4096]{3,2,1,0:T(8,128)}, f32[2,2,128,4096]{3,2,1,0:T(8,128)}, f32[2,2,2,256,1024]{4,3,2,1,0:T...) custom-call(s32[1]{0:T(128)} %bitcast.info, ...), custom_call_target="tpu_custom_call", output_to_operand_aliasing={{0}: (33, {}), {1}: (34, {}), {2}: (35, {}), {3}: (36, {}),... | custom-call | flops 838860800 | bytes 41943040 | tf_op jit(solution)/shard_map/pallas_call | solution.py:382
  722.9 14.2 %shard_map.193 = (f32[2,2,128,4096]{3,2,1,0:T(8,128)}, f32[2,2,128,4096]{3,2,1,0:T(8,128)}, f32[2,2,128,4096]{3,2,1,0:T(8,128)}, f32[2,2,2,256,1024]{4,3,2,1,0:T...) custom-call(s32[1]{0:T(128)} %bitcast.info, ...), custom_call_target="tpu_custom_call", output_to_operand_aliasing={{0}: (33, {}), {1}: (34, {}), {2}: (35, {}), {3}: (36, {}),... | custom-call | flops 838860800 | bytes 41943040 | tf_op jit(solution)/shard_map/pallas_call | solution.py:382
  743.2 14.1 %shard_map.194 = (f32[2,2,128,4096]{3,2,1,0:T(8,128)}, f32[2,2,128,4096]{3,2,1,0:T(8,128)}, f32[2,2,128,4096]{3,2,1,0:T(8,128)}, f32[2,2,2,256,1024]{4,3,2,1,0:T...) custom-call(s32[1]{0:T(128)} %bitcast.info, ...), custom_call_target="tpu_custom_call", output_to_operand_aliasing={{0}: (33, {}), {1}: (34, {}), {2}: (35, {}), {3}: (36, {}),... | custom-call | flops 838860800 | bytes 41943040 | tf_op jit(solution)/shard_map/pallas_call | solution.py:382
  759.4 82.6 %all-gather.5.cloned.1.call-done.refs_1_ = bf16[8192,1024]{1,0:T(8,128)(2,1)} async-done(((bf16[1024,1024]{1,0:T(8,128)(2,1)}), bf16[8192,1024]{1,0:T(8,128)(2,1)}) %all-gather.5.cloned.1.call-update) | async-done | bytes 16777232 | tf_op jit(solution)/shard_map/all_gather | solution.py:474
  842.0 45.0 %shard_map.195.refs_0_ = bf16[2048,1024]{1,0:T(8,128)(2,1)} custom-call(bf16[2,1,2048,1024]{3,2,1,0:T(8,128)(2,1)} %refs_0_.21, bf16[8192,1024]{1,0:T(8,128)(2,1)} %all-gather.5.cloned.1.call-done.refs_1_), custom_call_target="tpu_custom_call" | custom-call | flops 34359738368 | bytes 27262976 | tf_op jit(solution)/shard_map/pallas_call | solution.py:450
  887.0 41.0 %all-gather.9.cloned.1.call-done.refs_1_ = bf16[8192,1024]{1,0:T(8,128)(2,1)} async-done(((bf16[1024,1024]{1,0:T(8,128)(2,1)}), bf16[8192,1024]{1,0:T(8,128)(2,1)}) %all-gather.9.cloned.1.call-update) | async-done | bytes 16777232 | tf_op jit(solution)/shard_map/all_gather | solution.py:474
  928.0 45.1 %shard_map.196.refs_0_ = bf16[2048,1024]{1,0:T(8,128)(2,1)} custom-call(bf16[2,1,2048,1024]{3,2,1,0:T(8,128)(2,1)} %refs_0_.21, bf16[8192,1024]{1,0:T(8,128)(2,1)} %all-gather.9.cloned.1.call-done.refs_1_), custom_call_target="tpu_custom_call" | custom-call | flops 34359738368 | bytes 27262976 | tf_op jit(solution)/shard_map/pallas_call | solution.py:450
  973.1 41.5 %all-gather.11.cloned.1.call-done.refs_1_ = bf16[8192,1024]{1,0:T(8,128)(2,1)} async-done(((bf16[1024,1024]{1,0:T(8,128)(2,1)}), bf16[8192,1024]{1,0:T(8,128)(2,1)}) %all-gather.11.cloned.1.call-update) | async-done | bytes 16777232 | tf_op jit(solution)/shard_map/all_gather | solution.py:474
  1014.6 44.9 %shard_map.197.refs_2_ = bf16[2,1,2048,1024]{3,2,1,0:T(8,128)(2,1)} custom-call(bf16[2048,1024]{1,0:T(8,128)(2,1)} %shard_map.196.refs_0_, bf16[8192,1024]{1,0:T(8,128)(2,1)} %all-gather.11.cloned.1.call-done.refs_1_), custom_call_target="tpu_custom_call" | custom-call | flops 34359738368 | bytes 27262976 | tf_op jit(solution)/shard_map/pallas_call | solution.py:450
  1059.5 41.0 %all-gather.7.cloned.1.call-done.refs_1_ = bf16[8192,1024]{1,0:T(8,128)(2,1)} async-done(((bf16[1024,1024]{1,0:T(8,128)(2,1)}), bf16[8192,1024]{1,0:T(8,128)(2,1)}) %all-gather.7.cloned.1.call-update) | async-done | bytes 16777232 | tf_op jit(solution)/shard_map/all_gather | solution.py:474
  1100.5 45.0 %shard_map.198 = bf16[2,1,2048,1024]{3,2,1,0:T(8,128)(2,1)} custom-call(bf16[2048,1024]{1,0:T(8,128)(2,1)} %shard_map.195.refs_0_, bf16[8192,1024]{1,0:T(8,128)(2,1)} %all-gather.7.cloned.1.call-done.refs_1_, bf16[2,1,2048,1024]{3,2,1,0:T(8,128)(2,1)} %shard_map.197.refs_2_), custom_call_target="tpu_custom_call", output_to_operand_aliasing={{}: (2, {})} | custom-call | flops 34359738368 | bytes 27262976 | tf_op jit(solution)/shard_map/pallas_call | solution.py:450
  (239 shorter events, 118.7 us)
Async XLA Ops:
  7.2 834.8 %all-gather.5.cloned.1.call-start = ((), (), s32[]{:S(2)}) async-start(), calls=%async_computation | async-start | bytes 18874368 | tf_op jit(solution)/shard_map/all_gather | solution.py:474
  73.3 74.1 %collective-permute-start.48 = (bf16[128,1024]{1,0:T(8,128)(2,1)}, bf16[128,1024]{1,0:T(8,128)(2,1)S(1)}, u32[]{:S(2)}, u32[]{:S(2)}) collective-permute-start(bf16[128,1024]{1,0:T(8,128)(2,1)} %get-tuple-element.177), channel_id=1, source_target_pairs={{0,1},{1,0},{2,3},{3,2},{4,5},{5,4},{6,7},{7,6}} | collective-permute-start | bytes 786440 | tf_op jit(solution)/shard_map/ppermute | solution.py:471
  73.7 75.4 %collective-permute-start.50 = (bf16[128,1024]{1,0:T(8,128)(2,1)}, bf16[128,1024]{1,0:T(8,128)(2,1)S(1)}, u32[]{:S(2)}, u32[]{:S(2)}) collective-permute-start(bf16[128,1024]{1,0:T(8,128)(2,1)} %get-tuple-element.179), channel_id=1, source_target_pairs={{0,3},{1,2},{2,1},{3,0},{4,7},{5,6},{6,5},{7,4}} | collective-permute-start | bytes 786440 | tf_op jit(solution)/shard_map/ppermute | solution.py:471
  76.3 74.1 %collective-permute-start.52 = (bf16[128,1024]{1,0:T(8,128)(2,1)}, bf16[128,1024]{1,0:T(8,128)(2,1)S(1)}, u32[]{:S(2)}, u32[]{:S(2)}) collective-permute-start(bf16[128,1024]{1,0:T(8,128)(2,1)} %get-tuple-element.181), channel_id=1, source_target_pairs={{0,5},{1,4},{2,7},{3,6},{4,1},{5,0},{6,3},{7,2}} | collective-permute-start | bytes 786440 | tf_op jit(solution)/shard_map/ppermute | solution.py:471
  77.5 73.3 %collective-permute-start.54 = (bf16[128,1024]{1,0:T(8,128)(2,1)}, bf16[128,1024]{1,0:T(8,128)(2,1)S(1)}, u32[]{:S(2)}, u32[]{:S(2)}) collective-permute-start(bf16[128,1024]{1,0:T(8,128)(2,1)} %get-tuple-element.183), channel_id=1, source_target_pairs={{0,7},{1,6},{2,5},{3,4},{4,3},{5,2},{6,1},{7,0}} | collective-permute-start | bytes 786440 | tf_op jit(solution)/shard_map/ppermute | solution.py:471
  123.4 73.7 %collective-permute-start.55 = (bf16[128,1024]{1,0:T(8,128)(2,1)}, bf16[128,1024]{1,0:T(8,128)(2,1)S(1)}, u32[]{:S(2)}, u32[]{:S(2)}) collective-permute-start(bf16[128,1024]{1,0:T(8,128)(2,1)} %get-tuple-element.185), channel_id=1, source_target_pairs={{0,1},{1,0},{2,3},{3,2},{4,5},{5,4},{6,7},{7,6}} | collective-permute-start | bytes 786440 | tf_op jit(solution)/shard_map/ppermute | solution.py:471
  150.4 238.4 %collective-permute-start.33 = (f32[2048,1024]{1,0:T(8,128)}, f32[2048,1024]{1,0:T(8,128)}, u32[]{:S(2)}, u32[]{:S(2)}) collective-permute-start(f32[2048,1024]{1,0:T(8,128)} %get-tuple-element.158.refs_6_), channel_id=1, source_target_pairs={{0,1},{1,0},{2,3},{3,2},{4,5},{5,4},{6,7},{7,6}} | collective-permute-start | bytes 25165832 | tf_op jit(solution)/shard_map/ppermute | solution.py:471
  150.8 238.6 %collective-permute-start.32 = (f32[2048,1024]{1,0:T(8,128)}, f32[2048,1024]{1,0:T(8,128)}, u32[]{:S(2)}, u32[]{:S(2)}) collective-permute-start(f32[2048,1024]{1,0:T(8,128)} %get-tuple-element.159.refs_8_), channel_id=1, source_target_pairs={{0,1},{1,0},{2,3},{3,2},{4,5},{5,4},{6,7},{7,6}} | collective-permute-start | bytes 25165832 | tf_op jit(solution)/shard_map/ppermute | solution.py:471
  337.1 151.3 %collective-permute-start.3 = (f32[2048,1024]{1,0:T(8,128)}, f32[2048,1024]{1,0:T(8,128)}, u32[]{:S(2)}, u32[]{:S(2)}) collective-permute-start(f32[2048,1024]{1,0:T(8,128)} %get-tuple-element.118.refs_6_), channel_id=1, source_target_pairs={{0,1},{1,0},{2,3},{3,2},{4,5},{5,4},{6,7},{7,6}} | collective-permute-start | bytes 25165832 | tf_op jit(solution)/shard_map/ppermute | solution.py:471
  347.0 143.9 %collective-permute-start.2 = (f32[2048,1024]{1,0:T(8,128)}, f32[2048,1024]{1,0:T(8,128)}, u32[]{:S(2)}, u32[]{:S(2)}) collective-permute-start(f32[2048,1024]{1,0:T(8,128)} %get-tuple-element.119.refs_8_), channel_id=1, source_target_pairs={{0,1},{1,0},{2,3},{3,2},{4,5},{5,4},{6,7},{7,6}} | collective-permute-start | bytes 25165832 | tf_op jit(solution)/shard_map/ppermute | solution.py:471
  386.4 50.9 %collective-permute-start.30 = (bf16[384,1024]{1,0:T(8,128)(2,1)}, bf16[384,1024]{1,0:T(8,128)(2,1)S(1)}, u32[]{:S(2)}, u32[]{:S(2)}) collective-permute-start(bf16[384,1024]{1,0:T(8,128)(2,1)} %get-tuple-element.150), channel_id=1, source_target_pairs={{0,6},{1,7},{2,4},{3,5},{4,2},{5,3},{6,0},{7,1}} | collective-permute-start | bytes 2359304 | tf_op jit(solution)/shard_map/ppermute | solution.py:471
  388.9 51.0 %collective-permute-start.19 = (bf16[384,1024]{1,0:T(8,128)(2,1)}, bf16[384,1024]{1,0:T(8,128)(2,1)S(1)}, u32[]{:S(2)}, u32[]{:S(2)}) collective-permute-start(bf16[384,1024]{1,0:T(8,128)(2,1)} %get-tuple-element.138), channel_id=1, source_target_pairs={{0,2},{1,3},{2,0},{3,1},{4,6},{5,7},{6,4},{7,5}} | collective-permute-start | bytes 2359304 | tf_op jit(solution)/shard_map/ppermute | solution.py:471
  439.8 51.1 %collective-permute-start.41 = (bf16[128,1024]{1,0:T(8,128)(2,1)}, bf16[128,1024]{1,0:T(8,128)(2,1)S(1)}, u32[]{:S(2)}, u32[]{:S(2)}) collective-permute-start(bf16[128,1024]{1,0:T(8,128)(2,1)} %get-tuple-element.169), channel_id=1, source_target_pairs={{0,1},{1,0},{2,3},{3,2},{4,5},{5,4},{6,7},{7,6}} | collective-permute-start | bytes 786440 | tf_op jit(solution)/shard_map/ppermute | solution.py:471
  439.8 51.7 %collective-permute-start.43 = (bf16[128,1024]{1,0:T(8,128)(2,1)}, bf16[128,1024]{1,0:T(8,128)(2,1)S(1)}, u32[]{:S(2)}, u32[]{:S(2)}) collective-permute-start(bf16[128,1024]{1,0:T(8,128)(2,1)} %get-tuple-element.171), channel_id=1, source_target_pairs={{0,3},{1,2},{2,1},{3,0},{4,7},{5,6},{6,5},{7,4}} | collective-permute-start | bytes 786440 | tf_op jit(solution)/shard_map/ppermute | solution.py:471
  488.2 51.1 %collective-permute-start.45 = (bf16[128,1024]{1,0:T(8,128)(2,1)}, bf16[128,1024]{1,0:T(8,128)(2,1)S(1)}, u32[]{:S(2)}, u32[]{:S(2)}) collective-permute-start(bf16[128,1024]{1,0:T(8,128)(2,1)} %get-tuple-element.173), channel_id=1, source_target_pairs={{0,5},{1,4},{2,7},{3,6},{4,1},{5,0},{6,3},{7,2}} | collective-permute-start | bytes 786440 | tf_op jit(solution)/shard_map/ppermute | solution.py:471
  488.4 53.4 %collective-permute-start.47 = (bf16[128,1024]{1,0:T(8,128)(2,1)}, bf16[128,1024]{1,0:T(8,128)(2,1)S(1)}, u32[]{:S(2)}, u32[]{:S(2)}) collective-permute-start(bf16[128,1024]{1,0:T(8,128)(2,1)} %get-tuple-element.175), channel_id=1, source_target_pairs={{0,7},{1,6},{2,5},{3,4},{4,3},{5,2},{6,1},{7,0}} | collective-permute-start | bytes 786440 | tf_op jit(solution)/shard_map/ppermute | solution.py:471
  490.9 51.5 %collective-permute-start.34 = (bf16[128,1024]{1,0:T(8,128)(2,1)}, bf16[128,1024]{1,0:T(8,128)(2,1)S(1)}, u32[]{:S(2)}, u32[]{:S(2)}) collective-permute-start(bf16[128,1024]{1,0:T(8,128)(2,1)} %get-tuple-element.161), channel_id=1, source_target_pairs={{0,1},{1,0},{2,3},{3,2},{4,5},{5,4},{6,7},{7,6}} | collective-permute-start | bytes 786440 | tf_op jit(solution)/shard_map/ppermute | solution.py:471
  490.9 52.0 %collective-permute-start.36 = (bf16[128,1024]{1,0:T(8,128)(2,1)}, bf16[128,1024]{1,0:T(8,128)(2,1)S(1)}, u32[]{:S(2)}, u32[]{:S(2)}) collective-permute-start(bf16[128,1024]{1,0:T(8,128)(2,1)} %get-tuple-element.163), channel_id=1, source_target_pairs={{0,3},{1,2},{2,1},{3,0},{4,7},{5,6},{6,5},{7,4}} | collective-permute-start | bytes 786440 | tf_op jit(solution)/shard_map/ppermute | solution.py:471
  491.6 51.4 %collective-permute-start.38 = (bf16[128,1024]{1,0:T(8,128)(2,1)}, bf16[128,1024]{1,0:T(8,128)(2,1)S(1)}, u32[]{:S(2)}, u32[]{:S(2)}) collective-permute-start(bf16[128,1024]{1,0:T(8,128)(2,1)} %get-tuple-element.165), channel_id=1, source_target_pairs={{0,5},{1,4},{2,7},{3,6},{4,1},{5,0},{6,3},{7,2}} | collective-permute-start | bytes 786440 | tf_op jit(solution)/shard_map/ppermute | solution.py:471
  539.3 53.0 %collective-permute-start.40 = (bf16[128,1024]{1,0:T(8,128)(2,1)S(1)}, bf16[128,1024]{1,0:T(8,128)(2,1)S(1)}, u32[]{:S(2)}, u32[]{:S(2)}) collective-permute-start(bf16[128,1024]{1,0:T(8,128)(2,1)S(1)} %copy-done.52), channel_id=1, source_target_pairs={{0,7},{1,6},{2,5},{3,4},{4,3},{5,2},{6,1},{7,0}} | collective-permute-start | bytes 786440 | tf_op jit(solution)/shard_map/ppermute | solution.py:471
  541.8 98.9 %collective-permute-start.42 = (bf16[384,1024]{1,0:T(8,128)(2,1)}, bf16[384,1024]{1,0:T(8,128)(2,1)S(1)}, u32[]{:S(2)}, u32[]{:S(2)}) collective-permute-start(bf16[384,1024]{1,0:T(8,128)(2,1)} %get-tuple-element.170), channel_id=1, source_target_pairs={{0,2},{1,3},{2,0},{3,1},{4,6},{5,7},{6,4},{7,5}} | collective-permute-start | bytes 2359304 | tf_op jit(solution)/shard_map/ppermute | solution.py:471
  542.4 98.5 %collective-permute-start.44 = (bf16[384,1024]{1,0:T(8,128)(2,1)}, bf16[384,1024]{1,0:T(8,128)(2,1)S(1)}, u32[]{:S(2)}, u32[]{:S(2)}) collective-permute-start(bf16[384,1024]{1,0:T(8,128)(2,1)} %get-tuple-element.172), channel_id=1, source_target_pairs={{0,4},{1,5},{2,6},{3,7},{4,0},{5,1},{6,2},{7,3}} | collective-permute-start | bytes 2359304 | tf_op jit(solution)/shard_map/ppermute | solution.py:471
  543.1 51.1 %collective-permute-start.13 = (bf16[128,1024]{1,0:T(8,128)(2,1)}, bf16[128,1024]{1,0:T(8,128)(2,1)S(1)}, u32[]{:S(2)}, u32[]{:S(2)}) collective-permute-start(bf16[128,1024]{1,0:T(8,128)(2,1)} %get-tuple-element.131), channel_id=1, source_target_pairs={{0,3},{1,2},{2,1},{3,0},{4,7},{5,6},{6,5},{7,4}} | collective-permute-start | bytes 786440 | tf_op jit(solution)/shard_map/ppermute | solution.py:471
  641.0 50.8 %collective-permute-start.12 = (bf16[384,1024]{1,0:T(8,128)(2,1)}, bf16[384,1024]{1,0:T(8,128)(2,1)S(1)}, u32[]{:S(2)}, u32[]{:S(2)}) collective-permute-start(bf16[384,1024]{1,0:T(8,128)(2,1)} %get-tuple-element.130), channel_id=1, source_target_pairs={{0,2},{1,3},{2,0},{3,1},{4,6},{5,7},{6,4},{7,5}} | collective-permute-start | bytes 2359304 | tf_op jit(solution)/shard_map/ppermute | solution.py:471
  642.5 94.6 %collective-permute-start.14 = (bf16[384,1024]{1,0:T(8,128)(2,1)}, bf16[384,1024]{1,0:T(8,128)(2,1)S(1)}, u32[]{:S(2)}, u32[]{:S(2)}) collective-permute-start(bf16[384,1024]{1,0:T(8,128)(2,1)} %get-tuple-element.132), channel_id=1, source_target_pairs={{0,4},{1,5},{2,6},{3,7},{4,0},{5,1},{6,2},{7,3}} | collective-permute-start | bytes 2359304 | tf_op jit(solution)/shard_map/ppermute | solution.py:471
  658.1 79.0 %collective-permute-start.16 = (bf16[384,1024]{1,0:T(8,128)(2,1)}, bf16[384,1024]{1,0:T(8,128)(2,1)S(1)}, u32[]{:S(2)}, u32[]{:S(2)}) collective-permute-start(bf16[384,1024]{1,0:T(8,128)(2,1)} %get-tuple-element.134), channel_id=1, source_target_pairs={{0,6},{1,7},{2,4},{3,5},{4,2},{5,3},{6,0},{7,1}} | collective-permute-start | bytes 2359304 | tf_op jit(solution)/shard_map/ppermute | solution.py:471
  676.4 60.7 %collective-permute-start.5 = (bf16[384,1024]{1,0:T(8,128)(2,1)}, bf16[384,1024]{1,0:T(8,128)(2,1)}, u32[]{:S(2)}, u32[]{:S(2)}) collective-permute-start(bf16[384,1024]{1,0:T(8,128)(2,1)} %get-tuple-element.122), channel_id=1, source_target_pairs={{0,2},{1,3},{2,0},{3,1},{4,6},{5,7},{6,4},{7,5}} | collective-permute-start | bytes 2359304 | tf_op jit(solution)/shard_map/ppermute | solution.py:471
  676.4 66.0 %collective-permute-start.7 = (bf16[384,1024]{1,0:T(8,128)(2,1)}, bf16[384,1024]{1,0:T(8,128)(2,1)}, u32[]{:S(2)}, u32[]{:S(2)}) collective-permute-start(bf16[384,1024]{1,0:T(8,128)(2,1)} %get-tuple-element.124), channel_id=1, source_target_pairs={{0,4},{1,5},{2,6},{3,7},{4,0},{5,1},{6,2},{7,3}} | collective-permute-start | bytes 2359304 | tf_op jit(solution)/shard_map/ppermute | solution.py:471
  691.8 51.4 %collective-permute-start.9 = (bf16[384,1024]{1,0:T(8,128)(2,1)}, bf16[384,1024]{1,0:T(8,128)(2,1)}, u32[]{:S(2)}, u32[]{:S(2)}) collective-permute-start(bf16[384,1024]{1,0:T(8,128)(2,1)} %get-tuple-element.126), channel_id=1, source_target_pairs={{0,6},{1,7},{2,4},{3,5},{4,2},{5,3},{6,0},{7,1}} | collective-permute-start | bytes 2359304 | tf_op jit(solution)/shard_map/ppermute | solution.py:471
  757.3 170.6 %all-gather.9.cloned.1.call-start = ((), (), s32[]{:S(2)}) async-start(), calls=%async_computation.2 | async-start | bytes 18874368 | tf_op jit(solution)/shard_map/all_gather | solution.py:474
  758.1 256.5 %all-gather.11.cloned.1.call-start = ((), (), s32[]{:S(2)}) async-start(), calls=%async_computation.3 | async-start | bytes 18874368 | tf_op jit(solution)/shard_map/all_gather | solution.py:474
  758.8 341.6 %all-gather.7.cloned.1.call-start = ((), (), s32[]{:S(2)}) async-start(), calls=%async_computation.1 | async-start | bytes 18874368 | tf_op jit(solution)/shard_map/all_gather | solution.py:474
  (92 other events, 3447.2 us)
Sparse Core Ops, SparseCore 0:
  757.5 84.4 all-gather.4
  843.8 84.1 all-gather.8
  930.4 84.1 all-gather.10
  1016.3 84.1 all-gather.6

commit v2 on v1

--- a/solution.py
+++ b/solution.py
@@ -323,11 +323,13 @@
     return master, m1, m2
 
 
-def adam_kernel(n_alias, info, *refs):
+def adam_kernel(n_alias, split, info, *refs):
     up = refs[:16]
     down = refs[16:24]
     au, mu, m1u, m2u, ad, md, m1d, m2d = refs[24:32]
-    omu, om1u, om2u, omd, om1d, om2d, w_out = refs[32 + n_alias:]
+    omu, om1u, om2u, omd, om1d, om2d = refs[32 + n_alias:38 + n_alias]
+    w_up_out, w_down_out = refs[38 + n_alias], refs[-1]
+    down0 = 0 if split else DROWS
     core = lax.rem(info[0], 2)
     j = pl.program_id(0)
     up_rows = pl.ds(pl.multiple_of(j * ROWS, ROWS), ROWS)
@@ -343,7 +345,7 @@
             omu[0, 0, :, cs] = new[0]
             om1u[0, 0, :, cs] = new[1]
             om2u[0, 0, :, cs] = new[2]
-            w_out[up_rows, cs] = new[0].astype(BF16)
+            w_up_out[up_rows, cs] = new[0].astype(BF16)
         total = None
         for q in range(4):
             v = down[half * 4 + q][...].astype(F32)
@@ -352,10 +354,10 @@
         omd[0, 0, half] = new[0]
         om1d[0, 0, half] = new[1]
         om2d[0, 0, half] = new[2]
-        w_out[pl.ds(pl.multiple_of(DROWS + half * BW + j * (BW // 4), BW // 4), BW // 4), :] = new[0].astype(BF16)
-
-
-def adam_call(stage, layer, info, recv, states, prev):
+        w_down_out[pl.ds(pl.multiple_of(down0 + half * BW + j * (BW // 4), BW // 4), BW // 4), :] = new[0].astype(BF16)
+
+
+def adam_call(stage, layer, info, recv, states, prev, split):
     nj = 4
     dr = BW // nj
     up_spec = pl.BlockSpec((ROWS, BW), lambda j, s: (0, j))
@@ -379,21 +381,23 @@
     up_shape = jax.ShapeDtypeStruct(states[0].shape, F32)
     down_shape = jax.ShapeDtypeStruct(states[4].shape, F32)
     n_in = 1 + len(args) - n_alias
+    w_shapes = [jax.ShapeDtypeStruct((DROWS, D), BF16)] * 2 if split else [jax.ShapeDtypeStruct((2 * DROWS, D), BF16)]
     return pl.pallas_call(
-        functools.partial(adam_kernel, n_alias),
-        out_shape=[up_shape] * 3 + [down_shape] * 3 + [jax.ShapeDtypeStruct((2 * DROWS, D), BF16)],
+        functools.partial(adam_kernel, n_alias, split),
+        out_shape=[up_shape] * 3 + [down_shape] * 3 + w_shapes,
         grid_spec=pltpu.PrefetchScalarGridSpec(
             num_scalar_prefetch=1, grid=(nj,), in_specs=specs,
-            out_specs=[st_up] * 3 + [st_down] * 3 + [pl.BlockSpec((2 * DROWS, D), lambda j, s: (0, 0))]),
+            out_specs=[st_up] * 3 + [st_down] * 3 + [pl.BlockSpec(w.shape, lambda j, s: (0, 0)) for w in w_shapes]),
         input_output_aliases={n_in + k: k for k in range(n_alias)},
         compiler_params=pltpu.CompilerParams(dimension_semantics=("arbitrary",), vmem_limit_bytes=60 * 2 ** 20),
         cost_estimate=pl.CostEstimate(flops=20 * 2 ** 20 * 40, bytes_accessed=40 * 2 ** 20, transcendentals=2 ** 20),
     )(info, *args)
 
 
-def fwd_kernel(has_alias, *refs):
-    x_ref, w = refs[:2]
-    o_ref, w1s, w2s, sem = refs[2 + has_alias:]
+def fwd_kernel(has_alias, split, *refs):
+    x_ref, wu, wd = refs[0], refs[1], refs[1 + split]
+    o_ref, w1s, w2s, sem = refs[2 + split + has_alias:]
+    per_dev = DROWS if split else 2 * DROWS
     i = pl.program_id(0)
     CH = DROWS
     n_ch = FF // CH
@@ -401,9 +405,9 @@
     def copies(c):
         out = []
         for d in range(8):
-            src = w.at[pl.ds(2 * DROWS * d + (c // 2) * ROWS, ROWS), pl.ds((c % 2) * CH, CH)]
+            src = wu.at[pl.ds(per_dev * d + (c // 2) * ROWS, ROWS), pl.ds((c % 2) * CH, CH)]
             out.append(pltpu.make_async_copy(src, w1s.at[pl.ds(d * ROWS, ROWS), pl.ds(c * CH, CH)], sem.at[0, c]))
-        out.append(pltpu.make_async_copy(w.at[pl.ds(2 * DROWS * c + DROWS, CH), :], w2s.at[pl.ds(c * CH, CH), :], sem.at[1, c]))
+        out.append(pltpu.make_async_copy(wd.at[pl.ds(per_dev * c + per_dev - DROWS, CH), :], w2s.at[pl.ds(c * CH, CH), :], sem.at[1, c]))
         return out
 
     def run(wait):
@@ -440,15 +444,16 @@
         x_spec = pl.BlockSpec((TM, D), lambda i: (i, 0))
         out_shape = jax.ShapeDtypeStruct((2, 1, TOK, D), BF16)
         o_spec = pl.BlockSpec((1, 1, TM, D), lambda i: (stage, 0, i, 0))
-    args = [x, w]
-    specs = [x_spec, ANY]
+    split = len(w) - 1
+    args = [x, *w]
+    specs = [x_spec] + [ANY] * len(w)
     aliases = {}
     if y_prev is not None:
         args.append(y_prev)
         specs.append(ANY)
-        aliases = {2: 0}
+        aliases = {2 + split: 0}
     return pl.pallas_call(
-        functools.partial(fwd_kernel, len(args) - 2),
+        functools.partial(fwd_kernel, len(aliases), split),
         out_shape=out_shape,
         grid_spec=pltpu.PrefetchScalarGridSpec(
             num_scalar_prefetch=0, grid=(NB,), in_specs=specs, out_specs=o_spec,
@@ -459,7 +464,7 @@
     )(*args)
 
 
-SEQ = ("bwd_010a", "bwd_010b", "bwd_011", "bwd_110", "adam_01", "dx_01", "bwd_111", "bwd_000", "dx_11", "bwd_001", "bwd_100", "adam_00", "bwd_101", "adam_11", "adam_10", "fwd_00", "fwd_01", "fwd_10", "fwd_11")
+SEQ = ("bwd_010a", "bwd_010b", "bwd_011", "bwd_110", "adam_01", "dx_01", "bwd_111", "bwd_000", "dx_11", "adam_11", "bwd_001", "bwd_100", "adam_00", "bwd_101", "adam_10", "fwd_00", "fwd_01", "fwd_10", "fwd_11")
 
 
 def solution(mesh):
@@ -490,20 +495,22 @@
         dh = {}
         outs6 = ()
         full = {}
-        w_new = {}
         hid = {}
         y = None
 
         for name in SEQ:
             s, l = int(name.split("_")[1][0]), int(name.split("_")[1][1])
             if name.startswith("adam"):
-                res = adam_call(s, l, info, recv[s, l], states, outs6)
+                split = (s, l) == (1, 1)
+                res = adam_call(s, l, info, recv[s, l], states, outs6, split)
                 outs6 = tuple(res[:6])
-                w_new[s, l] = res[6]
-                if (s, l) != (1, 1):
-                    full[s, l] = gather(res[6])
+                if split:
+                    late = res[7]
+                    full[s, l] = [gather(res[6])]
+                else:
+                    full[s, l] = [gather(res[6])]
                 if (s, l) == (1, 0):
-                    full[1, 1] = gather(lax.optimization_barrier((w_new[1, 1], res[6]))[0])
+                    full[1, 1].append(gather(lax.optimization_barrier((late, res[6]))[0]))
                 continue
             if name.startswith("fwd"):
                 if l == 0:

time: 1160 us -> 1180 us (1.017)
  waiting for transfers between devices: 410 us -> 425 us
    all_gather x4 -> x5, waiting for transfers between devices: 206 us -> 220 us  [gather(): return lax.all_gather(a, 'fsdp', axis=0, tiled=True)]
  transfers between devices with their start and end apart: 66 -> 67, of which waited for: 22 -> 22; matrix products, arithmetic and copies ran while one was open for 0% -> 0% of each run, Pallas kernels for 50% -> 50%
where the time goes in v2:
time: 1180 us; the launch traced here: 1170 us
  Pallas kernels  667 us (57%)
  waiting for transfers between devices  425 us (36%)
  starting transfers between devices  59.6 us (5%)
  between operations  14.9 us (1%)
    pallas_call x9, Pallas kernels, bwd_call(): pl.pallas_call(functools.partial(bwd_kernel, stage, layer, half, mode, pa...  383 us
    all_gather x5, waiting for transfers between devices, gather(): return lax.all_gather(a, 'fsdp', axis=0, tiled=True)  220 us
    ppermute x62, waiting for transfers between devices, swap(): return lax.ppermute(a, 'fsdp', [(d, d ^ r) for d in range(n_dev)])  203 us
    pallas_call x4, Pallas kernels, fwd_call(): pl.pallas_call(functools.partial(fwd_kernel, len(aliases), split), out_sh...  180 us
    ppermute x62, starting transfers between devices, swap(): return lax.ppermute(a, 'fsdp', [(d, d ^ r) for d in range(n_dev)])  59.4 us
    pallas_call x4, Pallas kernels, adam_call(): pl.pallas_call(functools.partial(adam_kernel, n_alias, split), out_shape=...  57.1 us
    pallas_call x2, Pallas kernels, dx_call(): pl.pallas_call(functools.partial(dx_kernel, stage, layer), out_shape=[jax...  47.3 us
  transfers between devices with their start and end apart: 67, of which 22 were waited for; matrix products, arithmetic and copies ran while one was open for 0% of the time, Pallas kernels for 50%

profile of v2, /device:TPU:0, one launch (start us, length us, event | category | flops | bytes accessed | tf_op | source)
XLA Modules:
  0.0 1168.6 jit_solution(11479081525463415694)
XLA Ops:
  8.1 26.4 %shard_map.185 = (f32[1024,1024]{1,0:T(8,128)}, f32[1024,1024]{1,0:T(8,128)}, bf16[2048,1024]{1,0:T(8,128)(2,1)}) custom-call(s32[1]{0:T(128)} %bitcast.info, bf16[2,2,1,2048,1024]{4,3,2,1,0:T(8,128)(2,1)} %refs_0_.19, bf16[2,2,1,2048,1024]{4,3,2,1,0:T(8,128)(2,1)} %refs_0_.19, bf16[2,1,2048,1024]{3,2,1,0:T(8,128)(2,1)} %refs_2_.17, ...), custom_call_target="tpu_custom_call" | custom-call | flops 17179869184 | bytes 20971520 | tf_op jit(solution)/shard_map/pallas_call | solution.py:224
  45.2 28.1 %shard_map.186 = (bf16[384,1024]{1,0:T(8,128)(2,1)}, bf16[384,1024]{1,0:T(8,128)(2,1)}, bf16[384,1024]{1,0:T(8,128)(2,1)}, bf16[384,1024]{1,0:T(8,128)(2,1)}, bf...) custom-call(s32[1]{0:T(128)} %bitcast.info, ...), custom_call_target="tpu_custom_call" | custom-call | flops 17179869184 | bytes 20971520 | tf_op jit(solution)/shard_map/pallas_call | solution.py:224
  77.5 45.8 %shard_map.187 = (bf16[384,1024]{1,0:T(8,128)(2,1)}, bf16[384,1024]{1,0:T(8,128)(2,1)}, bf16[384,1024]{1,0:T(8,128)(2,1)}, bf16[384,1024]{1,0:T(8,128)(2,1)}, bf...) custom-call(s32[1]{0:T(128)} %bitcast.info, ...), custom_call_target="tpu_custom_call" | custom-call | flops 34359738368 | bytes 41943040 | tf_op jit(solution)/shard_map/pallas_call | solution.py:224
  123.8 23.6 %shard_map.188 = (f32[2048,1024]{1,0:T(8,128)}, f32[2048,1024]{1,0:T(8,128)}) custom-call(s32[1]{0:T(128)} %bitcast.info, bf16[2048,1024]{1,0:T(8,128)(2,1)} %get-tuple-element.137.h0o, bf16[2048,1024]{1,0:T(8,128)(2,1)} %get-tuple-element.140.h0p, bf16[2048,1024]{1,0:T(8,128)(2,1)} %get-tuple-element.141.h1o, bf16[2048,1024]{1,0:T(8,128)(2,1)} %get-tuple-element.142.h1p, ...), custom_call_target="tpu_custom_call" | custom-call | flops 17179869184 | bytes 39845888 | tf_op jit(solution)/shard_map/pallas_call | solution.py:305
  150.9 46.1 %shard_map.181 = (bf16[384,1024]{1,0:T(8,128)(2,1)}, bf16[384,1024]{1,0:T(8,128)(2,1)}, bf16[384,1024]{1,0:T(8,128)(2,1)}, bf16[384,1024]{1,0:T(8,128)(2,1)}, bf...) custom-call(s32[1]{0:T(128)} %bitcast.info, ...), custom_call_target="tpu_custom_call" | custom-call | flops 34359738368 | bytes 41943040 | tf_op jit(solution)/shard_map/pallas_call | solution.py:224
  199.2 45.6 %shard_map.180 = (bf16[384,1024]{1,0:T(8,128)(2,1)}, bf16[384,1024]{1,0:T(8,128)(2,1)}, bf16[384,1024]{1,0:T(8,128)(2,1)}, bf16[384,1024]{1,0:T(8,128)(2,1)}, bf...) custom-call(s32[1]{0:T(128)} %bitcast.info, ...), custom_call_target="tpu_custom_call" | custom-call | flops 34359738368 | bytes 41943040 | tf_op jit(solution)/shard_map/pallas_call | solution.py:224
  275.7 14.9 %collective-permute-done.49.refs_2_.refs_17_ = bf16[384,1024]{1,0:T(8,128)(2,1)} collective-permute-done((bf16[384,1024]{1,0:T(8,128)(2,1)}, bf16[384,1024]{1,0:T(8,128)(2,1)}, u32[]{:S(2)}, u32[]{:S(2)}) %collective-permute-start.49) | collective-permute-done | bytes 786464 | tf_op jit(solution)/shard_map/ppermute | solution.py:476
  290.9 19.4 %collective-permute-done.51.refs_4_.refs_18_ = bf16[384,1024]{1,0:T(8,128)(2,1)} collective-permute-done((bf16[384,1024]{1,0:T(8,128)(2,1)}, bf16[384,1024]{1,0:T(8,128)(2,1)}, u32[]{:S(2)}, u32[]{:S(2)}) %collective-permute-start.51) | collective-permute-done | bytes 786464 | tf_op jit(solution)/shard_map/ppermute | solution.py:476
  313.2 23.7 %shard_map.182 = (f32[2048,1024]{1,0:T(8,128)}, f32[2048,1024]{1,0:T(8,128)}) custom-call(s32[1]{0:T(128)} %bitcast.info, bf16[2048,1024]{1,0:T(8,128)(2,1)} %get-tuple-element.115.h0o, bf16[2048,1024]{1,0:T(8,128)(2,1)} %get-tuple-element.116.h0p, bf16[2048,1024]{1,0:T(8,128)(2,1)} %get-tuple-element.117.h1o, bf16[2048,1024]{1,0:T(8,128)(2,1)} %get-tuple-element.118.h1p, ...), custom_call_target="tpu_custom_call" | custom-call | flops 17179869184 | bytes 39845888 | tf_op jit(solution)/shard_map/pallas_call | solution.py:305
  348.2 18.9 %collective-permute-done.42.refs_10_.refs_21_ = bf16[384,1024]{1,0:T(8,128)(2,1)} collective-permute-done((bf16[384,1024]{1,0:T(8,128)(2,1)}, bf16[384,1024]{1,0:T(8,128)(2,1)}, u32[]{:S(2)}, u32[]{:S(2)}) %collective-permute-start.42) | collective-permute-done | bytes 786464 | tf_op jit(solution)/shard_map/ppermute | solution.py:476
  368.4 17.9 %collective-permute-done.44.refs_12_.refs_22_ = bf16[384,1024]{1,0:T(8,128)(2,1)} collective-permute-done((bf16[384,1024]{1,0:T(8,128)(2,1)S(1)}, bf16[384,1024]{1,0:T(8,128)(2,1)}, u32[]{:S(2)}, u32[]{:S(2)}) %collective-permute-start.44) | collective-permute-done | bytes 786464 | tf_op jit(solution)/shard_map/ppermute | solution.py:476
  389.8 47.5 %shard_map.190 = (bf16[384,1024]{1,0:T(8,128)(2,1)}, bf16[384,1024]{1,0:T(8,128)(2,1)}, bf16[384,1024]{1,0:T(8,128)(2,1)}, bf16[384,1024]{1,0:T(8,128)(2,1)}, bf...) custom-call(s32[1]{0:T(128)} %bitcast.info, ...), custom_call_target="tpu_custom_call" | custom-call | flops 34359738368 | bytes 41943040 | tf_op jit(solution)/shard_map/pallas_call | solution.py:224
  440.5 47.6 %shard_map.189 = (bf16[384,1024]{1,0:T(8,128)(2,1)}, bf16[384,1024]{1,0:T(8,128)(2,1)}, bf16[384,1024]{1,0:T(8,128)(2,1)}, bf16[384,1024]{1,0:T(8,128)(2,1)}, bf...) custom-call(s32[1]{0:T(128)} %bitcast.info, ...), custom_call_target="tpu_custom_call" | custom-call | flops 34359738368 | bytes 41943040 | tf_op jit(solution)/shard_map/pallas_call | solution.py:224
  491.7 47.6 %shard_map.184 = (bf16[384,1024]{1,0:T(8,128)(2,1)}, bf16[384,1024]{1,0:T(8,128)(2,1)}, bf16[384,1024]{1,0:T(8,128)(2,1)}, bf16[384,1024]{1,0:T(8,128)(2,1)}, bf...) custom-call(s32[1]{0:T(128)} %bitcast.info, ...), custom_call_target="tpu_custom_call" | custom-call | flops 34359738368 | bytes 41943040 | tf_op jit(solution)/shard_map/pallas_call | solution.py:224
  544.4 47.8 %shard_map.183 = (bf16[384,1024]{1,0:T(8,128)(2,1)}, bf16[384,1024]{1,0:T(8,128)(2,1)}, bf16[384,1024]{1,0:T(8,128)(2,1)}, bf16[384,1024]{1,0:T(8,128)(2,1)}, bf...) custom-call(s32[1]{0:T(128)} %bitcast.info, ...), custom_call_target="tpu_custom_call" | custom-call | flops 34359738368 | bytes 41943040 | tf_op jit(solution)/shard_map/pallas_call | solution.py:224
  594.3 12.2 %collective-permute-done.15.refs_13_ = bf16[128,1024]{1,0:T(8,128)(2,1)S(1)} collective-permute-done((bf16[128,1024]{1,0:T(8,128)(2,1)}, bf16[128,1024]{1,0:T(8,128)(2,1)S(1)}, u32[]{:S(2)}, u32[]{:S(2)}) %collective-permute-start.15) | collective-permute-done | bytes 262176 | tf_op jit(solution)/shard_map/ppermute | solution.py:476
  616.7 20.7 %collective-permute-done.8.refs_5_ = bf16[128,1024]{1,0:T(8,128)(2,1)S(1)} collective-permute-done((bf16[128,1024]{1,0:T(8,128)(2,1)}, bf16[128,1024]{1,0:T(8,128)(2,1)S(1)}, u32[]{:S(2)}, u32[]{:S(2)}) %collective-permute-start.8) | collective-permute-done | bytes 262176 | tf_op jit(solution)/shard_map/ppermute | solution.py:476
  645.6 13.1 %collective-permute-done.21.refs_2_.refs_17_ = bf16[384,1024]{1,0:T(8,128)(2,1)S(1)} collective-permute-done((bf16[384,1024]{1,0:T(8,128)(2,1)}, bf16[384,1024]{1,0:T(8,128)(2,1)S(1)}, u32[]{:S(2)}, u32[]{:S(2)}) %collective-permute-start.21) | collective-permute-done | bytes 786464 | tf_op jit(solution)/shard_map/ppermute | solution.py:476
  661.4 16.3 %collective-permute-done.23.refs_4_.refs_18_ = bf16[384,1024]{1,0:T(8,128)(2,1)S(1)} collective-permute-done((bf16[384,1024]{1,0:T(8,128)(2,1)}, bf16[384,1024]{1,0:T(8,128)(2,1)S(1)}, u32[]{:S(2)}, u32[]{:S(2)}) %collective-permute-start.23) | collective-permute-done | bytes 786464 | tf_op jit(solution)/shard_map/ppermute | solution.py:476
  679.5 12.9 %collective-permute-done.12.refs_10_.refs_21_ = bf16[384,1024]{1,0:T(8,128)(2,1)S(1)} collective-permute-done((bf16[384,1024]{1,0:T(8,128)(2,1)}, bf16[384,1024]{1,0:T(8,128)(2,1)S(1)}, u32[]{:S(2)}, u32[]{:S(2)}) %collective-permute-start.12) | collective-permute-done | bytes 786464 | tf_op jit(solution)/shard_map/ppermute | solution.py:476
  695.2 14.1 %shard_map.191 = (f32[2,2,128,4096]{3,2,1,0:T(8,128)}, f32[2,2,128,4096]{3,2,1,0:T(8,128)}, f32[2,2,128,4096]{3,2,1,0:T(8,128)}, f32[2,2,2,256,1024]{4,3,2,1,0:T...) custom-call(s32[1]{0:T(128)} %bitcast.info, ...), custom_call_target="tpu_custom_call" | custom-call | flops 838860800 | bytes 41943040 | tf_op jit(solution)/shard_map/pallas_call | solution.py:385
  709.3 14.6 %shard_map.192 = (f32[2,2,128,4096]{3,2,1,0:T(8,128)}, f32[2,2,128,4096]{3,2,1,0:T(8,128)}, f32[2,2,128,4096]{3,2,1,0:T(8,128)}, f32[2,2,2,256,1024]{4,3,2,1,0:T...) custom-call(s32[1]{0:T(128)} %bitcast.info, ...), custom_call_target="tpu_custom_call", output_to_operand_aliasing={{0}: (33, {}), {1}: (34, {}), {2}: (35, {}), {3}: (36, {}),... | custom-call | flops 838860800 | bytes 41943040 | tf_op jit(solution)/shard_map/pallas_call | solution.py:385
  723.9 14.2 %shard_map.193 = (f32[2,2,128,4096]{3,2,1,0:T(8,128)}, f32[2,2,128,4096]{3,2,1,0:T(8,128)}, f32[2,2,128,4096]{3,2,1,0:T(8,128)}, f32[2,2,2,256,1024]{4,3,2,1,0:T...) custom-call(s32[1]{0:T(128)} %bitcast.info, ...), custom_call_target="tpu_custom_call", output_to_operand_aliasing={{0}: (33, {}), {1}: (34, {}), {2}: (35, {}), {3}: (36, {}),... | custom-call | flops 838860800 | bytes 41943040 | tf_op jit(solution)/shard_map/pallas_call | solution.py:385
  744.4 14.2 %shard_map.194 = (f32[2,2,128,4096]{3,2,1,0:T(8,128)}, f32[2,2,128,4096]{3,2,1,0:T(8,128)}, f32[2,2,128,4096]{3,2,1,0:T(8,128)}, f32[2,2,2,256,1024]{4,3,2,1,0:T...) custom-call(s32[1]{0:T(128)} %bitcast.info, ...), custom_call_target="tpu_custom_call", output_to_operand_aliasing={{0}: (33, {}), {1}: (34, {}), {2}: (35, {}), {3}: (36, {}),... | custom-call | flops 838860800 | bytes 41943040 | tf_op jit(solution)/shard_map/pallas_call | solution.py:385
  761.3 81.9 %all-gather.6.cloned.1.call-done.refs_1_ = bf16[8192,1024]{1,0:T(8,128)(2,1)} async-done(((bf16[1024,1024]{1,0:T(8,128)(2,1)}), bf16[8192,1024]{1,0:T(8,128)(2,1)}) %all-gather.6.cloned.1.call-update) | async-done | bytes 16777232 | tf_op jit(solution)/shard_map/all_gather | solution.py:479
  843.3 45.0 %shard_map.195.refs_0_ = bf16[2048,1024]{1,0:T(8,128)(2,1)} custom-call(bf16[2,1,2048,1024]{3,2,1,0:T(8,128)(2,1)} %refs_0_.21, bf16[8192,1024]{1,0:T(8,128)(2,1)} %all-gather.6.cloned.1.call-done.refs_1_), custom_call_target="tpu_custom_call" | custom-call | flops 34359738368 | bytes 27262976 | tf_op jit(solution)/shard_map/pallas_call | solution.py:455
  888.2 41.1 %all-gather.12.cloned.1.call-done.refs_1_ = bf16[8192,1024]{1,0:T(8,128)(2,1)} async-done(((bf16[1024,1024]{1,0:T(8,128)(2,1)}), bf16[8192,1024]{1,0:T(8,128)(2,1)}) %all-gather.12.cloned.1.call-update) | async-done | bytes 16777232 | tf_op jit(solution)/shard_map/all_gather | solution.py:479
  929.3 45.1 %shard_map.196.refs_0_ = bf16[2048,1024]{1,0:T(8,128)(2,1)} custom-call(bf16[2,1,2048,1024]{3,2,1,0:T(8,128)(2,1)} %refs_0_.21, bf16[8192,1024]{1,0:T(8,128)(2,1)} %all-gather.12.cloned.1.call-done.refs_1_), custom_call_target="tpu_custom_call" | custom-call | flops 34359738368 | bytes 27262976 | tf_op jit(solution)/shard_map/pallas_call | solution.py:455
  974.5 41.5 %all-gather.14.cloned.1.call-done.refs_1_ = bf16[8192,1024]{1,0:T(8,128)(2,1)} async-done(((bf16[1024,1024]{1,0:T(8,128)(2,1)}), bf16[8192,1024]{1,0:T(8,128)(2,1)}) %all-gather.14.cloned.1.call-update) | async-done | bytes 16777232 | tf_op jit(solution)/shard_map/all_gather | solution.py:479
  1015.9 44.9 %shard_map.197.refs_3_ = bf16[2,1,2048,1024]{3,2,1,0:T(8,128)(2,1)} custom-call(bf16[2048,1024]{1,0:T(8,128)(2,1)} %shard_map.196.refs_0_, bf16[8192,1024]{1,0:T(8,128)(2,1)} %all-gather.14.cloned.1.call-done.refs_1_), custom_call_target="tpu_custom_call" | custom-call | flops 34359738368 | bytes 27262976 | tf_op jit(solution)/shard_map/pallas_call | solution.py:455
  1066.3 50.4 %all-gather.10.cloned.1.call-done.refs_2_ = bf16[4096,1024]{1,0:T(8,128)(2,1)} async-done(((bf16[512,1024]{1,0:T(8,128)(2,1)}), bf16[4096,1024]{1,0:T(8,128)(2,1)}) %all-gather.10.cloned.1.call-update) | async-done | bytes 8388624 | tf_op jit(solution)/shard_map/all_gather | solution.py:479
  1116.7 45.0 %shard_map.198 = bf16[2,1,2048,1024]{3,2,1,0:T(8,128)(2,1)} custom-call(bf16[2048,1024]{1,0:T(8,128)(2,1)} %shard_map.195.refs_0_, bf16[4096,1024]{1,0:T(8,128)(2,1)} %all-gather.8.cloned.1.call-done.refs_1_, bf16[4096,1024]{1,0:T(8,128)(2,1)} %all-gather.10.cloned.1.call-done.refs_2_, ...), custom_call_target="tpu_custom_call", output_to_operand_aliasing={{}: (3, {})} | custom-call | flops 34359738368 | bytes 27262976 | tf_op jit(solution)/shard_map/pallas_call | solution.py:455
  (240 shorter events, 125.4 us)
Async XLA Ops:
  7.2 836.1 %all-gather.6.cloned.1.call-start = ((), (), s32[]{:S(2)}) async-start(), calls=%async_computation | async-start | bytes 18874368 | tf_op jit(solution)/shard_map/all_gather | solution.py:479
  73.3 74.1 %collective-permute-start.48 = (bf16[128,1024]{1,0:T(8,128)(2,1)}, bf16[128,1024]{1,0:T(8,128)(2,1)S(1)}, u32[]{:S(2)}, u32[]{:S(2)}) collective-permute-start(bf16[128,1024]{1,0:T(8,128)(2,1)} %get-tuple-element.178), channel_id=1, source_target_pairs={{0,1},{1,0},{2,3},{3,2},{4,5},{5,4},{6,7},{7,6}} | collective-permute-start | bytes 786440 | tf_op jit(solution)/shard_map/ppermute | solution.py:476
  73.7 75.4 %collective-permute-start.50 = (bf16[128,1024]{1,0:T(8,128)(2,1)}, bf16[128,1024]{1,0:T(8,128)(2,1)S(1)}, u32[]{:S(2)}, u32[]{:S(2)}) collective-permute-start(bf16[128,1024]{1,0:T(8,128)(2,1)} %get-tuple-element.180), channel_id=1, source_target_pairs={{0,3},{1,2},{2,1},{3,0},{4,7},{5,6},{6,5},{7,4}} | collective-permute-start | bytes 786440 | tf_op jit(solution)/shard_map/ppermute | solution.py:476
  76.3 74.1 %collective-permute-start.52 = (bf16[128,1024]{1,0:T(8,128)(2,1)}, bf16[128,1024]{1,0:T(8,128)(2,1)S(1)}, u32[]{:S(2)}, u32[]{:S(2)}) collective-permute-start(bf16[128,1024]{1,0:T(8,128)(2,1)} %get-tuple-element.182), channel_id=1, source_target_pairs={{0,5},{1,4},{2,7},{3,6},{4,1},{5,0},{6,3},{7,2}} | collective-permute-start | bytes 786440 | tf_op jit(solution)/shard_map/ppermute | solution.py:476
  77.5 73.2 %collective-permute-start.54 = (bf16[128,1024]{1,0:T(8,128)(2,1)}, bf16[128,1024]{1,0:T(8,128)(2,1)S(1)}, u32[]{:S(2)}, u32[]{:S(2)}) collective-permute-start(bf16[128,1024]{1,0:T(8,128)(2,1)} %get-tuple-element.184), channel_id=1, source_target_pairs={{0,7},{1,6},{2,5},{3,4},{4,3},{5,2},{6,1},{7,0}} | collective-permute-start | bytes 786440 | tf_op jit(solution)/shard_map/ppermute | solution.py:476
  123.4 73.6 %collective-permute-start.55 = (bf16[128,1024]{1,0:T(8,128)(2,1)}, bf16[128,1024]{1,0:T(8,128)(2,1)S(1)}, u32[]{:S(2)}, u32[]{:S(2)}) collective-permute-start(bf16[128,1024]{1,0:T(8,128)(2,1)} %get-tuple-element.186), channel_id=1, source_target_pairs={{0,1},{1,0},{2,3},{3,2},{4,5},{5,4},{6,7},{7,6}} | collective-permute-start | bytes 786440 | tf_op jit(solution)/shard_map/ppermute | solution.py:476
  150.4 238.3 %collective-permute-start.19 = (f32[2048,1024]{1,0:T(8,128)}, f32[2048,1024]{1,0:T(8,128)}, u32[]{:S(2)}, u32[]{:S(2)}) collective-permute-start(f32[2048,1024]{1,0:T(8,128)} %get-tuple-element.143.refs_6_), channel_id=1, source_target_pairs={{0,1},{1,0},{2,3},{3,2},{4,5},{5,4},{6,7},{7,6}} | collective-permute-start | bytes 25165832 | tf_op jit(solution)/shard_map/ppermute | solution.py:476
  150.8 238.5 %collective-permute-start.18 = (f32[2048,1024]{1,0:T(8,128)}, f32[2048,1024]{1,0:T(8,128)}, u32[]{:S(2)}, u32[]{:S(2)}) collective-permute-start(f32[2048,1024]{1,0:T(8,128)} %get-tuple-element.144.refs_8_), channel_id=1, source_target_pairs={{0,1},{1,0},{2,3},{3,2},{4,5},{5,4},{6,7},{7,6}} | collective-permute-start | bytes 25165832 | tf_op jit(solution)/shard_map/ppermute | solution.py:476
  336.9 151.4 %collective-permute-start.3 = (f32[2048,1024]{1,0:T(8,128)}, f32[2048,1024]{1,0:T(8,128)}, u32[]{:S(2)}, u32[]{:S(2)}) collective-permute-start(f32[2048,1024]{1,0:T(8,128)} %get-tuple-element.119.refs_6_), channel_id=1, source_target_pairs={{0,1},{1,0},{2,3},{3,2},{4,5},{5,4},{6,7},{7,6}} | collective-permute-start | bytes 25165832 | tf_op jit(solution)/shard_map/ppermute | solution.py:476
  346.8 144.0 %collective-permute-start.2 = (f32[2048,1024]{1,0:T(8,128)}, f32[2048,1024]{1,0:T(8,128)}, u32[]{:S(2)}, u32[]{:S(2)}) collective-permute-start(f32[2048,1024]{1,0:T(8,128)} %get-tuple-element.120.refs_8_), channel_id=1, source_target_pairs={{0,1},{1,0},{2,3},{3,2},{4,5},{5,4},{6,7},{7,6}} | collective-permute-start | bytes 25165832 | tf_op jit(solution)/shard_map/ppermute | solution.py:476
  386.3 51.1 %collective-permute-start.46 = (bf16[384,1024]{1,0:T(8,128)(2,1)}, bf16[384,1024]{1,0:T(8,128)(2,1)S(1)}, u32[]{:S(2)}, u32[]{:S(2)}) collective-permute-start(bf16[384,1024]{1,0:T(8,128)(2,1)} %get-tuple-element.175), channel_id=1, source_target_pairs={{0,6},{1,7},{2,4},{3,5},{4,2},{5,3},{6,0},{7,1}} | collective-permute-start | bytes 2359304 | tf_op jit(solution)/shard_map/ppermute | solution.py:476
  388.7 51.1 %collective-permute-start.35 = (bf16[384,1024]{1,0:T(8,128)(2,1)}, bf16[384,1024]{1,0:T(8,128)(2,1)S(1)}, u32[]{:S(2)}, u32[]{:S(2)}) collective-permute-start(bf16[384,1024]{1,0:T(8,128)(2,1)} %get-tuple-element.163), channel_id=1, source_target_pairs={{0,2},{1,3},{2,0},{3,1},{4,6},{5,7},{6,4},{7,5}} | collective-permute-start | bytes 2359304 | tf_op jit(solution)/shard_map/ppermute | solution.py:476
  439.8 51.1 %collective-permute-start.27 = (bf16[128,1024]{1,0:T(8,128)(2,1)}, bf16[128,1024]{1,0:T(8,128)(2,1)S(1)}, u32[]{:S(2)}, u32[]{:S(2)}) collective-permute-start(bf16[128,1024]{1,0:T(8,128)(2,1)} %get-tuple-element.154), channel_id=1, source_target_pairs={{0,1},{1,0},{2,3},{3,2},{4,5},{5,4},{6,7},{7,6}} | collective-permute-start | bytes 786440 | tf_op jit(solution)/shard_map/ppermute | solution.py:476
  439.8 51.7 %collective-permute-start.29 = (bf16[128,1024]{1,0:T(8,128)(2,1)}, bf16[128,1024]{1,0:T(8,128)(2,1)S(1)}, u32[]{:S(2)}, u32[]{:S(2)}) collective-permute-start(bf16[128,1024]{1,0:T(8,128)(2,1)} %get-tuple-element.156), channel_id=1, source_target_pairs={{0,3},{1,2},{2,1},{3,0},{4,7},{5,6},{6,5},{7,4}} | collective-permute-start | bytes 786440 | tf_op jit(solution)/shard_map/ppermute | solution.py:476
  488.2 51.1 %collective-permute-start.31 = (bf16[128,1024]{1,0:T(8,128)(2,1)}, bf16[128,1024]{1,0:T(8,128)(2,1)S(1)}, u32[]{:S(2)}, u32[]{:S(2)}) collective-permute-start(bf16[128,1024]{1,0:T(8,128)(2,1)} %get-tuple-element.158), channel_id=1, source_target_pairs={{0,5},{1,4},{2,7},{3,6},{4,1},{5,0},{6,3},{7,2}} | collective-permute-start | bytes 786440 | tf_op jit(solution)/shard_map/ppermute | solution.py:476
  488.4 53.5 %collective-permute-start.33 = (bf16[128,1024]{1,0:T(8,128)(2,1)}, bf16[128,1024]{1,0:T(8,128)(2,1)S(1)}, u32[]{:S(2)}, u32[]{:S(2)}) collective-permute-start(bf16[128,1024]{1,0:T(8,128)(2,1)} %get-tuple-element.160), channel_id=1, source_target_pairs={{0,7},{1,6},{2,5},{3,4},{4,3},{5,2},{6,1},{7,0}} | collective-permute-start | bytes 786440 | tf_op jit(solution)/shard_map/ppermute | solution.py:476
  490.9 51.5 %collective-permute-start.20 = (bf16[128,1024]{1,0:T(8,128)(2,1)}, bf16[128,1024]{1,0:T(8,128)(2,1)S(1)}, u32[]{:S(2)}, u32[]{:S(2)}) collective-permute-start(bf16[128,1024]{1,0:T(8,128)(2,1)} %get-tuple-element.146), channel_id=1, source_target_pairs={{0,1},{1,0},{2,3},{3,2},{4,5},{5,4},{6,7},{7,6}} | collective-permute-start | bytes 786440 | tf_op jit(solution)/shard_map/ppermute | solution.py:476
  490.9 52.0 %collective-permute-start.22 = (bf16[128,1024]{1,0:T(8,128)(2,1)}, bf16[128,1024]{1,0:T(8,128)(2,1)S(1)}, u32[]{:S(2)}, u32[]{:S(2)}) collective-permute-start(bf16[128,1024]{1,0:T(8,128)(2,1)} %get-tuple-element.148), channel_id=1, source_target_pairs={{0,3},{1,2},{2,1},{3,0},{4,7},{5,6},{6,5},{7,4}} | collective-permute-start | bytes 786440 | tf_op jit(solution)/shard_map/ppermute | solution.py:476
  491.6 51.4 %collective-permute-start.24 = (bf16[128,1024]{1,0:T(8,128)(2,1)}, bf16[128,1024]{1,0:T(8,128)(2,1)S(1)}, u32[]{:S(2)}, u32[]{:S(2)}) collective-permute-start(bf16[128,1024]{1,0:T(8,128)(2,1)} %get-tuple-element.150), channel_id=1, source_target_pairs={{0,5},{1,4},{2,7},{3,6},{4,1},{5,0},{6,3},{7,2}} | collective-permute-start | bytes 786440 | tf_op jit(solution)/shard_map/ppermute | solution.py:476
  539.3 52.9 %collective-permute-start.26 = (bf16[128,1024]{1,0:T(8,128)(2,1)S(1)}, bf16[128,1024]{1,0:T(8,128)(2,1)S(1)}, u32[]{:S(2)}, u32[]{:S(2)}) collective-permute-start(bf16[128,1024]{1,0:T(8,128)(2,1)S(1)} %copy-done.50), channel_id=1, source_target_pairs={{0,7},{1,6},{2,5},{3,4},{4,3},{5,2},{6,1},{7,0}} | collective-permute-start | bytes 786440 | tf_op jit(solution)/shard_map/ppermute | solution.py:476
  541.8 100.2 %collective-permute-start.28 = (bf16[384,1024]{1,0:T(8,128)(2,1)}, bf16[384,1024]{1,0:T(8,128)(2,1)S(1)}, u32[]{:S(2)}, u32[]{:S(2)}) collective-permute-start(bf16[384,1024]{1,0:T(8,128)(2,1)} %get-tuple-element.155), channel_id=1, source_target_pairs={{0,2},{1,3},{2,0},{3,1},{4,6},{5,7},{6,4},{7,5}} | collective-permute-start | bytes 2359304 | tf_op jit(solution)/shard_map/ppermute | solution.py:476
  542.4 99.9 %collective-permute-start.30 = (bf16[384,1024]{1,0:T(8,128)(2,1)}, bf16[384,1024]{1,0:T(8,128)(2,1)S(1)}, u32[]{:S(2)}, u32[]{:S(2)}) collective-permute-start(bf16[384,1024]{1,0:T(8,128)(2,1)} %get-tuple-element.157), channel_id=1, source_target_pairs={{0,4},{1,5},{2,6},{3,7},{4,0},{5,1},{6,2},{7,3}} | collective-permute-start | bytes 2359304 | tf_op jit(solution)/shard_map/ppermute | solution.py:476
  543.0 51.3 %collective-permute-start.13 = (bf16[128,1024]{1,0:T(8,128)(2,1)}, bf16[128,1024]{1,0:T(8,128)(2,1)S(1)}, u32[]{:S(2)}, u32[]{:S(2)}) collective-permute-start(bf16[128,1024]{1,0:T(8,128)(2,1)} %get-tuple-element.132), channel_id=1, source_target_pairs={{0,3},{1,2},{2,1},{3,0},{4,7},{5,6},{6,5},{7,4}} | collective-permute-start | bytes 786440 | tf_op jit(solution)/shard_map/ppermute | solution.py:476
  643.8 94.3 %collective-permute-start.14 = (bf16[384,1024]{1,0:T(8,128)(2,1)}, bf16[384,1024]{1,0:T(8,128)(2,1)S(1)}, u32[]{:S(2)}, u32[]{:S(2)}) collective-permute-start(bf16[384,1024]{1,0:T(8,128)(2,1)} %get-tuple-element.133), channel_id=1, source_target_pairs={{0,4},{1,5},{2,6},{3,7},{4,0},{5,1},{6,2},{7,3}} | collective-permute-start | bytes 2359304 | tf_op jit(solution)/shard_map/ppermute | solution.py:476
  658.7 79.4 %collective-permute-start.16 = (bf16[384,1024]{1,0:T(8,128)(2,1)}, bf16[384,1024]{1,0:T(8,128)(2,1)S(1)}, u32[]{:S(2)}, u32[]{:S(2)}) collective-permute-start(bf16[384,1024]{1,0:T(8,128)(2,1)} %get-tuple-element.135), channel_id=1, source_target_pairs={{0,6},{1,7},{2,4},{3,5},{4,2},{5,3},{6,0},{7,1}} | collective-permute-start | bytes 2359304 | tf_op jit(solution)/shard_map/ppermute | solution.py:476
  677.7 60.5 %collective-permute-start.5 = (bf16[384,1024]{1,0:T(8,128)(2,1)}, bf16[384,1024]{1,0:T(8,128)(2,1)}, u32[]{:S(2)}, u32[]{:S(2)}) collective-permute-start(bf16[384,1024]{1,0:T(8,128)(2,1)} %get-tuple-element.123), channel_id=1, source_target_pairs={{0,2},{1,3},{2,0},{3,1},{4,6},{5,7},{6,4},{7,5}} | collective-permute-start | bytes 2359304 | tf_op jit(solution)/shard_map/ppermute | solution.py:476
  678.3 66.1 %collective-permute-start.7 = (bf16[384,1024]{1,0:T(8,128)(2,1)}, bf16[384,1024]{1,0:T(8,128)(2,1)}, u32[]{:S(2)}, u32[]{:S(2)}) collective-permute-start(bf16[384,1024]{1,0:T(8,128)(2,1)} %get-tuple-element.125), channel_id=1, source_target_pairs={{0,4},{1,5},{2,6},{3,7},{4,0},{5,1},{6,2},{7,3}} | collective-permute-start | bytes 2359304 | tf_op jit(solution)/shard_map/ppermute | solution.py:476
  692.5 52.0 %collective-permute-start.9 = (bf16[384,1024]{1,0:T(8,128)(2,1)}, bf16[384,1024]{1,0:T(8,128)(2,1)}, u32[]{:S(2)}, u32[]{:S(2)}) collective-permute-start(bf16[384,1024]{1,0:T(8,128)(2,1)} %get-tuple-element.127), channel_id=1, source_target_pairs={{0,6},{1,7},{2,4},{3,5},{4,2},{5,3},{6,0},{7,1}} | collective-permute-start | bytes 2359304 | tf_op jit(solution)/shard_map/ppermute | solution.py:476
  758.7 170.6 %all-gather.12.cloned.1.call-start = ((), (), s32[]{:S(2)}) async-start(), calls=%async_computation.3 | async-start | bytes 18874368 | tf_op jit(solution)/shard_map/all_gather | solution.py:479
  759.4 256.5 %all-gather.14.cloned.1.call-start = ((), (), s32[]{:S(2)}) async-start(), calls=%async_computation.4 | async-start | bytes 18874368 | tf_op jit(solution)/shard_map/all_gather | solution.py:479
  760.2 306.1 %all-gather.8.cloned.1.call-start = ((), (), s32[]{:S(2)}) async-start(), calls=%async_computation.1 | async-start | bytes 9437184 | tf_op jit(solution)/shard_map/all_gather | solution.py:479
  760.7 356.0 %all-gather.10.cloned.1.call-start = ((), (), s32[]{:S(2)}) async-start(), calls=%async_computation.2 | async-start | bytes 9437184 | tf_op jit(solution)/shard_map/all_gather | solution.py:479
  (92 other events, 3681.1 us)
Sparse Core Ops, SparseCore 0:
  758.8 84.4 all-gather.5
  845.1 84.1 all-gather.11
  931.7 84.1 all-gather.13
  1017.6 48.6 all-gather.7
  1068.0 48.6 all-gather.9

commit v3 on v2

--- a/solution.py
+++ b/solution.py
@@ -394,20 +394,16 @@
     )(info, *args)
 
 
-def fwd_kernel(has_alias, split, *refs):
-    x_ref, wu, wd = refs[0], refs[1], refs[1 + split]
-    o_ref, w1s, w2s, sem = refs[2 + split + has_alias:]
-    per_dev = DROWS if split else 2 * DROWS
+def fwd_kernel(has_alias, *refs):
+    x_ref, w = refs[:2]
+    o_ref, w1s, w2s, sem = refs[2 + has_alias:]
     i = pl.program_id(0)
     CH = DROWS
     n_ch = FF // CH
 
     def copies(c):
-        out = []
-        for d in range(8):
-            src = wu.at[pl.ds(per_dev * d + (c // 2) * ROWS, ROWS), pl.ds((c % 2) * CH, CH)]
-            out.append(pltpu.make_async_copy(src, w1s.at[pl.ds(d * ROWS, ROWS), pl.ds(c * CH, CH)], sem.at[0, c]))
-        out.append(pltpu.make_async_copy(wd.at[pl.ds(per_dev * c + per_dev - DROWS, CH), :], w2s.at[pl.ds(c * CH, CH), :], sem.at[1, c]))
+        out = up_copies(w, 2 * DROWS, c, w1s, sem.at[0, c])
+        out.append(pltpu.make_async_copy(w.at[pl.ds(2 * DROWS * c + DROWS, CH), :], w2s.at[pl.ds(c * CH, CH), :], sem.at[1, c]))
         return out
 
     def run(wait):
@@ -435,36 +431,117 @@
         run(False)
 
 
-def fwd_call(stage, layer, x, w, y_prev):
+def up_copies(w, per_dev, c, w1s, sem):
+    out = []
+    for d in range(8):
+        src = w.at[pl.ds(per_dev * d + (c // 2) * ROWS, ROWS), pl.ds((c % 2) * DROWS, DROWS)]
+        out.append(pltpu.make_async_copy(src, w1s.at[pl.ds(d * ROWS, ROWS), pl.ds(c * DROWS, DROWS)], sem))
+    return out
+
+
+def first_kernel(x_ref, wu, a_ref, w1s, sem):
+    i = pl.program_id(0)
+    CH = DROWS
+    n_ch = FF // CH
+
+    def run(wait):
+        x = x_ref[...].reshape(TM, D)
+        for c in range(n_ch):
+            if wait:
+                for cp in up_copies(wu, DROWS, c, w1s, sem.at[c]):
+                    cp.wait()
+            cs = pl.ds(c * CH, CH)
+            a_ref[:, cs] = gelu(dot(x, w1s[:, cs], 1, 0)).astype(BF16)
+
+    @pl.when(i == 0)
+    def _():
+        for c in range(n_ch):
+            for cp in up_copies(wu, DROWS, c, w1s, sem.at[c]):
+                cp.start()
+        run(True)
+
+    @pl.when(i > 0)
+    def _():
+        run(False)
+
+
+def second_kernel(has_alias, *refs):
+    x_ref, a_ref, wd = refs[:3]
+    o_ref, w2s, sem = refs[3 + has_alias:]
+    i = pl.program_id(0)
+    KH = FF // 4
+
+    def copy(c):
+        return pltpu.make_async_copy(wd.at[pl.ds(c * KH, KH), :], w2s.at[pl.ds(c * KH, KH), :], sem.at[c])
+
+    def store(acc):
+        x = x_ref[...].reshape(TM, D)
+        o_ref[...] = (x.astype(F32) + acc).astype(BF16).reshape(o_ref.shape)
+
+    @pl.when(i == 0)
+    def _():
+        for c in range(4):
+            copy(c).start()
+        acc = None
+        for c in range(4):
+            copy(c).wait()
+            part = dot(a_ref[:, pl.ds(c * KH, KH)], w2s[pl.ds(c * KH, KH), :], 1, 0)
+            acc = part if acc is None else acc + part
+        store(acc)
+
+    @pl.when(i > 0)
+    def _():
+        store(dot(a_ref[...], w2s[...], 1, 0))
+
+
+def x_spec_of(stage, layer):
     if layer == 0:
-        x_spec = pl.BlockSpec((1, 1, TM, D), lambda i: (stage, 0, i, 0))
-        out_shape = jax.ShapeDtypeStruct((TOK, D), BF16)
-        o_spec = pl.BlockSpec((TM, D), lambda i: (i, 0))
-    else:
-        x_spec = pl.BlockSpec((TM, D), lambda i: (i, 0))
-        out_shape = jax.ShapeDtypeStruct((2, 1, TOK, D), BF16)
-        o_spec = pl.BlockSpec((1, 1, TM, D), lambda i: (stage, 0, i, 0))
-    split = len(w) - 1
-    args = [x, *w]
-    specs = [x_spec] + [ANY] * len(w)
+        return pl.BlockSpec((1, 1, TM, D), lambda i: (stage, 0, i, 0))
+    return pl.BlockSpec((TM, D), lambda i: (i, 0))
+
+
+def out_of(stage, layer):
+    if layer == 0:
+        return jax.ShapeDtypeStruct((TOK, D), BF16), pl.BlockSpec((TM, D), lambda i: (i, 0))
+    return jax.ShapeDtypeStruct((2, 1, TOK, D), BF16), pl.BlockSpec((1, 1, TM, D), lambda i: (stage, 0, i, 0))
+
+
+def token_call(body, args, specs, out, y_prev, scratch, flops):
+    out_shape, o_spec = out
     aliases = {}
     if y_prev is not None:
-        args.append(y_prev)
-        specs.append(ANY)
-        aliases = {2 + split: 0}
+        aliases = {len(args): 0}
+        args, specs = args + [y_prev], specs + [ANY]
+    if body is not first_kernel:
+        body = functools.partial(body, len(aliases))
     return pl.pallas_call(
-        functools.partial(fwd_kernel, len(aliases), split),
+        body,
         out_shape=out_shape,
-        grid_spec=pltpu.PrefetchScalarGridSpec(
-            num_scalar_prefetch=0, grid=(NB,), in_specs=specs, out_specs=o_spec,
-            scratch_shapes=[pltpu.VMEM((D, FF), BF16), pltpu.VMEM((FF, D), BF16), pltpu.SemaphoreType.DMA((2, FF // DROWS))]),
+        grid_spec=pltpu.PrefetchScalarGridSpec(num_scalar_prefetch=0, grid=(NB,), in_specs=specs, out_specs=o_spec, scratch_shapes=scratch),
         input_output_aliases=aliases,
         compiler_params=pltpu.CompilerParams(dimension_semantics=("arbitrary",), vmem_limit_bytes=60 * 2 ** 20),
-        cost_estimate=pl.CostEstimate(flops=4 * TOK * D * FF, bytes_accessed=26 * 2 ** 20, transcendentals=TOK * FF),
+        cost_estimate=pl.CostEstimate(flops=flops, bytes_accessed=26 * 2 ** 20, transcendentals=TOK * FF),
     )(*args)
 
 
-SEQ = ("bwd_010a", "bwd_010b", "bwd_011", "bwd_110", "adam_01", "dx_01", "bwd_111", "bwd_000", "dx_11", "adam_11", "bwd_001", "bwd_100", "adam_00", "bwd_101", "adam_10", "fwd_00", "fwd_01", "fwd_10", "fwd_11")
+def fwd_call(stage, layer, x, w, y_prev):
+    scratch = [pltpu.VMEM((D, FF), BF16), pltpu.VMEM((FF, D), BF16), pltpu.SemaphoreType.DMA((2, FF // DROWS))]
+    return token_call(fwd_kernel, [x, w], [x_spec_of(stage, layer), ANY], out_of(stage, layer), y_prev, scratch, 4 * TOK * D * FF)
+
+
+def first_call(stage, layer, x, wu):
+    scratch = [pltpu.VMEM((D, FF), BF16), pltpu.SemaphoreType.DMA((FF // DROWS,))]
+    out = jax.ShapeDtypeStruct((TOK, FF), BF16), pl.BlockSpec((TM, FF), lambda i: (i, 0))
+    return token_call(first_kernel, [x, wu], [x_spec_of(stage, layer), ANY], out, None, scratch, 2 * TOK * D * FF)
+
+
+def second_call(stage, layer, x, act, wd, y_prev):
+    scratch = [pltpu.VMEM((FF, D), BF16), pltpu.SemaphoreType.DMA((4,))]
+    specs = [x_spec_of(stage, layer), pl.BlockSpec((TM, FF), lambda i: (i, 0)), ANY]
+    return token_call(second_kernel, [x, act, wd], specs, out_of(stage, layer), y_prev, scratch, 2 * TOK * D * FF)
+
+
+SEQ = ("bwd_010a", "bwd_010b", "bwd_011", "bwd_110", "adam_01", "dx_01", "bwd_111", "bwd_000", "bwd_001", "dx_11", "adam_11", "adam_00", "bwd_100", "bwd_101", "fwd_00", "adam_10", "fwd_01", "fwd_10a", "fwd_10b", "fwd_11a", "fwd_11b")
 
 
 def solution(mesh):
@@ -501,22 +578,33 @@
         for name in SEQ:
             s, l = int(name.split("_")[1][0]), int(name.split("_")[1][1])
             if name.startswith("adam"):
-                split = (s, l) == (1, 1)
-                res = adam_call(s, l, info, recv[s, l], states, outs6, split)
+                res = adam_call(s, l, info, recv[s, l], states, outs6, s == 1)
                 outs6 = tuple(res[:6])
-                if split:
-                    late = res[7]
-                    full[s, l] = [gather(res[6])]
+                w_new = res[6:]
+                if (s, l) == (1, 1):
+                    late = w_new
+                elif (s, l) == (1, 0):
+                    full[s, l] = [gather(w_new[0]), gather(w_new[1])]
+                    full[1, 1].append(gather(lax.optimization_barrier((late[1], w_new[0]))[0]))
                 else:
-                    full[s, l] = [gather(res[6])]
-                if (s, l) == (1, 0):
-                    full[1, 1].append(gather(lax.optimization_barrier((late, res[6]))[0]))
+                    full[s, l] = gather(w_new[0])
+                if (s, l) == (0, 0):
+                    full[1, 1] = [gather(lax.optimization_barrier((late[0], w_new[0]))[0])]
                 continue
             if name.startswith("fwd"):
+                x_in = x_next if l == 0 else hid[s]
+                y_prev = y if l == 1 else None
+                if name.endswith("a"):
+                    act = first_call(s, l, x_in, full[s, l][0])
+                    continue
+                if name.endswith("b"):
+                    out = second_call(s, l, x_in, act, full[s, l][1], y_prev)
+                else:
+                    out = fwd_call(s, l, x_in, full[s, l], y_prev)
                 if l == 0:
-                    hid[s] = fwd_call(s, 0, x_next, full[s, 0], None)
+                    hid[s] = out
                 else:
-                    y = fwd_call(s, 1, hid[s], full[s, 1], y)
+                    y = out
                 continue
             if name.startswith("dx"):
                 own, par = dx_call(s, l, info, dh[s, 0], dh[s, 1], w_up)

time: 1180 us -> 1170 us (level)
  waiting for transfers between devices: 425 us -> 402 us
  Pallas kernels: 667 us -> 685 us
    all_gather x5 -> x6, waiting for transfers between devices: 220 us -> 197 us  [gather(): return lax.all_gather(a, 'fsdp', axis=0, tiled=True)]
    pallas_call x4 -> x6, Pallas kernels: 180 us -> 198 us  [token_call(): pl.pallas_call(body, out_shape=out_shape, grid_spec=pltpu.PrefetchScalarG...]
  transfers between devices with their start and end apart: 67 -> 68, of which waited for: 22 -> 23; matrix products, arithmetic and copies ran while one was open for 0% -> 0% of each run, Pallas kernels for 50% -> 53%
where the time goes in v3:
time: 1170 us; the launch traced here: 1160 us
  Pallas kernels  685 us (59%)
  waiting for transfers between devices  402 us (34%)
  starting transfers between devices  59.6 us (5%)
  between operations  15.3 us (1%)
    pallas_call x9, Pallas kernels, bwd_call(): pl.pallas_call(functools.partial(bwd_kernel, stage, layer, half, mode, pa...  382 us
    ppermute x62, waiting for transfers between devices, swap(): return lax.ppermute(a, 'fsdp', [(d, d ^ r) for d in range(n_dev)])  203 us
    pallas_call x6, Pallas kernels, token_call(): pl.pallas_call(body, out_shape=out_shape, grid_spec=pltpu.PrefetchScalarG...  198 us
    all_gather x6, waiting for transfers between devices, gather(): return lax.all_gather(a, 'fsdp', axis=0, tiled=True)  197 us
    ppermute x62, starting transfers between devices, swap(): return lax.ppermute(a, 'fsdp', [(d, d ^ r) for d in range(n_dev)])  59.3 us
    pallas_call x4, Pallas kernels, adam_call(): pl.pallas_call(functools.partial(adam_kernel, n_alias, split), out_shape=...  57.7 us
    pallas_call x2, Pallas kernels, dx_call(): pl.pallas_call(functools.partial(dx_kernel, stage, layer), out_shape=[jax...  47.3 us
  transfers between devices with their start and end apart: 68, of which 23 were waited for; matrix products, arithmetic and copies ran while one was open for 0% of the time, Pallas kernels for 53%

profile of v3, /device:TPU:0, one launch (start us, length us, event | category | flops | bytes accessed | tf_op | source)
XLA Modules:
  0.0 1164.0 jit_solution(10528842874096208505)
XLA Ops:
  8.1 26.4 %shard_map.185 = (f32[1024,1024]{1,0:T(8,128)}, f32[1024,1024]{1,0:T(8,128)}, bf16[2048,1024]{1,0:T(8,128)(2,1)}) custom-call(s32[1]{0:T(128)} %bitcast.info, bf16[2,2,1,2048,1024]{4,3,2,1,0:T(8,128)(2,1)} %refs_0_.19, bf16[2,2,1,2048,1024]{4,3,2,1,0:T(8,128)(2,1)} %refs_0_.19, bf16[2,1,2048,1024]{3,2,1,0:T(8,128)(2,1)} %refs_2_.17, ...), custom_call_target="tpu_custom_call" | custom-call | flops 17179869184 | bytes 20971520 | tf_op jit(solution)/shard_map/pallas_call | solution.py:224
  45.2 28.1 %shard_map.186 = (bf16[384,1024]{1,0:T(8,128)(2,1)}, bf16[384,1024]{1,0:T(8,128)(2,1)}, bf16[384,1024]{1,0:T(8,128)(2,1)}, bf16[384,1024]{1,0:T(8,128)(2,1)}, bf...) custom-call(s32[1]{0:T(128)} %bitcast.info, ...), custom_call_target="tpu_custom_call" | custom-call | flops 17179869184 | bytes 20971520 | tf_op jit(solution)/shard_map/pallas_call | solution.py:224
  77.5 45.8 %shard_map.187 = (bf16[384,1024]{1,0:T(8,128)(2,1)}, bf16[384,1024]{1,0:T(8,128)(2,1)}, bf16[384,1024]{1,0:T(8,128)(2,1)}, bf16[384,1024]{1,0:T(8,128)(2,1)}, bf...) custom-call(s32[1]{0:T(128)} %bitcast.info, ...), custom_call_target="tpu_custom_call" | custom-call | flops 34359738368 | bytes 41943040 | tf_op jit(solution)/shard_map/pallas_call | solution.py:224
  123.7 23.6 %shard_map.188 = (f32[2048,1024]{1,0:T(8,128)}, f32[2048,1024]{1,0:T(8,128)}) custom-call(s32[1]{0:T(128)} %bitcast.info, bf16[2048,1024]{1,0:T(8,128)(2,1)} %get-tuple-element.139.h0o, bf16[2048,1024]{1,0:T(8,128)(2,1)} %get-tuple-element.142.h0p, bf16[2048,1024]{1,0:T(8,128)(2,1)} %get-tuple-element.143.h1o, bf16[2048,1024]{1,0:T(8,128)(2,1)} %get-tuple-element.144.h1p, ...), custom_call_target="tpu_custom_call" | custom-call | flops 17179869184 | bytes 39845888 | tf_op jit(solution)/shard_map/pallas_call | solution.py:305
  150.8 46.0 %shard_map.181 = (bf16[384,1024]{1,0:T(8,128)(2,1)}, bf16[384,1024]{1,0:T(8,128)(2,1)}, bf16[384,1024]{1,0:T(8,128)(2,1)}, bf16[384,1024]{1,0:T(8,128)(2,1)}, bf...) custom-call(s32[1]{0:T(128)} %bitcast.info, ...), custom_call_target="tpu_custom_call" | custom-call | flops 34359738368 | bytes 41943040 | tf_op jit(solution)/shard_map/pallas_call | solution.py:224
  199.1 45.7 %shard_map.180 = (bf16[384,1024]{1,0:T(8,128)(2,1)}, bf16[384,1024]{1,0:T(8,128)(2,1)}, bf16[384,1024]{1,0:T(8,128)(2,1)}, bf16[384,1024]{1,0:T(8,128)(2,1)}, bf...) custom-call(s32[1]{0:T(128)} %bitcast.info, ...), custom_call_target="tpu_custom_call" | custom-call | flops 34359738368 | bytes 41943040 | tf_op jit(solution)/shard_map/pallas_call | solution.py:224
  275.6 14.9 %collective-permute-done.49.refs_2_.refs_17_ = bf16[384,1024]{1,0:T(8,128)(2,1)} collective-permute-done((bf16[384,1024]{1,0:T(8,128)(2,1)}, bf16[384,1024]{1,0:T(8,128)(2,1)}, u32[]{:S(2)}, u32[]{:S(2)}) %collective-permute-start.49) | collective-permute-done | bytes 786464 | tf_op jit(solution)/shard_map/ppermute | solution.py:553
  290.9 19.4 %collective-permute-done.51.refs_4_.refs_18_ = bf16[384,1024]{1,0:T(8,128)(2,1)} collective-permute-done((bf16[384,1024]{1,0:T(8,128)(2,1)}, bf16[384,1024]{1,0:T(8,128)(2,1)}, u32[]{:S(2)}, u32[]{:S(2)}) %collective-permute-start.51) | collective-permute-done | bytes 786464 | tf_op jit(solution)/shard_map/ppermute | solution.py:553
  313.1 23.7 %shard_map.182 = (f32[2048,1024]{1,0:T(8,128)}, f32[2048,1024]{1,0:T(8,128)}) custom-call(s32[1]{0:T(128)} %bitcast.info, bf16[2048,1024]{1,0:T(8,128)(2,1)} %get-tuple-element.117.h0o, bf16[2048,1024]{1,0:T(8,128)(2,1)} %get-tuple-element.118.h0p, bf16[2048,1024]{1,0:T(8,128)(2,1)} %get-tuple-element.119.h1o, bf16[2048,1024]{1,0:T(8,128)(2,1)} %get-tuple-element.120.h1p, ...), custom_call_target="tpu_custom_call" | custom-call | flops 17179869184 | bytes 39845888 | tf_op jit(solution)/shard_map/pallas_call | solution.py:305
  348.1 18.9 %collective-permute-done.42.refs_10_.refs_21_ = bf16[384,1024]{1,0:T(8,128)(2,1)} collective-permute-done((bf16[384,1024]{1,0:T(8,128)(2,1)}, bf16[384,1024]{1,0:T(8,128)(2,1)}, u32[]{:S(2)}, u32[]{:S(2)}) %collective-permute-start.42) | collective-permute-done | bytes 786464 | tf_op jit(solution)/shard_map/ppermute | solution.py:553
  368.3 17.9 %collective-permute-done.44.refs_12_.refs_22_ = bf16[384,1024]{1,0:T(8,128)(2,1)} collective-permute-done((bf16[384,1024]{1,0:T(8,128)(2,1)S(1)}, bf16[384,1024]{1,0:T(8,128)(2,1)}, u32[]{:S(2)}, u32[]{:S(2)}) %collective-permute-start.44) | collective-permute-done | bytes 786464 | tf_op jit(solution)/shard_map/ppermute | solution.py:553
  389.7 47.5 %shard_map.190 = (bf16[384,1024]{1,0:T(8,128)(2,1)}, bf16[384,1024]{1,0:T(8,128)(2,1)}, bf16[384,1024]{1,0:T(8,128)(2,1)}, bf16[384,1024]{1,0:T(8,128)(2,1)}, bf...) custom-call(s32[1]{0:T(128)} %bitcast.info, ...), custom_call_target="tpu_custom_call" | custom-call | flops 34359738368 | bytes 41943040 | tf_op jit(solution)/shard_map/pallas_call | solution.py:224
  440.4 47.6 %shard_map.189 = (bf16[384,1024]{1,0:T(8,128)(2,1)}, bf16[384,1024]{1,0:T(8,128)(2,1)}, bf16[384,1024]{1,0:T(8,128)(2,1)}, bf16[384,1024]{1,0:T(8,128)(2,1)}, bf...) custom-call(s32[1]{0:T(128)} %bitcast.info, ...), custom_call_target="tpu_custom_call" | custom-call | flops 34359738368 | bytes 41943040 | tf_op jit(solution)/shard_map/pallas_call | solution.py:224
  491.6 47.5 %shard_map.184 = (bf16[384,1024]{1,0:T(8,128)(2,1)}, bf16[384,1024]{1,0:T(8,128)(2,1)}, bf16[384,1024]{1,0:T(8,128)(2,1)}, bf16[384,1024]{1,0:T(8,128)(2,1)}, bf...) custom-call(s32[1]{0:T(128)} %bitcast.info, ...), custom_call_target="tpu_custom_call" | custom-call | flops 34359738368 | bytes 41943040 | tf_op jit(solution)/shard_map/pallas_call | solution.py:224
  544.3 47.8 %shard_map.183 = (bf16[384,1024]{1,0:T(8,128)(2,1)}, bf16[384,1024]{1,0:T(8,128)(2,1)}, bf16[384,1024]{1,0:T(8,128)(2,1)}, bf16[384,1024]{1,0:T(8,128)(2,1)}, bf...) custom-call(s32[1]{0:T(128)} %bitcast.info, ...), custom_call_target="tpu_custom_call" | custom-call | flops 34359738368 | bytes 41943040 | tf_op jit(solution)/shard_map/pallas_call | solution.py:224
  616.5 20.7 %collective-permute-done.8.refs_5_ = bf16[128,1024]{1,0:T(8,128)(2,1)S(1)} collective-permute-done((bf16[128,1024]{1,0:T(8,128)(2,1)}, bf16[128,1024]{1,0:T(8,128)(2,1)S(1)}, u32[]{:S(2)}, u32[]{:S(2)}) %collective-permute-start.8) | collective-permute-done | bytes 262176 | tf_op jit(solution)/shard_map/ppermute | solution.py:553
  661.2 16.3 %collective-permute-done.23.refs_4_.refs_18_ = bf16[384,1024]{1,0:T(8,128)(2,1)S(1)} collective-permute-done((bf16[384,1024]{1,0:T(8,128)(2,1)}, bf16[384,1024]{1,0:T(8,128)(2,1)S(1)}, u32[]{:S(2)}, u32[]{:S(2)}) %collective-permute-start.23) | collective-permute-done | bytes 786464 | tf_op jit(solution)/shard_map/ppermute | solution.py:553
  695.0 14.1 %shard_map.191 = (f32[2,2,128,4096]{3,2,1,0:T(8,128)}, f32[2,2,128,4096]{3,2,1,0:T(8,128)}, f32[2,2,128,4096]{3,2,1,0:T(8,128)}, f32[2,2,2,256,1024]{4,3,2,1,0:T...) custom-call(s32[1]{0:T(128)} %bitcast.info, ...), custom_call_target="tpu_custom_call" | custom-call | flops 838860800 | bytes 41943040 | tf_op jit(solution)/shard_map/pallas_call | solution.py:385
  709.1 14.6 %shard_map.192 = (f32[2,2,128,4096]{3,2,1,0:T(8,128)}, f32[2,2,128,4096]{3,2,1,0:T(8,128)}, f32[2,2,128,4096]{3,2,1,0:T(8,128)}, f32[2,2,2,256,1024]{4,3,2,1,0:T...) custom-call(s32[1]{0:T(128)} %bitcast.info, ...), custom_call_target="tpu_custom_call", output_to_operand_aliasing={{0}: (33, {}), {1}: (34, {}), {2}: (35, {}), {3}: (36, {}),... | custom-call | flops 838860800 | bytes 41943040 | tf_op jit(solution)/shard_map/pallas_call | solution.py:385
  723.8 14.2 %shard_map.193 = (f32[2,2,128,4096]{3,2,1,0:T(8,128)}, f32[2,2,128,4096]{3,2,1,0:T(8,128)}, f32[2,2,128,4096]{3,2,1,0:T(8,128)}, f32[2,2,2,256,1024]{4,3,2,1,0:T...) custom-call(s32[1]{0:T(128)} %bitcast.info, ...), custom_call_target="tpu_custom_call", output_to_operand_aliasing={{0}: (33, {}), {1}: (34, {}), {2}: (35, {}), {3}: (36, {}),... | custom-call | flops 838860800 | bytes 41943040 | tf_op jit(solution)/shard_map/pallas_call | solution.py:385
  744.2 14.8 %shard_map.194 = (f32[2,2,128,4096]{3,2,1,0:T(8,128)}, f32[2,2,128,4096]{3,2,1,0:T(8,128)}, f32[2,2,128,4096]{3,2,1,0:T(8,128)}, f32[2,2,2,256,1024]{4,3,2,1,0:T...) custom-call(s32[1]{0:T(128)} %bitcast.info, ...), custom_call_target="tpu_custom_call", output_to_operand_aliasing={{0}: (33, {}), {1}: (34, {}), {2}: (35, {}), {3}: (36, {}),... | custom-call | flops 838860800 | bytes 41943040 | tf_op jit(solution)/shard_map/pallas_call | solution.py:385
  762.3 45.9 %all-gather.7.cloned.1.call-done.wu = bf16[4096,1024]{1,0:T(8,128)(2,1)} async-done(((bf16[512,1024]{1,0:T(8,128)(2,1)}), bf16[4096,1024]{1,0:T(8,128)(2,1)}) %all-gather.7.cloned.1.call-update) | async-done | bytes 8388624 | tf_op jit(solution)/shard_map/all_gather | solution.py:556
  808.2 29.0 %shard_map.195.refs_1_ = bf16[2048,4096]{1,0:T(8,128)(2,1)} custom-call(bf16[2,1,2048,1024]{3,2,1,0:T(8,128)(2,1)} %refs_0_.21, bf16[4096,1024]{1,0:T(8,128)(2,1)} %all-gather.7.cloned.1.call-done.wu), custom_call_target="tpu_custom_call" | custom-call | flops 17179869184 | bytes 27262976 | tf_op jit(solution)/shard_map/pallas_call | solution.py:517
  837.2 21.6 %all-gather.9.cloned.1.call-done.refs_2_ = bf16[4096,1024]{1,0:T(8,128)(2,1)} async-done(((bf16[512,1024]{1,0:T(8,128)(2,1)}), bf16[4096,1024]{1,0:T(8,128)(2,1)}) %all-gather.9.cloned.1.call-update) | async-done | bytes 8388624 | tf_op jit(solution)/shard_map/all_gather | solution.py:556
  858.8 25.1 %shard_map.196.x_ref.refs_0_ = bf16[2048,1024]{1,0:T(8,128)(2,1)} custom-call(bf16[2,1,2048,1024]{3,2,1,0:T(8,128)(2,1)} %refs_0_.21, bf16[2048,4096]{1,0:T(8,128)(2,1)} %shard_map.195.refs_1_, bf16[4096,1024]{1,0:T(8,128)(2,1)} %all-gather.9.cloned.1.call-done.refs_2_), custom_call_target="tpu_custom_call" | custom-call | flops 17179869184 | bytes 27262976 | tf_op jit(solution)/shard_map/pallas_call | solution.py:517
  883.9 25.4 %all-gather.11.cloned.1.call-done.wu = bf16[4096,1024]{1,0:T(8,128)(2,1)} async-done(((bf16[512,1024]{1,0:T(8,128)(2,1)}), bf16[4096,1024]{1,0:T(8,128)(2,1)}) %all-gather.11.cloned.1.call-update) | async-done | bytes 8388624 | tf_op jit(solution)/shard_map/all_gather | solution.py:556
  909.4 28.9 %shard_map.197.refs_1_ = bf16[2048,4096]{1,0:T(8,128)(2,1)} custom-call(bf16[2048,1024]{1,0:T(8,128)(2,1)} %shard_map.196.x_ref.refs_0_, bf16[4096,1024]{1,0:T(8,128)(2,1)} %all-gather.11.cloned.1.call-done.wu), custom_call_target="tpu_custom_call" | custom-call | flops 17179869184 | bytes 27262976 | tf_op jit(solution)/shard_map/pallas_call | solution.py:517
  938.3 56.9 %all-gather.15.cloned.1.call-done.refs_1_ = bf16[8192,1024]{1,0:T(8,128)(2,1)} async-done(((bf16[1024,1024]{1,0:T(8,128)(2,1)}), bf16[8192,1024]{1,0:T(8,128)(2,1)}) %all-gather.15.cloned.1.call-update) | async-done | bytes 16777232 | tf_op jit(solution)/shard_map/all_gather | solution.py:556
  995.2 44.9 %shard_map.198.refs_0_ = bf16[2048,1024]{1,0:T(8,128)(2,1)} custom-call(bf16[2,1,2048,1024]{3,2,1,0:T(8,128)(2,1)} %refs_0_.21, bf16[8192,1024]{1,0:T(8,128)(2,1)} %all-gather.15.cloned.1.call-done.refs_1_), custom_call_target="tpu_custom_call" | custom-call | flops 34359738368 | bytes 27262976 | tf_op jit(solution)/shard_map/pallas_call | solution.py:517
  1040.2 41.5 %all-gather.17.cloned.1.call-done.refs_1_ = bf16[8192,1024]{1,0:T(8,128)(2,1)} async-done(((bf16[1024,1024]{1,0:T(8,128)(2,1)}), bf16[8192,1024]{1,0:T(8,128)(2,1)}) %all-gather.17.cloned.1.call-update) | async-done | bytes 16777232 | tf_op jit(solution)/shard_map/all_gather | solution.py:556
  1081.7 45.2 %shard_map.199.refs_3_ = bf16[2,1,2048,1024]{3,2,1,0:T(8,128)(2,1)} custom-call(bf16[2048,1024]{1,0:T(8,128)(2,1)} %shard_map.198.refs_0_, bf16[8192,1024]{1,0:T(8,128)(2,1)} %all-gather.17.cloned.1.call-done.refs_1_), custom_call_target="tpu_custom_call" | custom-call | flops 34359738368 | bytes 27262976 | tf_op jit(solution)/shard_map/pallas_call | solution.py:517
  1132.1 24.6 %shard_map.200 = bf16[2,1,2048,1024]{3,2,1,0:T(8,128)(2,1)} custom-call(bf16[2048,1024]{1,0:T(8,128)(2,1)} %shard_map.196.x_ref.refs_0_, bf16[2048,4096]{1,0:T(8,128)(2,1)} %shard_map.197.refs_1_, bf16[4096,1024]{1,0:T(8,128)(2,1)} %all-gather.13.cloned.1.call-done.refs_2_, bf16[2,1,2048,1024]{3,2,1,0:T(8,128)(2,1)} %shard_map.199.refs_3_), custom_call_target="tpu_custom_call", output_to_operand_aliasing={{}: (3, {})} | custom-call | flops 17179869184 | bytes 27262976 | tf_op jit(solution)/shard_map/pallas_call | solution.py:517
  (245 shorter events, 163.9 us)
Async XLA Ops:
  7.2 801.1 %all-gather.7.cloned.1.call-start = ((), (), s32[]{:S(2)}) async-start(), calls=%async_computation | async-start | bytes 9437184 | tf_op jit(solution)/shard_map/all_gather | solution.py:556
  73.3 74.0 %collective-permute-start.48 = (bf16[128,1024]{1,0:T(8,128)(2,1)}, bf16[128,1024]{1,0:T(8,128)(2,1)S(1)}, u32[]{:S(2)}, u32[]{:S(2)}) collective-permute-start(bf16[128,1024]{1,0:T(8,128)(2,1)} %get-tuple-element.180), channel_id=1, source_target_pairs={{0,1},{1,0},{2,3},{3,2},{4,5},{5,4},{6,7},{7,6}} | collective-permute-start | bytes 786440 | tf_op jit(solution)/shard_map/ppermute | solution.py:553
  73.7 75.4 %collective-permute-start.50 = (bf16[128,1024]{1,0:T(8,128)(2,1)}, bf16[128,1024]{1,0:T(8,128)(2,1)S(1)}, u32[]{:S(2)}, u32[]{:S(2)}) collective-permute-start(bf16[128,1024]{1,0:T(8,128)(2,1)} %get-tuple-element.182), channel_id=1, source_target_pairs={{0,3},{1,2},{2,1},{3,0},{4,7},{5,6},{6,5},{7,4}} | collective-permute-start | bytes 786440 | tf_op jit(solution)/shard_map/ppermute | solution.py:553
  76.3 74.1 %collective-permute-start.52 = (bf16[128,1024]{1,0:T(8,128)(2,1)}, bf16[128,1024]{1,0:T(8,128)(2,1)S(1)}, u32[]{:S(2)}, u32[]{:S(2)}) collective-permute-start(bf16[128,1024]{1,0:T(8,128)(2,1)} %get-tuple-element.184), channel_id=1, source_target_pairs={{0,5},{1,4},{2,7},{3,6},{4,1},{5,0},{6,3},{7,2}} | collective-permute-start | bytes 786440 | tf_op jit(solution)/shard_map/ppermute | solution.py:553
  77.5 73.2 %collective-permute-start.54 = (bf16[128,1024]{1,0:T(8,128)(2,1)}, bf16[128,1024]{1,0:T(8,128)(2,1)S(1)}, u32[]{:S(2)}, u32[]{:S(2)}) collective-permute-start(bf16[128,1024]{1,0:T(8,128)(2,1)} %get-tuple-element.186), channel_id=1, source_target_pairs={{0,7},{1,6},{2,5},{3,4},{4,3},{5,2},{6,1},{7,0}} | collective-permute-start | bytes 786440 | tf_op jit(solution)/shard_map/ppermute | solution.py:553
  123.3 73.6 %collective-permute-start.55 = (bf16[128,1024]{1,0:T(8,128)(2,1)}, bf16[128,1024]{1,0:T(8,128)(2,1)S(1)}, u32[]{:S(2)}, u32[]{:S(2)}) collective-permute-start(bf16[128,1024]{1,0:T(8,128)(2,1)} %get-tuple-element.188), channel_id=1, source_target_pairs={{0,1},{1,0},{2,3},{3,2},{4,5},{5,4},{6,7},{7,6}} | collective-permute-start | bytes 786440 | tf_op jit(solution)/shard_map/ppermute | solution.py:553
  150.3 238.3 %collective-permute-start.19 = (f32[2048,1024]{1,0:T(8,128)}, f32[2048,1024]{1,0:T(8,128)}, u32[]{:S(2)}, u32[]{:S(2)}) collective-permute-start(f32[2048,1024]{1,0:T(8,128)} %get-tuple-element.145.refs_6_), channel_id=1, source_target_pairs={{0,1},{1,0},{2,3},{3,2},{4,5},{5,4},{6,7},{7,6}} | collective-permute-start | bytes 25165832 | tf_op jit(solution)/shard_map/ppermute | solution.py:553
  150.7 238.5 %collective-permute-start.18 = (f32[2048,1024]{1,0:T(8,128)}, f32[2048,1024]{1,0:T(8,128)}, u32[]{:S(2)}, u32[]{:S(2)}) collective-permute-start(f32[2048,1024]{1,0:T(8,128)} %get-tuple-element.146.refs_8_), channel_id=1, source_target_pairs={{0,1},{1,0},{2,3},{3,2},{4,5},{5,4},{6,7},{7,6}} | collective-permute-start | bytes 25165832 | tf_op jit(solution)/shard_map/ppermute | solution.py:553
  336.9 151.4 %collective-permute-start.3 = (f32[2048,1024]{1,0:T(8,128)}, f32[2048,1024]{1,0:T(8,128)}, u32[]{:S(2)}, u32[]{:S(2)}) collective-permute-start(f32[2048,1024]{1,0:T(8,128)} %get-tuple-element.121.refs_6_), channel_id=1, source_target_pairs={{0,1},{1,0},{2,3},{3,2},{4,5},{5,4},{6,7},{7,6}} | collective-permute-start | bytes 25165832 | tf_op jit(solution)/shard_map/ppermute | solution.py:553
  346.8 144.0 %collective-permute-start.2 = (f32[2048,1024]{1,0:T(8,128)}, f32[2048,1024]{1,0:T(8,128)}, u32[]{:S(2)}, u32[]{:S(2)}) collective-permute-start(f32[2048,1024]{1,0:T(8,128)} %get-tuple-element.122.refs_8_), channel_id=1, source_target_pairs={{0,1},{1,0},{2,3},{3,2},{4,5},{5,4},{6,7},{7,6}} | collective-permute-start | bytes 25165832 | tf_op jit(solution)/shard_map/ppermute | solution.py:553
  386.2 51.1 %collective-permute-start.46 = (bf16[384,1024]{1,0:T(8,128)(2,1)}, bf16[384,1024]{1,0:T(8,128)(2,1)S(1)}, u32[]{:S(2)}, u32[]{:S(2)}) collective-permute-start(bf16[384,1024]{1,0:T(8,128)(2,1)} %get-tuple-element.177), channel_id=1, source_target_pairs={{0,6},{1,7},{2,4},{3,5},{4,2},{5,3},{6,0},{7,1}} | collective-permute-start | bytes 2359304 | tf_op jit(solution)/shard_map/ppermute | solution.py:553
  388.6 51.1 %collective-permute-start.35 = (bf16[384,1024]{1,0:T(8,128)(2,1)}, bf16[384,1024]{1,0:T(8,128)(2,1)S(1)}, u32[]{:S(2)}, u32[]{:S(2)}) collective-permute-start(bf16[384,1024]{1,0:T(8,128)(2,1)} %get-tuple-element.165), channel_id=1, source_target_pairs={{0,2},{1,3},{2,0},{3,1},{4,6},{5,7},{6,4},{7,5}} | collective-permute-start | bytes 2359304 | tf_op jit(solution)/shard_map/ppermute | solution.py:553
  439.8 51.7 %collective-permute-start.29 = (bf16[128,1024]{1,0:T(8,128)(2,1)}, bf16[128,1024]{1,0:T(8,128)(2,1)S(1)}, u32[]{:S(2)}, u32[]{:S(2)}) collective-permute-start(bf16[128,1024]{1,0:T(8,128)(2,1)} %get-tuple-element.158), channel_id=1, source_target_pairs={{0,3},{1,2},{2,1},{3,0},{4,7},{5,6},{6,5},{7,4}} | collective-permute-start | bytes 786440 | tf_op jit(solution)/shard_map/ppermute | solution.py:553
  488.1 51.1 %collective-permute-start.31 = (bf16[128,1024]{1,0:T(8,128)(2,1)}, bf16[128,1024]{1,0:T(8,128)(2,1)S(1)}, u32[]{:S(2)}, u32[]{:S(2)}) collective-permute-start(bf16[128,1024]{1,0:T(8,128)(2,1)} %get-tuple-element.160), channel_id=1, source_target_pairs={{0,5},{1,4},{2,7},{3,6},{4,1},{5,0},{6,3},{7,2}} | collective-permute-start | bytes 786440 | tf_op jit(solution)/shard_map/ppermute | solution.py:553
  488.3 53.4 %collective-permute-start.33 = (bf16[128,1024]{1,0:T(8,128)(2,1)}, bf16[128,1024]{1,0:T(8,128)(2,1)S(1)}, u32[]{:S(2)}, u32[]{:S(2)}) collective-permute-start(bf16[128,1024]{1,0:T(8,128)(2,1)} %get-tuple-element.162), channel_id=1, source_target_pairs={{0,7},{1,6},{2,5},{3,4},{4,3},{5,2},{6,1},{7,0}} | collective-permute-start | bytes 786440 | tf_op jit(solution)/shard_map/ppermute | solution.py:553
  490.8 51.5 %collective-permute-start.20 = (bf16[128,1024]{1,0:T(8,128)(2,1)}, bf16[128,1024]{1,0:T(8,128)(2,1)S(1)}, u32[]{:S(2)}, u32[]{:S(2)}) collective-permute-start(bf16[128,1024]{1,0:T(8,128)(2,1)} %get-tuple-element.148), channel_id=1, source_target_pairs={{0,1},{1,0},{2,3},{3,2},{4,5},{5,4},{6,7},{7,6}} | collective-permute-start | bytes 786440 | tf_op jit(solution)/shard_map/ppermute | solution.py:553
  490.8 52.0 %collective-permute-start.22 = (bf16[128,1024]{1,0:T(8,128)(2,1)}, bf16[128,1024]{1,0:T(8,128)(2,1)S(1)}, u32[]{:S(2)}, u32[]{:S(2)}) collective-permute-start(bf16[128,1024]{1,0:T(8,128)(2,1)} %get-tuple-element.150), channel_id=1, source_target_pairs={{0,3},{1,2},{2,1},{3,0},{4,7},{5,6},{6,5},{7,4}} | collective-permute-start | bytes 786440 | tf_op jit(solution)/shard_map/ppermute | solution.py:553
  491.4 51.4 %collective-permute-start.24 = (bf16[128,1024]{1,0:T(8,128)(2,1)}, bf16[128,1024]{1,0:T(8,128)(2,1)S(1)}, u32[]{:S(2)}, u32[]{:S(2)}) collective-permute-start(bf16[128,1024]{1,0:T(8,128)(2,1)} %get-tuple-element.152), channel_id=1, source_target_pairs={{0,5},{1,4},{2,7},{3,6},{4,1},{5,0},{6,3},{7,2}} | collective-permute-start | bytes 786440 | tf_op jit(solution)/shard_map/ppermute | solution.py:553
  539.2 52.9 %collective-permute-start.26 = (bf16[128,1024]{1,0:T(8,128)(2,1)S(1)}, bf16[128,1024]{1,0:T(8,128)(2,1)S(1)}, u32[]{:S(2)}, u32[]{:S(2)}) collective-permute-start(bf16[128,1024]{1,0:T(8,128)(2,1)S(1)} %copy-done.50), channel_id=1, source_target_pairs={{0,7},{1,6},{2,5},{3,4},{4,3},{5,2},{6,1},{7,0}} | collective-permute-start | bytes 786440 | tf_op jit(solution)/shard_map/ppermute | solution.py:553
  541.7 100.1 %collective-permute-start.28 = (bf16[384,1024]{1,0:T(8,128)(2,1)}, bf16[384,1024]{1,0:T(8,128)(2,1)S(1)}, u32[]{:S(2)}, u32[]{:S(2)}) collective-permute-start(bf16[384,1024]{1,0:T(8,128)(2,1)} %get-tuple-element.157), channel_id=1, source_target_pairs={{0,2},{1,3},{2,0},{3,1},{4,6},{5,7},{6,4},{7,5}} | collective-permute-start | bytes 2359304 | tf_op jit(solution)/shard_map/ppermute | solution.py:553
  542.3 99.8 %collective-permute-start.30 = (bf16[384,1024]{1,0:T(8,128)(2,1)}, bf16[384,1024]{1,0:T(8,128)(2,1)S(1)}, u32[]{:S(2)}, u32[]{:S(2)}) collective-permute-start(bf16[384,1024]{1,0:T(8,128)(2,1)} %get-tuple-element.159), channel_id=1, source_target_pairs={{0,4},{1,5},{2,6},{3,7},{4,0},{5,1},{6,2},{7,3}} | collective-permute-start | bytes 2359304 | tf_op jit(solution)/shard_map/ppermute | solution.py:553
  542.8 51.2 %collective-permute-start.13 = (bf16[128,1024]{1,0:T(8,128)(2,1)}, bf16[128,1024]{1,0:T(8,128)(2,1)S(1)}, u32[]{:S(2)}, u32[]{:S(2)}) collective-permute-start(bf16[128,1024]{1,0:T(8,128)(2,1)} %get-tuple-element.134), channel_id=1, source_target_pairs={{0,3},{1,2},{2,1},{3,0},{4,7},{5,6},{6,5},{7,4}} | collective-permute-start | bytes 786440 | tf_op jit(solution)/shard_map/ppermute | solution.py:553
  643.6 94.3 %collective-permute-start.14 = (bf16[384,1024]{1,0:T(8,128)(2,1)}, bf16[384,1024]{1,0:T(8,128)(2,1)S(1)}, u32[]{:S(2)}, u32[]{:S(2)}) collective-permute-start(bf16[384,1024]{1,0:T(8,128)(2,1)} %get-tuple-element.135), channel_id=1, source_target_pairs={{0,4},{1,5},{2,6},{3,7},{4,0},{5,1},{6,2},{7,3}} | collective-permute-start | bytes 2359304 | tf_op jit(solution)/shard_map/ppermute | solution.py:553
  658.6 79.4 %collective-permute-start.16 = (bf16[384,1024]{1,0:T(8,128)(2,1)}, bf16[384,1024]{1,0:T(8,128)(2,1)S(1)}, u32[]{:S(2)}, u32[]{:S(2)}) collective-permute-start(bf16[384,1024]{1,0:T(8,128)(2,1)} %get-tuple-element.137), channel_id=1, source_target_pairs={{0,6},{1,7},{2,4},{3,5},{4,2},{5,3},{6,0},{7,1}} | collective-permute-start | bytes 2359304 | tf_op jit(solution)/shard_map/ppermute | solution.py:553
  677.5 60.5 %collective-permute-start.5 = (bf16[384,1024]{1,0:T(8,128)(2,1)}, bf16[384,1024]{1,0:T(8,128)(2,1)}, u32[]{:S(2)}, u32[]{:S(2)}) collective-permute-start(bf16[384,1024]{1,0:T(8,128)(2,1)} %get-tuple-element.125), channel_id=1, source_target_pairs={{0,2},{1,3},{2,0},{3,1},{4,6},{5,7},{6,4},{7,5}} | collective-permute-start | bytes 2359304 | tf_op jit(solution)/shard_map/ppermute | solution.py:553
  678.1 66.1 %collective-permute-start.7 = (bf16[384,1024]{1,0:T(8,128)(2,1)}, bf16[384,1024]{1,0:T(8,128)(2,1)}, u32[]{:S(2)}, u32[]{:S(2)}) collective-permute-start(bf16[384,1024]{1,0:T(8,128)(2,1)} %get-tuple-element.127), channel_id=1, source_target_pairs={{0,4},{1,5},{2,6},{3,7},{4,0},{5,1},{6,2},{7,3}} | collective-permute-start | bytes 2359304 | tf_op jit(solution)/shard_map/ppermute | solution.py:553
  692.3 51.9 %collective-permute-start.9 = (bf16[384,1024]{1,0:T(8,128)(2,1)}, bf16[384,1024]{1,0:T(8,128)(2,1)}, u32[]{:S(2)}, u32[]{:S(2)}) collective-permute-start(bf16[384,1024]{1,0:T(8,128)(2,1)} %get-tuple-element.129), channel_id=1, source_target_pairs={{0,6},{1,7},{2,4},{3,5},{4,2},{5,3},{6,0},{7,1}} | collective-permute-start | bytes 2359304 | tf_op jit(solution)/shard_map/ppermute | solution.py:553
  759.1 99.7 %all-gather.9.cloned.1.call-start = ((), (), s32[]{:S(2)}) async-start(), calls=%async_computation.1 | async-start | bytes 9437184 | tf_op jit(solution)/shard_map/all_gather | solution.py:556
  759.9 149.5 %all-gather.11.cloned.1.call-start = ((), (), s32[]{:S(2)}) async-start(), calls=%async_computation.2 | async-start | bytes 9437184 | tf_op jit(solution)/shard_map/all_gather | solution.py:556
  760.6 234.6 %all-gather.15.cloned.1.call-start = ((), (), s32[]{:S(2)}) async-start(), calls=%async_computation.4 | async-start | bytes 18874368 | tf_op jit(solution)/shard_map/all_gather | solution.py:556
  761.2 320.5 %all-gather.17.cloned.1.call-start = ((), (), s32[]{:S(2)}) async-start(), calls=%async_computation.5 | async-start | bytes 18874368 | tf_op jit(solution)/shard_map/all_gather | solution.py:556
  761.8 370.3 %all-gather.13.cloned.1.call-start = ((), (), s32[]{:S(2)}) async-start(), calls=%async_computation.3 | async-start | bytes 9437184 | tf_op jit(solution)/shard_map/all_gather | solution.py:556
  (93 other events, 3731.7 us)
Sparse Core Ops, SparseCore 0:
  759.2 48.9 all-gather.6
  810.1 48.6 all-gather.8
  860.6 48.6 all-gather.10
  911.0 84.1 all-gather.14
  997.5 84.1 all-gather.16
  1083.4 48.6 all-gather.12

commit v4 on v2

--- a/solution.py
+++ b/solution.py
@@ -55,36 +55,49 @@
     return h * (0.5 * t + 0.5)
 
 
-def bwd_kernel(stage, layer, half, mode, part, info, *refs):
+def flip(v, mask):
+    total = 0
+    for b in range(3):
+        bit = lax.rem(lax.div(v, 2 ** b), 2)
+        total = total + 2 ** b * (1 - bit if (mask >> b) & 1 else bit)
+    return total
+
+
+def bwd_kernel(stage, layer, half, mode, part, *refs):
     it = iter(refs)
     take = lambda k: [next(it) for _ in range(k)]
-    xo, xp, do, dp, w_up, w_down = take(6)
+    info = next(it) if part == "all" else None
+    if part == "all":
+        xo, xp, do, dp, w_up, w_down = take(6)
+    else:
+        xo, do, w_up, w_down = take(4)
     n_extra = {1: 0, 3: 2}[mode]
     extra_own, extra_par = take(n_extra), take(n_extra)
-    sums_in = take(2) if part == "par" else None
-    if part == "own":
-        sums_out = take(2)
-    else:
-        outs_even, outs_odd = take(4), take(4)
+    outs_even, outs_odd = take(4), take(4)
     if mode != 3:
-        dho = next(it) if part != "par" else None
-        dhp = next(it) if part != "own" else None
-    xb, db, w1s, w2s, acc1, acc2, act, dhs, insem, wsem, ssem = take(11)
+        dho, dhp = take(2)
+    if part == "swap":
+        xp, dp = take(2)
+    xb, db, w1s, w2s, acc1, acc2, act, dhs, insem, wsem = take(10)
     eb, esem = take(2) if n_extra else (None, None)
     outsem = next(it) if mode != 3 else None
+    if part == "swap":
+        send_sem, recv_sem = take(2)
     i = pl.program_id(0)
-    n = 2 * NB if part == "all" else NB
-    base = NB if part == "par" else 0
+    n = 2 * NB
     slot = lax.rem(i, 2)
-    me = info[0]
+    me = info[0] if part == "all" else lax.axis_index('fsdp')
     core = lax.rem(me, 2)
     chip = lax.div(me, 2)
+    partner = flip(me, 1)
 
     def in_copies(own, j, slot):
         rows = pl.ds(pl.multiple_of(j * TM, TM), TM)
         xs, ds, es = (xo, do, extra_own) if own else (xp, dp, extra_par)
-        out = [pltpu.make_async_copy(xs.at[stage, layer, 0, rows], xb.at[slot], insem.at[0, slot]),
-               pltpu.make_async_copy(ds.at[stage, 0, rows], db.at[slot], insem.at[1, slot])]
+        xs = xs.at[rows] if len(xs.shape) == 2 else xs.at[stage, layer, 0, rows]
+        ds = ds.at[rows] if len(ds.shape) == 2 else ds.at[stage, 0, rows]
+        out = [pltpu.make_async_copy(xs, xb.at[slot], insem.at[0, slot]),
+               pltpu.make_async_copy(ds, db.at[slot], insem.at[1, slot])]
         for k, e in enumerate(es):
             out.append(pltpu.make_async_copy(e.at[rows], eb.at[k, slot], esem.at[k, slot]))
         return out
@@ -108,26 +121,36 @@
             out.append(pltpu.make_async_copy(w_down.at[stage, layer, pl.ds(f0, BW), :], w2s.at[pl.ds(j * BW, BW), :], wsem.at[1, j]))
         return out
 
+    def swap_copies():
+        pairs = ((xo.at[stage, layer, 0], xp), (do.at[stage, 0], dp))
+        return [pltpu.make_async_remote_copy(src_ref=a, dst_ref=b, send_sem=send_sem.at[k], recv_sem=recv_sem.at[k], device_id=(partner,), device_id_type=pl.DeviceIdType.MESH)
+                for k, (a, b) in enumerate(pairs)]
+
     @pl.when(i == 0)
     def _():
-        fetch(base, 0)
+        fetch(0, 0)
         for c in w_copies():
             c.start()
-        if part == "par":
-            loads = [pltpu.make_async_copy(a, b, ssem.at[k]) for k, (a, b) in enumerate(zip(sums_in, (acc1, acc2)))]
-            for c in loads:
+        if part == "swap":
+            barrier = pltpu.get_barrier_semaphore()
+            pl.semaphore_signal(barrier, inc=1, device_id=(partner,), device_id_type=pl.DeviceIdType.MESH)
+            pl.semaphore_wait(barrier, 1)
+            for c in swap_copies():
                 c.start()
-            for c in loads:
-                c.wait()
-        else:
-            acc1[...] = jnp.zeros_like(acc1)
-            acc2[...] = jnp.zeros_like(acc2)
+        acc1[...] = jnp.zeros_like(acc1)
+        acc2[...] = jnp.zeros_like(acc2)
         for c in w_copies():
             c.wait()
 
+    if part == "swap":
+        @pl.when(i == NB - 1)
+        def _():
+            for c in swap_copies():
+                c.wait()
+
     @pl.when(i + 1 < n)
     def _():
-        fetch(base + i + 1, 1 - slot)
+        fetch(i + 1, 1 - slot)
 
     for c in in_copies(True, 0, slot):
         c.wait()
@@ -139,7 +162,7 @@
     if mode != 3:
         @pl.when(i >= 2)
         def _():
-            dh_copy(part != "par", 0, slot).wait()
+            dh_copy(True, 0, slot).wait()
 
     CH = 256
     n_ch = FC // CH
@@ -166,69 +189,61 @@
     for c in range(n_ch):
         back(c)
     if mode != 3:
-        if part != "par":
-            @pl.when(i < NB)
-            def _():
-                dh_copy(True, i, slot).start()
-
-        if part != "own":
-            @pl.when(i + base >= NB)
-            def _():
-                dh_copy(False, i + base - NB, slot).start()
+        @pl.when(i < NB)
+        def _():
+            dh_copy(True, i, slot).start()
+
+        @pl.when(i >= NB)
+        def _():
+            dh_copy(False, i - NB, slot).start()
 
     @pl.when(i == n - 1)
     def _():
-        if part == "own":
-            saves = [pltpu.make_async_copy(a, b, ssem.at[k]) for k, (a, b) in enumerate(zip((acc1, acc2), sums_out))]
-            for c in saves:
-                c.start()
-            for c in saves:
-                c.wait()
-        else:
-            for q in range(4):
-                dev = jnp.bitwise_xor(me, 2 * q)
-                oc = jnp.bitwise_xor(chip, q)
-                outs_even[q][0:ROWS, :] = acc1[pl.ds(pl.multiple_of(dev * ROWS, ROWS), ROWS), :].astype(BF16)
-                outs_even[q][ROWS:ROWS + BW, :] = acc2[pl.ds(pl.multiple_of(oc * BW, BW), BW), :].astype(BF16)
-                dev = jnp.bitwise_xor(me, 2 * q + 1)
-                outs_odd[q][...] = acc1[pl.ds(pl.multiple_of(dev * ROWS, ROWS), ROWS), :].astype(BF16)
+        for q in range(4):
+            dev = flip(me, 2 * q)
+            oc = flip(chip, q)
+            outs_even[q][0:ROWS, :] = acc1[pl.ds(pl.multiple_of(dev * ROWS, ROWS), ROWS), :].astype(BF16)
+            outs_even[q][ROWS:ROWS + BW, :] = acc2[pl.ds(pl.multiple_of(oc * BW, BW), BW), :].astype(BF16)
+            dev = flip(me, 2 * q + 1)
+            outs_odd[q][...] = acc1[pl.ds(pl.multiple_of(dev * ROWS, ROWS), ROWS), :].astype(BF16)
         if mode != 3:
-            dh_copy(part != "par", 0, 0).wait()
-            dh_copy(part != "par", 0, 1).wait()
-
-
-def bwd_call(stage, layer, half, mode, part, info, base_args, extra_own=(), extra_par=(), sums=()):
-    sum_shapes = [jax.ShapeDtypeStruct((D, FC), F32), jax.ShapeDtypeStruct((FC, D), F32)]
-    if part == "own":
-        out_shape, out_specs = list(sum_shapes), [ANY] * 2
-    else:
-        out_shape = [jax.ShapeDtypeStruct((ROWS + BW, FC), BF16)] * 4 + [jax.ShapeDtypeStruct((ROWS, FC), BF16)] * 4
-        out_specs = [pl.BlockSpec((ROWS + BW, FC), lambda i, s: (0, 0))] * 4 + [pl.BlockSpec((ROWS, FC), lambda i, s: (0, 0))] * 4
+            dh_copy(True, 0, 0).wait()
+            dh_copy(True, 0, 1).wait()
+
+
+def bwd_call(stage, layer, half, mode, part, info, base_args, extra_own=(), extra_par=()):
+    out_shape = [jax.ShapeDtypeStruct((ROWS + BW, FC), BF16)] * 4 + [jax.ShapeDtypeStruct((ROWS, FC), BF16)] * 4
+    out_specs = [pl.BlockSpec((ROWS + BW, FC), lambda *_: (0, 0))] * 4 + [pl.BlockSpec((ROWS, FC), lambda *_: (0, 0))] * 4
     scratch = [
         pltpu.VMEM((2, TM, D), BF16), pltpu.VMEM((2, TM, D), BF16),
         pltpu.VMEM((D, FC), BF16), pltpu.VMEM((FC, D), BF16),
         pltpu.VMEM((D, FC), F32), pltpu.VMEM((FC, D), F32),
         pltpu.VMEM((TM, FC), BF16), pltpu.VMEM((2, TM, FC), BF16),
-        pltpu.SemaphoreType.DMA((2, 2)), pltpu.SemaphoreType.DMA((2, 4)), pltpu.SemaphoreType.DMA((2,)),
+        pltpu.SemaphoreType.DMA((2, 2)), pltpu.SemaphoreType.DMA((2, 4)),
     ]
-    args = list(base_args) + list(extra_own) + list(extra_par) + list(sums)
+    args = list(base_args) + list(extra_own) + list(extra_par)
     n_extra = len(extra_own)
     if n_extra:
         scratch += [pltpu.VMEM((n_extra, 2, TM, D), F32), pltpu.SemaphoreType.DMA((n_extra, 2))]
-    n_tok = 2 * TOK if part == "all" else TOK
     if mode != 3:
-        k = 2 if part == "all" else 1
-        out_shape += [jax.ShapeDtypeStruct((TOK, FC), BF16)] * k
-        out_specs += [ANY] * k
+        out_shape += [jax.ShapeDtypeStruct((TOK, FC), BF16)] * 2
+        out_specs += [ANY] * 2
         scratch += [pltpu.SemaphoreType.DMA((2,))]
-    return pl.pallas_call(
+    params = dict(dimension_semantics=("arbitrary",), vmem_limit_bytes=60 * 2 ** 20)
+    if part == "swap":
+        out_shape += [jax.ShapeDtypeStruct((TOK, D), BF16)] * 2
+        out_specs += [ANY] * 2
+        scratch += [pltpu.SemaphoreType.DMA((2,)), pltpu.SemaphoreType.DMA((2,))]
+        params.update(collective_id=0, has_side_effects=True)
+    call = pl.pallas_call(
         functools.partial(bwd_kernel, stage, layer, half, mode, part),
         out_shape=out_shape,
         grid_spec=pltpu.PrefetchScalarGridSpec(
-            num_scalar_prefetch=1, grid=(n_tok // TM,), in_specs=[ANY] * len(args), out_specs=out_specs, scratch_shapes=scratch),
-        compiler_params=pltpu.CompilerParams(dimension_semantics=("arbitrary",), vmem_limit_bytes=60 * 2 ** 20),
-        cost_estimate=pl.CostEstimate(flops=8 * n_tok * D * FC, bytes_accessed=n_tok * 10 * 2 ** 10, transcendentals=n_tok * FC),
-    )(info, *args)
+            num_scalar_prefetch=int(part == "all"), grid=(2 * NB,), in_specs=[ANY] * len(args), out_specs=out_specs, scratch_shapes=scratch),
+        compiler_params=pltpu.CompilerParams(**params),
+        cost_estimate=pl.CostEstimate(flops=16 * TOK * D * FC, bytes_accessed=40 * 2 ** 20, transcendentals=2 * TOK * FC),
+    )
+    return call(*args) if part == "swap" else call(info, *args)
 
 
 def dx_kernel(stage, layer, info, h0o, h0p, h1o, h1p, w_up, dxo, dxp, dhb, w1s, dxb, insem, wsem, outsem):
@@ -464,7 +479,7 @@
     )(*args)
 
 
-SEQ = ("bwd_010a", "bwd_010b", "bwd_011", "bwd_110", "adam_01", "dx_01", "bwd_111", "bwd_000", "dx_11", "adam_11", "bwd_001", "bwd_100", "adam_00", "bwd_101", "adam_10", "fwd_00", "fwd_01", "fwd_10", "fwd_11")
+SEQ = ("bwd_010", "bwd_011", "bwd_110", "adam_01", "dx_01", "bwd_111", "bwd_000", "dx_11", "adam_11", "bwd_001", "bwd_100", "adam_00", "bwd_101", "adam_10", "fwd_00", "fwd_01", "fwd_10", "fwd_11")
 
 
 def solution(mesh):
@@ -484,7 +499,6 @@
 
         g_par = swap(grad_out, 1)
         x_par = swap(x_saved, 1)
-        base_own = (x_saved, x_saved, grad_out, grad_out, w_up, w_down)
         base = (x_saved, x_par, grad_out, g_par, w_up, w_down)
 
         down5 = lambda a: a.reshape(2, 2, HALVES, BW, D)
@@ -523,16 +537,14 @@
                 dx[s] = ((own, swap(par, 1)), (par, swap(own, 1)))
                 continue
             half = int(name[6])
-            if name == "bwd_010a":
-                sum1, sum2, dh_own = bwd_call(s, l, half, 1, "own", info, base_own)
-                continue
-            if name == "bwd_010b":
-                outs = bwd_call(s, l, half, 1, "par", info, base, sums=(sum1, sum2))
-                dh[s, half] = (dh_own, outs[8])
+            if name == "bwd_010":
+                outs = bwd_call(s, l, half, 1, "swap", info, (x_saved, grad_out, w_up, w_down))
+                dh[s, half] = tuple(outs[8:10])
+                landed = (x_saved, outs[10], grad_out, outs[11], w_up, w_down)
             elif l == 0:
                 outs = bwd_call(s, l, half, 3, "all", info, base, *dx[s])
             else:
-                outs = bwd_call(s, l, half, 1, "all", info, base)
+                outs = bwd_call(s, l, half, 1, "all", info, landed if name == "bwd_011" else base)
                 dh[s, half] = tuple(outs[8:])
             msgs = [outs[0], outs[4], outs[1], outs[5], outs[2], outs[6], outs[3], outs[7]]
             recv.setdefault((s, l), []).append([msgs[0]] + [swap(msgs[r], r) for r in range(1, 8)])

time: 1180 us -> 1100 us (0.932)
  waiting for transfers between devices: 425 us -> 327 us
  Pallas kernels: 667 us -> 691 us
    all_gather x5, waiting for transfers between devices: 220 us -> 48.2 us  [gather(): return lax.all_gather(a, 'fsdp', axis=0, tiled=True)]
    ppermute x62, waiting for transfers between devices: 203 us -> 277 us  [swap(): return lax.ppermute(a, 'fsdp', [(d, d ^ r) for d in range(n_dev)])]
    pallas_call x9 -> x8, Pallas kernels: 383 us -> 404 us  [bwd_call(): return call(*args) if part == 'swap' else call(info, *args)]
  transfers between devices with their start and end apart: 67 -> 67, of which waited for: 22 -> 20; matrix products, arithmetic and copies ran while one was open for 0% -> 0% of each run, Pallas kernels for 50% -> 58%
where the time goes in v4:
time: 1100 us; the launch traced here: 1090 us
  Pallas kernels  691 us (63%)
  waiting for transfers between devices  327 us (30%)
  starting transfers between devices  52.4 us (5%)
  between operations  14.9 us (1%)
    pallas_call x8, Pallas kernels, bwd_call(): return call(*args) if part == 'swap' else call(info, *args)  404 us
    ppermute x62, waiting for transfers between devices, swap(): return lax.ppermute(a, 'fsdp', [(d, d ^ r) for d in range(n_dev)])  277 us
    pallas_call x4, Pallas kernels, fwd_call(): pl.pallas_call(functools.partial(fwd_kernel, len(aliases), split), out_sh...  181 us
    pallas_call x4, Pallas kernels, adam_call(): pl.pallas_call(functools.partial(adam_kernel, n_alias, split), out_shape=...  57.2 us
    ppermute x62, starting transfers between devices, swap(): return lax.ppermute(a, 'fsdp', [(d, d ^ r) for d in range(n_dev)])  52.2 us
    all_gather x5, waiting for transfers between devices, gather(): return lax.all_gather(a, 'fsdp', axis=0, tiled=True)  48.2 us
    pallas_call x2, Pallas kernels, dx_call(): pl.pallas_call(functools.partial(dx_kernel, stage, layer), out_shape=[jax...  48.1 us
  transfers between devices with their start and end apart: 67, of which 20 were waited for; matrix products, arithmetic and copies ran while one was open for 0% of the time, Pallas kernels for 58%

profile of v4, /device:TPU:0, one launch (start us, length us, event | category | flops | bytes accessed | tf_op | source)
XLA Modules:
  0.0 1089.6 jit_solution(4411043855273420842)
XLA Ops:
  8.1 76.8 %shard_map.185 = (bf16[384,1024]{1,0:T(8,128)(2,1)}, bf16[384,1024]{1,0:T(8,128)(2,1)}, bf16[384,1024]{1,0:T(8,128)(2,1)}, bf16[384,1024]{1,0:T(8,128)(2,1)}, bf...) custom-call(bf16[2,2,1,2048,1024]{4,3,2,1,0:T(8,128)(2,1)} %refs_1_., ...), custom_call_target="tpu_custom_call" | custom-call | flops 34359738368 | bytes 41943040 | tf_op jit(solution)/shard_map/pallas_call | solution.py:246
  90.3 45.6 %shard_map.186 = (bf16[384,1024]{1,0:T(8,128)(2,1)}, bf16[384,1024]{1,0:T(8,128)(2,1)}, bf16[384,1024]{1,0:T(8,128)(2,1)}, bf16[384,1024]{1,0:T(8,128)(2,1)}, bf...) custom-call(s32[1]{0:T(128)} %bitcast.refs_0_.info, ...), custom_call_target="tpu_custom_call" | custom-call | flops 34359738368 | bytes 41943040 | tf_op jit(solution)/shard_map/pallas_call | solution.py:246
  138.2 23.8 %shard_map.187 = (f32[2048,1024]{1,0:T(8,128)}, f32[2048,1024]{1,0:T(8,128)}) custom-call(s32[1]{0:T(128)} %bitcast.refs_0_.info, bf16[2048,1024]{1,0:T(8,128)(2,1)} %get-tuple-element.137.h0o, bf16[2048,1024]{1,0:T(8,128)(2,1)} %get-tuple-element.138.h0p, bf16[2048,1024]{1,0:T(8,128)(2,1)} %get-tuple-element.141.h1o, ...), custom_call_target="tpu_custom_call" | custom-call | flops 17179869184 | bytes 39845888 | tf_op jit(solution)/shard_map/pallas_call | solution.py:320
  172.1 19.6 %collective-permute-done.49.refs_2_.refs_17_ = bf16[384,1024]{1,0:T(8,128)(2,1)} collective-permute-done((bf16[384,1024]{1,0:T(8,128)(2,1)}, bf16[384,1024]{1,0:T(8,128)(2,1)}, u32[]{:S(2)}, u32[]{:S(2)}) %collective-permute-start.49) | collective-permute-done | bytes 786464 | tf_op jit(solution)/shard_map/ppermute | solution.py:491
  192.3 18.8 %collective-permute-done.51.refs_4_.refs_18_ = bf16[384,1024]{1,0:T(8,128)(2,1)} collective-permute-done((bf16[384,1024]{1,0:T(8,128)(2,1)}, bf16[384,1024]{1,0:T(8,128)(2,1)}, u32[]{:S(2)}, u32[]{:S(2)}) %collective-permute-start.51) | collective-permute-done | bytes 786464 | tf_op jit(solution)/shard_map/ppermute | solution.py:491
  214.6 45.7 %shard_map.181 = (bf16[384,1024]{1,0:T(8,128)(2,1)}, bf16[384,1024]{1,0:T(8,128)(2,1)}, bf16[384,1024]{1,0:T(8,128)(2,1)}, bf16[384,1024]{1,0:T(8,128)(2,1)}, bf...) custom-call(s32[1]{0:T(128)} %bitcast.refs_0_.info, ...), custom_call_target="tpu_custom_call" | custom-call | flops 34359738368 | bytes 41943040 | tf_op jit(solution)/shard_map/pallas_call | solution.py:246
  262.4 46.0 %shard_map.180 = (bf16[384,1024]{1,0:T(8,128)(2,1)}, bf16[384,1024]{1,0:T(8,128)(2,1)}, bf16[384,1024]{1,0:T(8,128)(2,1)}, bf16[384,1024]{1,0:T(8,128)(2,1)}, bf...) custom-call(s32[1]{0:T(128)} %bitcast.refs_0_.info, ...), custom_call_target="tpu_custom_call" | custom-call | flops 34359738368 | bytes 41943040 | tf_op jit(solution)/shard_map/pallas_call | solution.py:246
  313.0 47.4 %shard_map.189 = (bf16[384,1024]{1,0:T(8,128)(2,1)}, bf16[384,1024]{1,0:T(8,128)(2,1)}, bf16[384,1024]{1,0:T(8,128)(2,1)}, bf16[384,1024]{1,0:T(8,128)(2,1)}, bf...) custom-call(s32[1]{0:T(128)} %bitcast.refs_0_.info, ...), custom_call_target="tpu_custom_call" | custom-call | flops 34359738368 | bytes 41943040 | tf_op jit(solution)/shard_map/pallas_call | solution.py:246
  365.7 47.6 %shard_map.188 = (bf16[384,1024]{1,0:T(8,128)(2,1)}, bf16[384,1024]{1,0:T(8,128)(2,1)}, bf16[384,1024]{1,0:T(8,128)(2,1)}, bf16[384,1024]{1,0:T(8,128)(2,1)}, bf...) custom-call(s32[1]{0:T(128)} %bitcast.refs_0_.info, ...), custom_call_target="tpu_custom_call" | custom-call | flops 34359738368 | bytes 41943040 | tf_op jit(solution)/shard_map/pallas_call | solution.py:246
  416.5 10.6 collective-permute-done.31.refs_13_
  437.6 22.2 %collective-permute-done.24.refs_5_ = bf16[128,1024]{1,0:T(8,128)(2,1)S(1)} collective-permute-done((bf16[128,1024]{1,0:T(8,128)(2,1)}, bf16[128,1024]{1,0:T(8,128)(2,1)S(1)}, u32[]{:S(2)}, u32[]{:S(2)}) %collective-permute-start.24) | collective-permute-done | bytes 262176 | tf_op jit(solution)/shard_map/ppermute | solution.py:491
  465.4 15.7 %collective-permute-done.35.refs_2_.refs_17_ = bf16[384,1024]{1,0:T(8,128)(2,1)S(1)} collective-permute-done((bf16[384,1024]{1,0:T(8,128)(2,1)}, bf16[384,1024]{1,0:T(8,128)(2,1)S(1)}, u32[]{:S(2)}, u32[]{:S(2)}) %collective-permute-start.35) | collective-permute-done | bytes 786464 | tf_op jit(solution)/shard_map/ppermute | solution.py:491
  481.1 18.1 %collective-permute-done.37.refs_4_.refs_18_ = bf16[384,1024]{1,0:T(8,128)(2,1)S(1)} collective-permute-done((bf16[384,1024]{1,0:T(8,128)(2,1)}, bf16[384,1024]{1,0:T(8,128)(2,1)S(1)}, u32[]{:S(2)}, u32[]{:S(2)}) %collective-permute-start.37) | collective-permute-done | bytes 786464 | tf_op jit(solution)/shard_map/ppermute | solution.py:491
  501.2 13.6 %collective-permute-done.28.refs_10_.refs_21_ = bf16[384,1024]{1,0:T(8,128)(2,1)S(1)} collective-permute-done((bf16[384,1024]{1,0:T(8,128)(2,1)}, bf16[384,1024]{1,0:T(8,128)(2,1)S(1)}, u32[]{:S(2)}, u32[]{:S(2)}) %collective-permute-start.28) | collective-permute-done | bytes 786464 | tf_op jit(solution)/shard_map/ppermute | solution.py:491
  514.9 14.3 %shard_map.190 = (f32[2,2,128,4096]{3,2,1,0:T(8,128)}, f32[2,2,128,4096]{3,2,1,0:T(8,128)}, f32[2,2,128,4096]{3,2,1,0:T(8,128)}, f32[2,2,2,256,1024]{4,3,2,1,0:T...) custom-call(s32[1]{0:T(128)} %bitcast.refs_0_.info, ...), custom_call_target="tpu_custom_call" | custom-call | flops 838860800 | bytes 41943040 | tf_op jit(solution)/shard_map/pallas_call | solution.py:400
  529.3 14.7 %shard_map.191 = (f32[2,2,128,4096]{3,2,1,0:T(8,128)}, f32[2,2,128,4096]{3,2,1,0:T(8,128)}, f32[2,2,128,4096]{3,2,1,0:T(8,128)}, f32[2,2,2,256,1024]{4,3,2,1,0:T...) custom-call(s32[1]{0:T(128)} %bitcast.refs_0_.info, ...), custom_call_target="tpu_custom_call", output_to_operand_aliasing={{0}: (33, {}), {1}: (34, {}), {2}: (35, {}), {3}: (36, {}),... | custom-call | flops 838860800 | bytes 41943040 | tf_op jit(solution)/shard_map/pallas_call | solution.py:400
  548.7 16.9 %collective-permute-done.23.refs_4_.refs_18_ = bf16[384,1024]{1,0:T(8,128)(2,1)} collective-permute-done((bf16[384,1024]{1,0:T(8,128)(2,1)}, bf16[384,1024]{1,0:T(8,128)(2,1)}, u32[]{:S(2)}, u32[]{:S(2)}) %collective-permute-start.23) | collective-permute-done | bytes 786464 | tf_op jit(solution)/shard_map/ppermute | solution.py:491
  565.6 14.2 %shard_map.192 = (f32[2,2,128,4096]{3,2,1,0:T(8,128)}, f32[2,2,128,4096]{3,2,1,0:T(8,128)}, f32[2,2,128,4096]{3,2,1,0:T(8,128)}, f32[2,2,2,256,1024]{4,3,2,1,0:T...) custom-call(s32[1]{0:T(128)} %bitcast.refs_0_.info, ...), custom_call_target="tpu_custom_call", output_to_operand_aliasing={{0}: (33, {}), {1}: (34, {}), {2}: (35, {}), {3}: (36, {}),... | custom-call | flops 838860800 | bytes 41943040 | tf_op jit(solution)/shard_map/pallas_call | solution.py:400
  580.7 24.3 %shard_map.182 = (f32[2048,1024]{1,0:T(8,128)}, f32[2048,1024]{1,0:T(8,128)}) custom-call(s32[1]{0:T(128)} %bitcast.refs_0_.info, bf16[2048,1024]{1,0:T(8,128)(2,1)} %get-tuple-element.115.h0o, bf16[2048,1024]{1,0:T(8,128)(2,1)} %get-tuple-element.116.h0p, bf16[2048,1024]{1,0:T(8,128)(2,1)} %get-tuple-element.117.h1o, ...), custom_call_target="tpu_custom_call" | custom-call | flops 17179869184 | bytes 39845888 | tf_op jit(solution)/shard_map/pallas_call | solution.py:320
  605.5 16.5 %collective-permute-done.3.refs_10_ = f32[2048,1024]{1,0:T(8,128)} collective-permute-done((f32[2048,1024]{1,0:T(8,128)}, f32[2048,1024]{1,0:T(8,128)}, u32[]{:S(2)}, u32[]{:S(2)}) %collective-permute-start.3) | collective-permute-done | bytes 8388640 | tf_op jit(solution)/shard_map/ppermute | solution.py:491
  622.1 16.3 %collective-permute-done.2.refs_8_ = f32[2048,1024]{1,0:T(8,128)} collective-permute-done((f32[2048,1024]{1,0:T(8,128)}, f32[2048,1024]{1,0:T(8,128)}, u32[]{:S(2)}, u32[]{:S(2)}) %collective-permute-start.2) | collective-permute-done | bytes 8388640 | tf_op jit(solution)/shard_map/ppermute | solution.py:491
  638.4 47.8 %shard_map.184 = (bf16[384,1024]{1,0:T(8,128)(2,1)}, bf16[384,1024]{1,0:T(8,128)(2,1)}, bf16[384,1024]{1,0:T(8,128)(2,1)}, bf16[384,1024]{1,0:T(8,128)(2,1)}, bf...) custom-call(s32[1]{0:T(128)} %bitcast.refs_0_.info, ...), custom_call_target="tpu_custom_call" | custom-call | flops 34359738368 | bytes 41943040 | tf_op jit(solution)/shard_map/pallas_call | solution.py:246
  690.6 47.5 %shard_map.183 = (bf16[384,1024]{1,0:T(8,128)(2,1)}, bf16[384,1024]{1,0:T(8,128)(2,1)}, bf16[384,1024]{1,0:T(8,128)(2,1)}, bf16[384,1024]{1,0:T(8,128)(2,1)}, bf...) custom-call(s32[1]{0:T(128)} %bitcast.refs_0_.info, ...), custom_call_target="tpu_custom_call" | custom-call | flops 34359738368 | bytes 41943040 | tf_op jit(solution)/shard_map/pallas_call | solution.py:246
  766.4 37.5 %collective-permute-done.14.refs_12_.refs_22_ = bf16[384,1024]{1,0:T(8,128)(2,1)S(1)} collective-permute-done((bf16[384,1024]{1,0:T(8,128)(2,1)}, bf16[384,1024]{1,0:T(8,128)(2,1)S(1)}, u32[]{:S(2)}, u32[]{:S(2)}) %collective-permute-start.14) | collective-permute-done | bytes 786464 | tf_op jit(solution)/shard_map/ppermute | solution.py:491
  803.9 11.7 %collective-permute-done.5.refs_2_.refs_17_ = bf16[384,1024]{1,0:T(8,128)(2,1)S(1)} collective-permute-done((bf16[384,1024]{1,0:T(8,128)(2,1)}, bf16[384,1024]{1,0:T(8,128)(2,1)S(1)}, u32[]{:S(2)}, u32[]{:S(2)}) %collective-permute-start.5) | collective-permute-done | bytes 786464 | tf_op jit(solution)/shard_map/ppermute | solution.py:491
  815.6 22.0 %collective-permute-done.7.refs_4_.refs_18_ = bf16[384,1024]{1,0:T(8,128)(2,1)S(1)} collective-permute-done((bf16[384,1024]{1,0:T(8,128)(2,1)}, bf16[384,1024]{1,0:T(8,128)(2,1)S(1)}, u32[]{:S(2)}, u32[]{:S(2)}) %collective-permute-start.7) | collective-permute-done | bytes 786464 | tf_op jit(solution)/shard_map/ppermute | solution.py:491
  838.4 14.1 %shard_map.193 = (f32[2,2,128,4096]{3,2,1,0:T(8,128)}, f32[2,2,128,4096]{3,2,1,0:T(8,128)}, f32[2,2,128,4096]{3,2,1,0:T(8,128)}, f32[2,2,2,256,1024]{4,3,2,1,0:T...) custom-call(s32[1]{0:T(128)} %bitcast.refs_0_.info, ...), custom_call_target="tpu_custom_call", output_to_operand_aliasing={{0}: (33, {}), {1}: (34, {}), {2}: (35, {}), {3}: (36, {}),... | custom-call | flops 838860800 | bytes 41943040 | tf_op jit(solution)/shard_map/pallas_call | solution.py:400
  853.8 45.3 %shard_map.195.refs_0_ = bf16[2048,1024]{1,0:T(8,128)(2,1)} custom-call(bf16[2,1,2048,1024]{3,2,1,0:T(8,128)(2,1)} %refs_0_.5, bf16[8192,1024]{1,0:T(8,128)(2,1)} %all-gather.12.cloned.1.call-done.refs_1_), custom_call_target="tpu_custom_call" | custom-call | flops 34359738368 | bytes 27262976 | tf_op jit(solution)/shard_map/pallas_call | solution.py:470
  899.1 45.2 %shard_map.196.refs_3_ = bf16[2,1,2048,1024]{3,2,1,0:T(8,128)(2,1)} custom-call(bf16[2048,1024]{1,0:T(8,128)(2,1)} %shard_map.195.refs_0_, bf16[8192,1024]{1,0:T(8,128)(2,1)} %all-gather.14.cloned.1.call-done.refs_1_), custom_call_target="tpu_custom_call" | custom-call | flops 34359738368 | bytes 27262976 | tf_op jit(solution)/shard_map/pallas_call | solution.py:470
  944.4 45.2 %shard_map.194.refs_0_ = bf16[2048,1024]{1,0:T(8,128)(2,1)} custom-call(bf16[2,1,2048,1024]{3,2,1,0:T(8,128)(2,1)} %refs_0_.5, bf16[8192,1024]{1,0:T(8,128)(2,1)} %all-gather.6.cloned.1.call-done.refs_1_), custom_call_target="tpu_custom_call" | custom-call | flops 34359738368 | bytes 27262976 | tf_op jit(solution)/shard_map/pallas_call | solution.py:470
  989.6 48.1 %all-gather.10.cloned.1.call-done.refs_2_ = bf16[4096,1024]{1,0:T(8,128)(2,1)} async-done(((bf16[512,1024]{1,0:T(8,128)(2,1)}), bf16[4096,1024]{1,0:T(8,128)(2,1)}) %all-gather.10.cloned.1.call-update) | async-done | bytes 8388624 | tf_op jit(solution)/shard_map/all_gather | solution.py:494
  1037.7 45.0 %shard_map.197 = bf16[2,1,2048,1024]{3,2,1,0:T(8,128)(2,1)} custom-call(bf16[2048,1024]{1,0:T(8,128)(2,1)} %shard_map.194.refs_0_, bf16[4096,1024]{1,0:T(8,128)(2,1)} %all-gather.8.cloned.1.call-done.refs_1_, bf16[4096,1024]{1,0:T(8,128)(2,1)} %all-gather.10.cloned.1.call-done.refs_2_, ...), custom_call_target="tpu_custom_call", output_to_operand_aliasing={{}: (3, {})} | custom-call | flops 34359738368 | bytes 27262976 | tf_op jit(solution)/shard_map/pallas_call | solution.py:470
  (233 shorter events, 96.4 us)
Async XLA Ops:
  7.2 846.6 %all-gather.12.cloned.1.call-start = ((), (), s32[]{:S(2)}) async-start(), calls=%async_computation.3 | async-start | bytes 18874368 | tf_op jit(solution)/shard_map/all_gather | solution.py:494
  7.2 205.9 %collective-permute-start = (bf16[2,2,1,2048,1024]{4,3,2,1,0:T(8,128)(2,1)}, bf16[2,2,1,2048,1024]{4,3,2,1,0:T(8,128)(2,1)}, u32[]{:S(2)}, u32[]{:S(2)}) collective-permute-start(bf16[2,2,1,2048,1024]{4,3,2,1,0:T(8,128)(2,1)} %refs_1_.15), channel_id=1, source_target_pairs={{0,1},{1,0},{2,3},{3,2},{4,5},{5,4},{6,7},{7,6}} | collective-permute-start | bytes 50331656 | tf_op jit(solution)/shard_map/ppermute | solution.py:491
  8.1 204.1 %collective-permute-start.1 = (bf16[2,1,2048,1024]{3,2,1,0:T(8,128)(2,1)}, bf16[2,1,2048,1024]{3,2,1,0:T(8,128)(2,1)}, u32[]{:S(2)}, u32[]{:S(2)}) collective-permute-start(bf16[2,1,2048,1024]{3,2,1,0:T(8,128)(2,1)} %refs_3_.15), channel_id=1, source_target_pairs={{0,1},{1,0},{2,3},{3,2},{4,5},{5,4},{6,7},{7,6}} | collective-permute-start | bytes 25165832 | tf_op jit(solution)/shard_map/ppermute | solution.py:491
  85.3 50.6 %collective-permute-start.50 = (bf16[128,1024]{1,0:T(8,128)(2,1)}, bf16[128,1024]{1,0:T(8,128)(2,1)S(1)}, u32[]{:S(2)}, u32[]{:S(2)}) collective-permute-start(bf16[128,1024]{1,0:T(8,128)(2,1)} %get-tuple-element.180), channel_id=1, source_target_pairs={{0,3},{1,2},{2,1},{3,0},{4,7},{5,6},{6,5},{7,4}} | collective-permute-start | bytes 786440 | tf_op jit(solution)/shard_map/ppermute | solution.py:491
  162.1 147.6 %collective-permute-start.19 = (f32[2048,1024]{1,0:T(8,128)}, f32[2048,1024]{1,0:T(8,128)}, u32[]{:S(2)}, u32[]{:S(2)}) collective-permute-start(f32[2048,1024]{1,0:T(8,128)} %get-tuple-element.143.refs_7_), channel_id=1, source_target_pairs={{0,1},{1,0},{2,3},{3,2},{4,5},{5,4},{6,7},{7,6}} | collective-permute-start | bytes 25165832 | tf_op jit(solution)/shard_map/ppermute | solution.py:491
  162.5 148.4 %collective-permute-start.18 = (f32[2048,1024]{1,0:T(8,128)}, f32[2048,1024]{1,0:T(8,128)}, u32[]{:S(2)}, u32[]{:S(2)}) collective-permute-start(f32[2048,1024]{1,0:T(8,128)} %get-tuple-element.144.refs_9_), channel_id=1, source_target_pairs={{0,1},{1,0},{2,3},{3,2},{4,5},{5,4},{6,7},{7,6}} | collective-permute-start | bytes 25165832 | tf_op jit(solution)/shard_map/ppermute | solution.py:491
  308.5 52.0 %collective-permute-start.45 = (bf16[128,1024]{1,0:T(8,128)(2,1)}, bf16[128,1024]{1,0:T(8,128)(2,1)S(1)}, u32[]{:S(2)}, u32[]{:S(2)}) collective-permute-start(bf16[128,1024]{1,0:T(8,128)(2,1)} %get-tuple-element.174), channel_id=1, source_target_pairs={{0,5},{1,4},{2,7},{3,6},{4,1},{5,0},{6,3},{7,2}} | collective-permute-start | bytes 786440 | tf_op jit(solution)/shard_map/ppermute | solution.py:491
  309.7 52.1 %collective-permute-start.47 = (bf16[128,1024]{1,0:T(8,128)(2,1)}, bf16[128,1024]{1,0:T(8,128)(2,1)S(1)}, u32[]{:S(2)}, u32[]{:S(2)}) collective-permute-start(bf16[128,1024]{1,0:T(8,128)(2,1)} %get-tuple-element.176), channel_id=1, source_target_pairs={{0,7},{1,6},{2,5},{3,4},{4,3},{5,2},{6,1},{7,0}} | collective-permute-start | bytes 786440 | tf_op jit(solution)/shard_map/ppermute | solution.py:491
  310.9 52.7 %collective-permute-start.34 = (bf16[128,1024]{1,0:T(8,128)(2,1)}, bf16[128,1024]{1,0:T(8,128)(2,1)S(1)}, u32[]{:S(2)}, u32[]{:S(2)}) collective-permute-start(bf16[128,1024]{1,0:T(8,128)(2,1)} %get-tuple-element.162), channel_id=1, source_target_pairs={{0,1},{1,0},{2,3},{3,2},{4,5},{5,4},{6,7},{7,6}} | collective-permute-start | bytes 786440 | tf_op jit(solution)/shard_map/ppermute | solution.py:491
  310.9 54.0 %collective-permute-start.36 = (bf16[128,1024]{1,0:T(8,128)(2,1)}, bf16[128,1024]{1,0:T(8,128)(2,1)S(1)}, u32[]{:S(2)}, u32[]{:S(2)}) collective-permute-start(bf16[128,1024]{1,0:T(8,128)(2,1)} %get-tuple-element.164), channel_id=1, source_target_pairs={{0,3},{1,2},{2,1},{3,0},{4,7},{5,6},{6,5},{7,4}} | collective-permute-start | bytes 786440 | tf_op jit(solution)/shard_map/ppermute | solution.py:491
  311.9 53.7 %collective-permute-start.38 = (bf16[128,1024]{1,0:T(8,128)(2,1)}, bf16[128,1024]{1,0:T(8,128)(2,1)S(1)}, u32[]{:S(2)}, u32[]{:S(2)}) collective-permute-start(bf16[128,1024]{1,0:T(8,128)(2,1)} %get-tuple-element.166), channel_id=1, source_target_pairs={{0,5},{1,4},{2,7},{3,6},{4,1},{5,0},{6,3},{7,2}} | collective-permute-start | bytes 786440 | tf_op jit(solution)/shard_map/ppermute | solution.py:491
  361.2 100.6 %collective-permute-start.42 = (bf16[384,1024]{1,0:T(8,128)(2,1)}, bf16[384,1024]{1,0:T(8,128)(2,1)S(1)}, u32[]{:S(2)}, u32[]{:S(2)}) collective-permute-start(bf16[384,1024]{1,0:T(8,128)(2,1)} %get-tuple-element.171), channel_id=1, source_target_pairs={{0,2},{1,3},{2,0},{3,1},{4,6},{5,7},{6,4},{7,5}} | collective-permute-start | bytes 2359304 | tf_op jit(solution)/shard_map/ppermute | solution.py:491
  362.5 102.3 %collective-permute-start.44 = (bf16[384,1024]{1,0:T(8,128)(2,1)}, bf16[384,1024]{1,0:T(8,128)(2,1)S(1)}, u32[]{:S(2)}, u32[]{:S(2)}) collective-permute-start(bf16[384,1024]{1,0:T(8,128)(2,1)} %get-tuple-element.173), channel_id=1, source_target_pairs={{0,4},{1,5},{2,6},{3,7},{4,0},{5,1},{6,2},{7,3}} | collective-permute-start | bytes 2359304 | tf_op jit(solution)/shard_map/ppermute | solution.py:491
  365.5 50.5 %collective-permute-start.29 = (bf16[128,1024]{1,0:T(8,128)(2,1)}, bf16[128,1024]{1,0:T(8,128)(2,1)S(1)}, u32[]{:S(2)}, u32[]{:S(2)}) collective-permute-start(bf16[128,1024]{1,0:T(8,128)(2,1)} %get-tuple-element.156), channel_id=1, source_target_pairs={{0,3},{1,2},{2,1},{3,0},{4,7},{5,6},{6,5},{7,4}} | collective-permute-start | bytes 786440 | tf_op jit(solution)/shard_map/ppermute | solution.py:491
  465.3 78.6 %collective-permute-start.30 = (bf16[384,1024]{1,0:T(8,128)(2,1)}, bf16[384,1024]{1,0:T(8,128)(2,1)S(1)}, u32[]{:S(2)}, u32[]{:S(2)}) collective-permute-start(bf16[384,1024]{1,0:T(8,128)(2,1)} %get-tuple-element.157), channel_id=1, source_target_pairs={{0,4},{1,5},{2,6},{3,7},{4,0},{5,1},{6,2},{7,3}} | collective-permute-start | bytes 2359304 | tf_op jit(solution)/shard_map/ppermute | solution.py:491
  481.1 62.8 %collective-permute-start.32 = (bf16[384,1024]{1,0:T(8,128)(2,1)}, bf16[384,1024]{1,0:T(8,128)(2,1)S(1)}, u32[]{:S(2)}, u32[]{:S(2)}) collective-permute-start(bf16[384,1024]{1,0:T(8,128)(2,1)} %get-tuple-element.159), channel_id=1, source_target_pairs={{0,6},{1,7},{2,4},{3,5},{4,2},{5,3},{6,0},{7,1}} | collective-permute-start | bytes 2359304 | tf_op jit(solution)/shard_map/ppermute | solution.py:491
  500.7 64.9 %collective-permute-start.23 = (bf16[384,1024]{1,0:T(8,128)(2,1)}, bf16[384,1024]{1,0:T(8,128)(2,1)}, u32[]{:S(2)}, u32[]{:S(2)}) collective-permute-start(bf16[384,1024]{1,0:T(8,128)(2,1)} %get-tuple-element.149), channel_id=1, source_target_pairs={{0,4},{1,5},{2,6},{3,7},{4,0},{5,1},{6,2},{7,3}} | collective-permute-start | bytes 2359304 | tf_op jit(solution)/shard_map/ppermute | solution.py:491
  514.9 50.7 %collective-permute-start.25 = (bf16[384,1024]{1,0:T(8,128)(2,1)}, bf16[384,1024]{1,0:T(8,128)(2,1)}, u32[]{:S(2)}, u32[]{:S(2)}) collective-permute-start(bf16[384,1024]{1,0:T(8,128)(2,1)} %get-tuple-element.151), channel_id=1, source_target_pairs={{0,6},{1,7},{2,4},{3,5},{4,2},{5,3},{6,0},{7,1}} | collective-permute-start | bytes 2359304 | tf_op jit(solution)/shard_map/ppermute | solution.py:491
  579.9 319.3 %all-gather.14.cloned.1.call-start = ((), (), s32[]{:S(2)}) async-start(), calls=%async_computation.4 | async-start | bytes 18874368 | tf_op jit(solution)/shard_map/all_gather | solution.py:494
  580.6 363.7 %all-gather.6.cloned.1.call-start = ((), (), s32[]{:S(2)}) async-start(), calls=%async_computation | async-start | bytes 18874368 | tf_op jit(solution)/shard_map/all_gather | solution.py:494
  686.2 52.0 %collective-permute-start.11 = (bf16[128,1024]{1,0:T(8,128)(2,1)}, bf16[128,1024]{1,0:T(8,128)(2,1)S(1)}, u32[]{:S(2)}, u32[]{:S(2)}) collective-permute-start(bf16[128,1024]{1,0:T(8,128)(2,1)} %get-tuple-element.130), channel_id=1, source_target_pairs={{0,1},{1,0},{2,3},{3,2},{4,5},{5,4},{6,7},{7,6}} | collective-permute-start | bytes 786440 | tf_op jit(solution)/shard_map/ppermute | solution.py:491
  686.3 51.9 %collective-permute-start.13 = (bf16[128,1024]{1,0:T(8,128)(2,1)}, bf16[128,1024]{1,0:T(8,128)(2,1)S(1)}, u32[]{:S(2)}, u32[]{:S(2)}) collective-permute-start(bf16[128,1024]{1,0:T(8,128)(2,1)} %get-tuple-element.132), channel_id=1, source_target_pairs={{0,3},{1,2},{2,1},{3,0},{4,7},{5,6},{6,5},{7,4}} | collective-permute-start | bytes 786440 | tf_op jit(solution)/shard_map/ppermute | solution.py:491
  687.4 51.9 %collective-permute-start.15 = (bf16[128,1024]{1,0:T(8,128)(2,1)}, bf16[128,1024]{1,0:T(8,128)(2,1)S(1)}, u32[]{:S(2)}, u32[]{:S(2)}) collective-permute-start(bf16[128,1024]{1,0:T(8,128)(2,1)} %get-tuple-element.134), channel_id=1, source_target_pairs={{0,5},{1,4},{2,7},{3,6},{4,1},{5,0},{6,3},{7,2}} | collective-permute-start | bytes 786440 | tf_op jit(solution)/shard_map/ppermute | solution.py:491
  687.7 51.9 %collective-permute-start.17 = (bf16[128,1024]{1,0:T(8,128)(2,1)}, bf16[128,1024]{1,0:T(8,128)(2,1)S(1)}, u32[]{:S(2)}, u32[]{:S(2)}) collective-permute-start(bf16[128,1024]{1,0:T(8,128)(2,1)} %get-tuple-element.136), channel_id=1, source_target_pairs={{0,7},{1,6},{2,5},{3,4},{4,3},{5,2},{6,1},{7,0}} | collective-permute-start | bytes 786440 | tf_op jit(solution)/shard_map/ppermute | solution.py:491
  689.5 75.8 %collective-permute-start.12 = (bf16[384,1024]{1,0:T(8,128)(2,1)}, bf16[384,1024]{1,0:T(8,128)(2,1)S(1)}, u32[]{:S(2)}, u32[]{:S(2)}) collective-permute-start(bf16[384,1024]{1,0:T(8,128)(2,1)} %get-tuple-element.131), channel_id=1, source_target_pairs={{0,2},{1,3},{2,0},{3,1},{4,6},{5,7},{6,4},{7,5}} | collective-permute-start | bytes 2359304 | tf_op jit(solution)/shard_map/ppermute | solution.py:491
  741.6 62.3 %collective-permute-start.14 = (bf16[384,1024]{1,0:T(8,128)(2,1)}, bf16[384,1024]{1,0:T(8,128)(2,1)S(1)}, u32[]{:S(2)}, u32[]{:S(2)}) collective-permute-start(bf16[384,1024]{1,0:T(8,128)(2,1)} %get-tuple-element.133), channel_id=1, source_target_pairs={{0,4},{1,5},{2,6},{3,7},{4,0},{5,1},{6,2},{7,3}} | collective-permute-start | bytes 2359304 | tf_op jit(solution)/shard_map/ppermute | solution.py:491
  752.7 51.2 %collective-permute-start.16 = (bf16[384,1024]{1,0:T(8,128)(2,1)}, bf16[384,1024]{1,0:T(8,128)(2,1)S(1)}, u32[]{:S(2)}, u32[]{:S(2)}) collective-permute-start(bf16[384,1024]{1,0:T(8,128)(2,1)} %get-tuple-element.135), channel_id=1, source_target_pairs={{0,6},{1,7},{2,4},{3,5},{4,2},{5,3},{6,0},{7,1}} | collective-permute-start | bytes 2359304 | tf_op jit(solution)/shard_map/ppermute | solution.py:491
  754.6 60.9 %collective-permute-start.5 = (bf16[384,1024]{1,0:T(8,128)(2,1)}, bf16[384,1024]{1,0:T(8,128)(2,1)S(1)}, u32[]{:S(2)}, u32[]{:S(2)}) collective-permute-start(bf16[384,1024]{1,0:T(8,128)(2,1)} %get-tuple-element.123), channel_id=1, source_target_pairs={{0,2},{1,3},{2,0},{3,1},{4,6},{5,7},{6,4},{7,5}} | collective-permute-start | bytes 2359304 | tf_op jit(solution)/shard_map/ppermute | solution.py:491
  763.8 73.7 %collective-permute-start.7 = (bf16[384,1024]{1,0:T(8,128)(2,1)}, bf16[384,1024]{1,0:T(8,128)(2,1)S(1)}, u32[]{:S(2)}, u32[]{:S(2)}) collective-permute-start(bf16[384,1024]{1,0:T(8,128)(2,1)} %get-tuple-element.125), channel_id=1, source_target_pairs={{0,4},{1,5},{2,6},{3,7},{4,0},{5,1},{6,2},{7,3}} | collective-permute-start | bytes 2359304 | tf_op jit(solution)/shard_map/ppermute | solution.py:491
  765.4 72.2 %collective-permute-start.9 = (bf16[384,1024]{1,0:T(8,128)(2,1)}, bf16[384,1024]{1,0:T(8,128)(2,1)}, u32[]{:S(2)}, u32[]{:S(2)}) collective-permute-start(bf16[384,1024]{1,0:T(8,128)(2,1)} %get-tuple-element.127), channel_id=1, source_target_pairs={{0,6},{1,7},{2,4},{3,5},{4,2},{5,3},{6,0},{7,1}} | collective-permute-start | bytes 2359304 | tf_op jit(solution)/shard_map/ppermute | solution.py:491
  852.6 137.0 %all-gather.8.cloned.1.call-start = ((), (), s32[]{:S(2)}) async-start(), calls=%async_computation.1 | async-start | bytes 9437184 | tf_op jit(solution)/shard_map/all_gather | solution.py:494
  853.1 184.6 %all-gather.10.cloned.1.call-start = ((), (), s32[]{:S(2)}) async-start(), calls=%async_computation.2 | async-start | bytes 9437184 | tf_op jit(solution)/shard_map/all_gather | solution.py:494
  (89 other events, 3119.1 us)
Sparse Core Ops, SparseCore 0:
  580.0 84.1 all-gather.11
  666.0 134.9 all-gather.13
  852.7 84.1 all-gather.5
  938.6 48.6 all-gather.7
  989.0 48.6 all-gather.9

commit v5 on v4

--- a/solution.py
+++ b/solution.py
@@ -229,7 +229,7 @@
         out_shape += [jax.ShapeDtypeStruct((TOK, FC), BF16)] * 2
         out_specs += [ANY] * 2
         scratch += [pltpu.SemaphoreType.DMA((2,))]
-    params = dict(dimension_semantics=("arbitrary",), vmem_limit_bytes=60 * 2 ** 20)
+    params = dict(dimension_semantics=("arbitrary",), vmem_limit_bytes=63 * 2 ** 20)
     if part == "swap":
         out_shape += [jax.ShapeDtypeStruct((TOK, D), BF16)] * 2
         out_specs += [ANY] * 2
@@ -324,7 +324,7 @@
             num_scalar_prefetch=1, grid=(2 * NB,), in_specs=[ANY] * 5, out_specs=[ANY] * 2,
             scratch_shapes=[pltpu.VMEM((2, TM, HALVES * FC), BF16), pltpu.VMEM((D, HALVES * FC), BF16), pltpu.VMEM((2, TM, D), F32),
                             pltpu.SemaphoreType.DMA((2, 2)), pltpu.SemaphoreType.DMA((2, 4)), pltpu.SemaphoreType.DMA((2,))]),
-        compiler_params=pltpu.CompilerParams(dimension_semantics=("arbitrary",), vmem_limit_bytes=60 * 2 ** 20),
+        compiler_params=pltpu.CompilerParams(dimension_semantics=("arbitrary",), vmem_limit_bytes=63 * 2 ** 20),
         cost_estimate=pl.CostEstimate(flops=4 * TOK * D * HALVES * FC, bytes_accessed=38 * 2 ** 20, transcendentals=0),
     )(info, *args)
 
@@ -404,7 +404,7 @@
             num_scalar_prefetch=1, grid=(nj,), in_specs=specs,
             out_specs=[st_up] * 3 + [st_down] * 3 + [pl.BlockSpec(w.shape, lambda j, s: (0, 0)) for w in w_shapes]),
         input_output_aliases={n_in + k: k for k in range(n_alias)},
-        compiler_params=pltpu.CompilerParams(dimension_semantics=("arbitrary",), vmem_limit_bytes=60 * 2 ** 20),
+        compiler_params=pltpu.CompilerParams(dimension_semantics=("arbitrary",), vmem_limit_bytes=63 * 2 ** 20),
         cost_estimate=pl.CostEstimate(flops=20 * 2 ** 20 * 40, bytes_accessed=40 * 2 ** 20, transcendentals=2 ** 20),
     )(info, *args)
 
@@ -474,7 +474,7 @@
             num_scalar_prefetch=0, grid=(NB,), in_specs=specs, out_specs=o_spec,
             scratch_shapes=[pltpu.VMEM((D, FF), BF16), pltpu.VMEM((FF, D), BF16), pltpu.SemaphoreType.DMA((2, FF // DROWS))]),
         input_output_aliases=aliases,
-        compiler_params=pltpu.CompilerParams(dimension_semantics=("arbitrary",), vmem_limit_bytes=60 * 2 ** 20),
+        compiler_params=pltpu.CompilerParams(dimension_semantics=("arbitrary",), vmem_limit_bytes=63 * 2 ** 20),
         cost_estimate=pl.CostEstimate(flops=4 * TOK * D * FF, bytes_accessed=26 * 2 ** 20, transcendentals=TOK * FF),
     )(*args)
 

time: 1100 us -> 1100 us (level)
  no operation moved by 1% of the time
where the time goes in v5:
time: 1100 us; the launch traced here: 1090 us
  Pallas kernels  690 us (63%)
  waiting for transfers between devices  324 us (29%)
  starting transfers between devices  56.5 us (5%)
  between operations  14.6 us (1%)
    pallas_call x8, Pallas kernels, bwd_call(): return call(*args) if part == 'swap' else call(info, *args)  405 us
    ppermute x62, waiting for transfers between devices, swap(): return lax.ppermute(a, 'fsdp', [(d, d ^ r) for d in range(n_dev)])  274 us
    pallas_call x4, Pallas kernels, fwd_call(): pl.pallas_call(functools.partial(fwd_kernel, len(aliases), split), out_sh...  181 us
    pallas_call x4, Pallas kernels, adam_call(): pl.pallas_call(functools.partial(adam_kernel, n_alias, split), out_shape=...  56.9 us
    ppermute x62, starting transfers between devices, swap(): return lax.ppermute(a, 'fsdp', [(d, d ^ r) for d in range(n_dev)])  56.3 us
    all_gather x5, waiting for transfers between devices, gather(): return lax.all_gather(a, 'fsdp', axis=0, tiled=True)  48.2 us
    pallas_call x2, Pallas kernels, dx_call(): pl.pallas_call(functools.partial(dx_kernel, stage, layer), out_shape=[jax...  48 us
  transfers between devices with their start and end apart: 67, of which 20 were waited for; matrix products, arithmetic and copies ran while one was open for 0% of the time, Pallas kernels for 58%

profile of v5, /device:TPU:0, one launch (start us, length us, event | category | flops | bytes accessed | tf_op | source)
XLA Modules:
  0.0 1086.7 jit_solution(5851298216808898653)
XLA Ops:
  8.1 76.9 %shard_map.185 = (bf16[384,1024]{1,0:T(8,128)(2,1)}, bf16[384,1024]{1,0:T(8,128)(2,1)}, bf16[384,1024]{1,0:T(8,128)(2,1)}, bf16[384,1024]{1,0:T(8,128)(2,1)}, bf...) custom-call(bf16[2,2,1,2048,1024]{4,3,2,1,0:T(8,128)(2,1)} %refs_1_., ...), custom_call_target="tpu_custom_call" | custom-call | flops 34359738368 | bytes 41943040 | tf_op jit(solution)/shard_map/pallas_call | solution.py:246
  90.5 45.6 %shard_map.186 = (bf16[384,1024]{1,0:T(8,128)(2,1)}, bf16[384,1024]{1,0:T(8,128)(2,1)}, bf16[384,1024]{1,0:T(8,128)(2,1)}, bf16[384,1024]{1,0:T(8,128)(2,1)}, bf...) custom-call(s32[1]{0:T(128)} %bitcast.refs_0_.info, ...), custom_call_target="tpu_custom_call" | custom-call | flops 34359738368 | bytes 41943040 | tf_op jit(solution)/shard_map/pallas_call | solution.py:246
  138.3 23.7 %shard_map.187 = (f32[2048,1024]{1,0:T(8,128)}, f32[2048,1024]{1,0:T(8,128)}) custom-call(s32[1]{0:T(128)} %bitcast.refs_0_.info, bf16[2048,1024]{1,0:T(8,128)(2,1)} %get-tuple-element.137.h0o, bf16[2048,1024]{1,0:T(8,128)(2,1)} %get-tuple-element.138.h0p, bf16[2048,1024]{1,0:T(8,128)(2,1)} %get-tuple-element.141.h1o, ...), custom_call_target="tpu_custom_call" | custom-call | flops 17179869184 | bytes 39845888 | tf_op jit(solution)/shard_map/pallas_call | solution.py:320
  172.3 19.6 %collective-permute-done.49.refs_2_.refs_17_ = bf16[384,1024]{1,0:T(8,128)(2,1)} collective-permute-done((bf16[384,1024]{1,0:T(8,128)(2,1)}, bf16[384,1024]{1,0:T(8,128)(2,1)}, u32[]{:S(2)}, u32[]{:S(2)}) %collective-permute-start.49) | collective-permute-done | bytes 786464 | tf_op jit(solution)/shard_map/ppermute | solution.py:491
  192.4 18.8 %collective-permute-done.51.refs_4_.refs_18_ = bf16[384,1024]{1,0:T(8,128)(2,1)} collective-permute-done((bf16[384,1024]{1,0:T(8,128)(2,1)}, bf16[384,1024]{1,0:T(8,128)(2,1)}, u32[]{:S(2)}, u32[]{:S(2)}) %collective-permute-start.51) | collective-permute-done | bytes 786464 | tf_op jit(solution)/shard_map/ppermute | solution.py:491
  214.7 45.6 %shard_map.181 = (bf16[384,1024]{1,0:T(8,128)(2,1)}, bf16[384,1024]{1,0:T(8,128)(2,1)}, bf16[384,1024]{1,0:T(8,128)(2,1)}, bf16[384,1024]{1,0:T(8,128)(2,1)}, bf...) custom-call(s32[1]{0:T(128)} %bitcast.refs_0_.info, ...), custom_call_target="tpu_custom_call" | custom-call | flops 34359738368 | bytes 41943040 | tf_op jit(solution)/shard_map/pallas_call | solution.py:246
  262.5 46.1 %shard_map.180 = (bf16[384,1024]{1,0:T(8,128)(2,1)}, bf16[384,1024]{1,0:T(8,128)(2,1)}, bf16[384,1024]{1,0:T(8,128)(2,1)}, bf16[384,1024]{1,0:T(8,128)(2,1)}, bf...) custom-call(s32[1]{0:T(128)} %bitcast.refs_0_.info, ...), custom_call_target="tpu_custom_call" | custom-call | flops 34359738368 | bytes 41943040 | tf_op jit(solution)/shard_map/pallas_call | solution.py:246
  313.1 47.4 %shard_map.189 = (bf16[384,1024]{1,0:T(8,128)(2,1)}, bf16[384,1024]{1,0:T(8,128)(2,1)}, bf16[384,1024]{1,0:T(8,128)(2,1)}, bf16[384,1024]{1,0:T(8,128)(2,1)}, bf...) custom-call(s32[1]{0:T(128)} %bitcast.refs_0_.info, ...), custom_call_target="tpu_custom_call" | custom-call | flops 34359738368 | bytes 41943040 | tf_op jit(solution)/shard_map/pallas_call | solution.py:246
  365.0 47.6 %shard_map.188 = (bf16[384,1024]{1,0:T(8,128)(2,1)}, bf16[384,1024]{1,0:T(8,128)(2,1)}, bf16[384,1024]{1,0:T(8,128)(2,1)}, bf16[384,1024]{1,0:T(8,128)(2,1)}, bf...) custom-call(s32[1]{0:T(128)} %bitcast.refs_0_.info, ...), custom_call_target="tpu_custom_call" | custom-call | flops 34359738368 | bytes 41943040 | tf_op jit(solution)/shard_map/pallas_call | solution.py:246
  415.8 10.6 collective-permute-done.31.refs_13_
  436.3 22.9 %collective-permute-done.24.refs_5_ = bf16[128,1024]{1,0:T(8,128)(2,1)S(1)} collective-permute-done((bf16[128,1024]{1,0:T(8,128)(2,1)}, bf16[128,1024]{1,0:T(8,128)(2,1)S(1)}, u32[]{:S(2)}, u32[]{:S(2)}) %collective-permute-start.24) | collective-permute-done | bytes 262176 | tf_op jit(solution)/shard_map/ppermute | solution.py:491
  464.5 15.4 %collective-permute-done.35.refs_2_.refs_17_ = bf16[384,1024]{1,0:T(8,128)(2,1)} collective-permute-done((bf16[384,1024]{1,0:T(8,128)(2,1)}, bf16[384,1024]{1,0:T(8,128)(2,1)}, u32[]{:S(2)}, u32[]{:S(2)}) %collective-permute-start.35) | collective-permute-done | bytes 786464 | tf_op jit(solution)/shard_map/ppermute | solution.py:491
  481.1 16.2 %collective-permute-done.37.refs_4_.refs_18_ = bf16[384,1024]{1,0:T(8,128)(2,1)} collective-permute-done((bf16[384,1024]{1,0:T(8,128)(2,1)}, bf16[384,1024]{1,0:T(8,128)(2,1)}, u32[]{:S(2)}, u32[]{:S(2)}) %collective-permute-start.37) | collective-permute-done | bytes 786464 | tf_op jit(solution)/shard_map/ppermute | solution.py:491
  499.2 14.4 %collective-permute-done.28.refs_10_.refs_21_ = bf16[384,1024]{1,0:T(8,128)(2,1)} collective-permute-done((bf16[384,1024]{1,0:T(8,128)(2,1)}, bf16[384,1024]{1,0:T(8,128)(2,1)}, u32[]{:S(2)}, u32[]{:S(2)}) %collective-permute-start.28) | collective-permute-done | bytes 786464 | tf_op jit(solution)/shard_map/ppermute | solution.py:491
  514.8 14.1 %shard_map.190 = (f32[2,2,128,4096]{3,2,1,0:T(8,128)}, f32[2,2,128,4096]{3,2,1,0:T(8,128)}, f32[2,2,128,4096]{3,2,1,0:T(8,128)}, f32[2,2,2,256,1024]{4,3,2,1,0:T...) custom-call(s32[1]{0:T(128)} %bitcast.refs_0_.info, ...), custom_call_target="tpu_custom_call" | custom-call | flops 838860800 | bytes 41943040 | tf_op jit(solution)/shard_map/pallas_call | solution.py:400
  528.9 14.6 %shard_map.191 = (f32[2,2,128,4096]{3,2,1,0:T(8,128)}, f32[2,2,128,4096]{3,2,1,0:T(8,128)}, f32[2,2,128,4096]{3,2,1,0:T(8,128)}, f32[2,2,2,256,1024]{4,3,2,1,0:T...) custom-call(s32[1]{0:T(128)} %bitcast.refs_0_.info, ...), custom_call_target="tpu_custom_call", output_to_operand_aliasing={{0}: (33, {}), {1}: (34, {}), {2}: (35, {}), {3}: (36, {}),... | custom-call | flops 838860800 | bytes 41943040 | tf_op jit(solution)/shard_map/pallas_call | solution.py:400
  547.4 16.2 %collective-permute-done.23.refs_4_.refs_18_ = bf16[384,1024]{1,0:T(8,128)(2,1)} collective-permute-done((bf16[384,1024]{1,0:T(8,128)(2,1)}, bf16[384,1024]{1,0:T(8,128)(2,1)}, u32[]{:S(2)}, u32[]{:S(2)}) %collective-permute-start.23) | collective-permute-done | bytes 786464 | tf_op jit(solution)/shard_map/ppermute | solution.py:491
  563.5 14.1 %shard_map.192 = (f32[2,2,128,4096]{3,2,1,0:T(8,128)}, f32[2,2,128,4096]{3,2,1,0:T(8,128)}, f32[2,2,128,4096]{3,2,1,0:T(8,128)}, f32[2,2,2,256,1024]{4,3,2,1,0:T...) custom-call(s32[1]{0:T(128)} %bitcast.refs_0_.info, ...), custom_call_target="tpu_custom_call", output_to_operand_aliasing={{0}: (33, {}), {1}: (34, {}), {2}: (35, {}), {3}: (36, {}),... | custom-call | flops 838860800 | bytes 41943040 | tf_op jit(solution)/shard_map/pallas_call | solution.py:400
  578.5 24.3 %shard_map.182 = (f32[2048,1024]{1,0:T(8,128)}, f32[2048,1024]{1,0:T(8,128)}) custom-call(s32[1]{0:T(128)} %bitcast.refs_0_.info, bf16[2048,1024]{1,0:T(8,128)(2,1)} %get-tuple-element.115.h0o, bf16[2048,1024]{1,0:T(8,128)(2,1)} %get-tuple-element.116.h0p, bf16[2048,1024]{1,0:T(8,128)(2,1)} %get-tuple-element.117.h1o, ...), custom_call_target="tpu_custom_call" | custom-call | flops 17179869184 | bytes 39845888 | tf_op jit(solution)/shard_map/pallas_call | solution.py:320
  603.3 16.5 %collective-permute-done.3.refs_10_ = f32[2048,1024]{1,0:T(8,128)} collective-permute-done((f32[2048,1024]{1,0:T(8,128)}, f32[2048,1024]{1,0:T(8,128)}, u32[]{:S(2)}, u32[]{:S(2)}) %collective-permute-start.3) | collective-permute-done | bytes 8388640 | tf_op jit(solution)/shard_map/ppermute | solution.py:491
  619.9 16.3 %collective-permute-done.2.refs_8_ = f32[2048,1024]{1,0:T(8,128)} collective-permute-done((f32[2048,1024]{1,0:T(8,128)}, f32[2048,1024]{1,0:T(8,128)}, u32[]{:S(2)}, u32[]{:S(2)}) %collective-permute-start.2) | collective-permute-done | bytes 8388640 | tf_op jit(solution)/shard_map/ppermute | solution.py:491
  636.2 47.8 %shard_map.184 = (bf16[384,1024]{1,0:T(8,128)(2,1)}, bf16[384,1024]{1,0:T(8,128)(2,1)}, bf16[384,1024]{1,0:T(8,128)(2,1)}, bf16[384,1024]{1,0:T(8,128)(2,1)}, bf...) custom-call(s32[1]{0:T(128)} %bitcast.refs_0_.info, ...), custom_call_target="tpu_custom_call" | custom-call | flops 34359738368 | bytes 41943040 | tf_op jit(solution)/shard_map/pallas_call | solution.py:246
  688.5 47.6 %shard_map.183 = (bf16[384,1024]{1,0:T(8,128)(2,1)}, bf16[384,1024]{1,0:T(8,128)(2,1)}, bf16[384,1024]{1,0:T(8,128)(2,1)}, bf16[384,1024]{1,0:T(8,128)(2,1)}, bf...) custom-call(s32[1]{0:T(128)} %bitcast.refs_0_.info, ...), custom_call_target="tpu_custom_call" | custom-call | flops 34359738368 | bytes 41943040 | tf_op jit(solution)/shard_map/pallas_call | solution.py:246
  764.6 37.2 %collective-permute-done.14.refs_12_.refs_22_ = bf16[384,1024]{1,0:T(8,128)(2,1)} collective-permute-done((bf16[384,1024]{1,0:T(8,128)(2,1)}, bf16[384,1024]{1,0:T(8,128)(2,1)}, u32[]{:S(2)}, u32[]{:S(2)}) %collective-permute-start.14) | collective-permute-done | bytes 786464 | tf_op jit(solution)/shard_map/ppermute | solution.py:491
  801.8 11.7 %collective-permute-done.5.refs_2_.refs_17_ = bf16[384,1024]{1,0:T(8,128)(2,1)} collective-permute-done((bf16[384,1024]{1,0:T(8,128)(2,1)}, bf16[384,1024]{1,0:T(8,128)(2,1)}, u32[]{:S(2)}, u32[]{:S(2)}) %collective-permute-start.5) | collective-permute-done | bytes 786464 | tf_op jit(solution)/shard_map/ppermute | solution.py:491
  813.5 22.0 %collective-permute-done.7.refs_4_.refs_18_ = bf16[384,1024]{1,0:T(8,128)(2,1)} collective-permute-done((bf16[384,1024]{1,0:T(8,128)(2,1)}, bf16[384,1024]{1,0:T(8,128)(2,1)}, u32[]{:S(2)}, u32[]{:S(2)}) %collective-permute-start.7) | collective-permute-done | bytes 786464 | tf_op jit(solution)/shard_map/ppermute | solution.py:491
  835.5 14.1 %shard_map.193 = (f32[2,2,128,4096]{3,2,1,0:T(8,128)}, f32[2,2,128,4096]{3,2,1,0:T(8,128)}, f32[2,2,128,4096]{3,2,1,0:T(8,128)}, f32[2,2,2,256,1024]{4,3,2,1,0:T...) custom-call(s32[1]{0:T(128)} %bitcast.refs_0_.info, ...), custom_call_target="tpu_custom_call", output_to_operand_aliasing={{0}: (33, {}), {1}: (34, {}), {2}: (35, {}), {3}: (36, {}),... | custom-call | flops 838860800 | bytes 41943040 | tf_op jit(solution)/shard_map/pallas_call | solution.py:400
  850.8 45.3 %shard_map.195.refs_0_ = bf16[2048,1024]{1,0:T(8,128)(2,1)} custom-call(bf16[2,1,2048,1024]{3,2,1,0:T(8,128)(2,1)} %refs_0_.5, bf16[8192,1024]{1,0:T(8,128)(2,1)} %all-gather.12.cloned.1.call-done.refs_1_), custom_call_target="tpu_custom_call" | custom-call | flops 34359738368 | bytes 27262976 | tf_op jit(solution)/shard_map/pallas_call | solution.py:470
  896.1 45.2 %shard_map.196.refs_3_ = bf16[2,1,2048,1024]{3,2,1,0:T(8,128)(2,1)} custom-call(bf16[2048,1024]{1,0:T(8,128)(2,1)} %shard_map.195.refs_0_, bf16[8192,1024]{1,0:T(8,128)(2,1)} %all-gather.14.cloned.1.call-done.refs_1_), custom_call_target="tpu_custom_call" | custom-call | flops 34359738368 | bytes 27262976 | tf_op jit(solution)/shard_map/pallas_call | solution.py:470
  941.4 45.2 %shard_map.194.refs_0_ = bf16[2048,1024]{1,0:T(8,128)(2,1)} custom-call(bf16[2,1,2048,1024]{3,2,1,0:T(8,128)(2,1)} %refs_0_.5, bf16[8192,1024]{1,0:T(8,128)(2,1)} %all-gather.6.cloned.1.call-done.refs_1_), custom_call_target="tpu_custom_call" | custom-call | flops 34359738368 | bytes 27262976 | tf_op jit(solution)/shard_map/pallas_call | solution.py:470
  986.6 48.1 %all-gather.10.cloned.1.call-done.refs_2_ = bf16[4096,1024]{1,0:T(8,128)(2,1)} async-done(((bf16[512,1024]{1,0:T(8,128)(2,1)}), bf16[4096,1024]{1,0:T(8,128)(2,1)}) %all-gather.10.cloned.1.call-update) | async-done | bytes 8388624 | tf_op jit(solution)/shard_map/all_gather | solution.py:494
  1034.7 45.0 %shard_map.197 = bf16[2,1,2048,1024]{3,2,1,0:T(8,128)(2,1)} custom-call(bf16[2048,1024]{1,0:T(8,128)(2,1)} %shard_map.194.refs_0_, bf16[4096,1024]{1,0:T(8,128)(2,1)} %all-gather.8.cloned.1.call-done.refs_1_, bf16[4096,1024]{1,0:T(8,128)(2,1)} %all-gather.10.cloned.1.call-done.refs_2_, ...), custom_call_target="tpu_custom_call", output_to_operand_aliasing={{}: (3, {})} | custom-call | flops 34359738368 | bytes 27262976 | tf_op jit(solution)/shard_map/pallas_call | solution.py:470
  (161 shorter events, 95.8 us)
Async XLA Ops:
  7.2 843.6 %all-gather.12.cloned.1.call-start = ((), (), s32[]{:S(2)}) async-start(), calls=%async_computation.3 | async-start | bytes 18874368 | tf_op jit(solution)/shard_map/all_gather | solution.py:494
  7.2 205.9 %collective-permute-start = (bf16[2,2,1,2048,1024]{4,3,2,1,0:T(8,128)(2,1)}, bf16[2,2,1,2048,1024]{4,3,2,1,0:T(8,128)(2,1)}, u32[]{:S(2)}, u32[]{:S(2)}) collective-permute-start(bf16[2,2,1,2048,1024]{4,3,2,1,0:T(8,128)(2,1)} %refs_1_.15), channel_id=1, source_target_pairs={{0,1},{1,0},{2,3},{3,2},{4,5},{5,4},{6,7},{7,6}} | collective-permute-start | bytes 50331656 | tf_op jit(solution)/shard_map/ppermute | solution.py:491
  8.1 204.3 %collective-permute-start.1 = (bf16[2,1,2048,1024]{3,2,1,0:T(8,128)(2,1)}, bf16[2,1,2048,1024]{3,2,1,0:T(8,128)(2,1)}, u32[]{:S(2)}, u32[]{:S(2)}) collective-permute-start(bf16[2,1,2048,1024]{3,2,1,0:T(8,128)(2,1)} %refs_3_.15), channel_id=1, source_target_pairs={{0,1},{1,0},{2,3},{3,2},{4,5},{5,4},{6,7},{7,6}} | collective-permute-start | bytes 25165832 | tf_op jit(solution)/shard_map/ppermute | solution.py:491
  85.4 50.7 %collective-permute-start.50 = (bf16[128,1024]{1,0:T(8,128)(2,1)}, bf16[128,1024]{1,0:T(8,128)(2,1)S(1)}, u32[]{:S(2)}, u32[]{:S(2)}) collective-permute-start(bf16[128,1024]{1,0:T(8,128)(2,1)} %get-tuple-element.180), channel_id=1, source_target_pairs={{0,3},{1,2},{2,1},{3,0},{4,7},{5,6},{6,5},{7,4}} | collective-permute-start | bytes 786440 | tf_op jit(solution)/shard_map/ppermute | solution.py:491
  162.1 147.7 %collective-permute-start.19 = (f32[2048,1024]{1,0:T(8,128)}, f32[2048,1024]{1,0:T(8,128)}, u32[]{:S(2)}, u32[]{:S(2)}) collective-permute-start(f32[2048,1024]{1,0:T(8,128)} %get-tuple-element.143.refs_7_), channel_id=1, source_target_pairs={{0,1},{1,0},{2,3},{3,2},{4,5},{5,4},{6,7},{7,6}} | collective-permute-start | bytes 25165832 | tf_op jit(solution)/shard_map/ppermute | solution.py:491
  162.5 148.6 %collective-permute-start.18 = (f32[2048,1024]{1,0:T(8,128)}, f32[2048,1024]{1,0:T(8,128)}, u32[]{:S(2)}, u32[]{:S(2)}) collective-permute-start(f32[2048,1024]{1,0:T(8,128)} %get-tuple-element.144.refs_9_), channel_id=1, source_target_pairs={{0,1},{1,0},{2,3},{3,2},{4,5},{5,4},{6,7},{7,6}} | collective-permute-start | bytes 25165832 | tf_op jit(solution)/shard_map/ppermute | solution.py:491
  308.5 52.0 %collective-permute-start.45 = (bf16[128,1024]{1,0:T(8,128)(2,1)}, bf16[128,1024]{1,0:T(8,128)(2,1)S(1)}, u32[]{:S(2)}, u32[]{:S(2)}) collective-permute-start(bf16[128,1024]{1,0:T(8,128)(2,1)} %get-tuple-element.174), channel_id=1, source_target_pairs={{0,5},{1,4},{2,7},{3,6},{4,1},{5,0},{6,3},{7,2}} | collective-permute-start | bytes 786440 | tf_op jit(solution)/shard_map/ppermute | solution.py:491
  309.7 52.1 %collective-permute-start.47 = (bf16[128,1024]{1,0:T(8,128)(2,1)}, bf16[128,1024]{1,0:T(8,128)(2,1)}, u32[]{:S(2)}, u32[]{:S(2)}) collective-permute-start(bf16[128,1024]{1,0:T(8,128)(2,1)} %get-tuple-element.176), channel_id=1, source_target_pairs={{0,7},{1,6},{2,5},{3,4},{4,3},{5,2},{6,1},{7,0}} | collective-permute-start | bytes 786440 | tf_op jit(solution)/shard_map/ppermute | solution.py:491
  311.0 52.0 %collective-permute-start.34 = (bf16[128,1024]{1,0:T(8,128)(2,1)}, bf16[128,1024]{1,0:T(8,128)(2,1)}, u32[]{:S(2)}, u32[]{:S(2)}) collective-permute-start(bf16[128,1024]{1,0:T(8,128)(2,1)} %get-tuple-element.162), channel_id=1, source_target_pairs={{0,1},{1,0},{2,3},{3,2},{4,5},{5,4},{6,7},{7,6}} | collective-permute-start | bytes 786440 | tf_op jit(solution)/shard_map/ppermute | solution.py:491
  311.1 53.2 %collective-permute-start.36 = (bf16[128,1024]{1,0:T(8,128)(2,1)}, bf16[128,1024]{1,0:T(8,128)(2,1)}, u32[]{:S(2)}, u32[]{:S(2)}) collective-permute-start(bf16[128,1024]{1,0:T(8,128)(2,1)} %get-tuple-element.164), channel_id=1, source_target_pairs={{0,3},{1,2},{2,1},{3,0},{4,7},{5,6},{6,5},{7,4}} | collective-permute-start | bytes 786440 | tf_op jit(solution)/shard_map/ppermute | solution.py:491
  311.9 53.0 %collective-permute-start.38 = (bf16[128,1024]{1,0:T(8,128)(2,1)}, bf16[128,1024]{1,0:T(8,128)(2,1)}, u32[]{:S(2)}, u32[]{:S(2)}) collective-permute-start(bf16[128,1024]{1,0:T(8,128)(2,1)} %get-tuple-element.166), channel_id=1, source_target_pairs={{0,5},{1,4},{2,7},{3,6},{4,1},{5,0},{6,3},{7,2}} | collective-permute-start | bytes 786440 | tf_op jit(solution)/shard_map/ppermute | solution.py:491
  361.2 99.7 %collective-permute-start.42 = (bf16[384,1024]{1,0:T(8,128)(2,1)}, bf16[384,1024]{1,0:T(8,128)(2,1)S(1)}, u32[]{:S(2)}, u32[]{:S(2)}) collective-permute-start(bf16[384,1024]{1,0:T(8,128)(2,1)} %get-tuple-element.171), channel_id=1, source_target_pairs={{0,2},{1,3},{2,0},{3,1},{4,6},{5,7},{6,4},{7,5}} | collective-permute-start | bytes 2359304 | tf_op jit(solution)/shard_map/ppermute | solution.py:491
  361.8 100.9 %collective-permute-start.44 = (bf16[384,1024]{1,0:T(8,128)(2,1)}, bf16[384,1024]{1,0:T(8,128)(2,1)}, u32[]{:S(2)}, u32[]{:S(2)}) collective-permute-start(bf16[384,1024]{1,0:T(8,128)(2,1)} %get-tuple-element.173), channel_id=1, source_target_pairs={{0,4},{1,5},{2,6},{3,7},{4,0},{5,1},{6,2},{7,3}} | collective-permute-start | bytes 2359304 | tf_op jit(solution)/shard_map/ppermute | solution.py:491
  364.9 50.5 %collective-permute-start.29 = (bf16[128,1024]{1,0:T(8,128)(2,1)}, bf16[128,1024]{1,0:T(8,128)(2,1)}, u32[]{:S(2)}, u32[]{:S(2)}) collective-permute-start(bf16[128,1024]{1,0:T(8,128)(2,1)} %get-tuple-element.156), channel_id=1, source_target_pairs={{0,3},{1,2},{2,1},{3,0},{4,7},{5,6},{6,5},{7,4}} | collective-permute-start | bytes 786440 | tf_op jit(solution)/shard_map/ppermute | solution.py:491
  462.7 50.9 %collective-permute-start.28 = (bf16[384,1024]{1,0:T(8,128)(2,1)}, bf16[384,1024]{1,0:T(8,128)(2,1)}, u32[]{:S(2)}, u32[]{:S(2)}) collective-permute-start(bf16[384,1024]{1,0:T(8,128)(2,1)} %get-tuple-element.155), channel_id=1, source_target_pairs={{0,2},{1,3},{2,0},{3,1},{4,6},{5,7},{6,4},{7,5}} | collective-permute-start | bytes 2359304 | tf_op jit(solution)/shard_map/ppermute | solution.py:491
  463.2 80.3 %collective-permute-start.30 = (bf16[384,1024]{1,0:T(8,128)(2,1)}, bf16[384,1024]{1,0:T(8,128)(2,1)}, u32[]{:S(2)}, u32[]{:S(2)}) collective-permute-start(bf16[384,1024]{1,0:T(8,128)(2,1)} %get-tuple-element.157), channel_id=1, source_target_pairs={{0,4},{1,5},{2,6},{3,7},{4,0},{5,1},{6,2},{7,3}} | collective-permute-start | bytes 2359304 | tf_op jit(solution)/shard_map/ppermute | solution.py:491
  479.8 63.7 %collective-permute-start.32 = (bf16[384,1024]{1,0:T(8,128)(2,1)}, bf16[384,1024]{1,0:T(8,128)(2,1)}, u32[]{:S(2)}, u32[]{:S(2)}) collective-permute-start(bf16[384,1024]{1,0:T(8,128)(2,1)} %get-tuple-element.159), channel_id=1, source_target_pairs={{0,6},{1,7},{2,4},{3,5},{4,2},{5,3},{6,0},{7,1}} | collective-permute-start | bytes 2359304 | tf_op jit(solution)/shard_map/ppermute | solution.py:491
  498.7 64.8 %collective-permute-start.23 = (bf16[384,1024]{1,0:T(8,128)(2,1)}, bf16[384,1024]{1,0:T(8,128)(2,1)}, u32[]{:S(2)}, u32[]{:S(2)}) collective-permute-start(bf16[384,1024]{1,0:T(8,128)(2,1)} %get-tuple-element.149), channel_id=1, source_target_pairs={{0,4},{1,5},{2,6},{3,7},{4,0},{5,1},{6,2},{7,3}} | collective-permute-start | bytes 2359304 | tf_op jit(solution)/shard_map/ppermute | solution.py:491
  577.7 318.5 %all-gather.14.cloned.1.call-start = ((), (), s32[]{:S(2)}) async-start(), calls=%async_computation.4 | async-start | bytes 18874368 | tf_op jit(solution)/shard_map/all_gather | solution.py:494
  578.4 363.0 %all-gather.6.cloned.1.call-start = ((), (), s32[]{:S(2)}) async-start(), calls=%async_computation | async-start | bytes 18874368 | tf_op jit(solution)/shard_map/all_gather | solution.py:494
  684.1 52.1 %collective-permute-start.11 = (bf16[128,1024]{1,0:T(8,128)(2,1)}, bf16[128,1024]{1,0:T(8,128)(2,1)}, u32[]{:S(2)}, u32[]{:S(2)}) collective-permute-start(bf16[128,1024]{1,0:T(8,128)(2,1)} %get-tuple-element.130), channel_id=1, source_target_pairs={{0,1},{1,0},{2,3},{3,2},{4,5},{5,4},{6,7},{7,6}} | collective-permute-start | bytes 786440 | tf_op jit(solution)/shard_map/ppermute | solution.py:491
  684.2 52.0 %collective-permute-start.13 = (bf16[128,1024]{1,0:T(8,128)(2,1)}, bf16[128,1024]{1,0:T(8,128)(2,1)}, u32[]{:S(2)}, u32[]{:S(2)}) collective-permute-start(bf16[128,1024]{1,0:T(8,128)(2,1)} %get-tuple-element.132), channel_id=1, source_target_pairs={{0,3},{1,2},{2,1},{3,0},{4,7},{5,6},{6,5},{7,4}} | collective-permute-start | bytes 786440 | tf_op jit(solution)/shard_map/ppermute | solution.py:491
  685.3 51.9 %collective-permute-start.15 = (bf16[128,1024]{1,0:T(8,128)(2,1)}, bf16[128,1024]{1,0:T(8,128)(2,1)}, u32[]{:S(2)}, u32[]{:S(2)}) collective-permute-start(bf16[128,1024]{1,0:T(8,128)(2,1)} %get-tuple-element.134), channel_id=1, source_target_pairs={{0,5},{1,4},{2,7},{3,6},{4,1},{5,0},{6,3},{7,2}} | collective-permute-start | bytes 786440 | tf_op jit(solution)/shard_map/ppermute | solution.py:491
  685.6 52.2 %collective-permute-start.17 = (bf16[128,1024]{1,0:T(8,128)(2,1)}, bf16[128,1024]{1,0:T(8,128)(2,1)}, u32[]{:S(2)}, u32[]{:S(2)}) collective-permute-start(bf16[128,1024]{1,0:T(8,128)(2,1)} %get-tuple-element.136), channel_id=1, source_target_pairs={{0,7},{1,6},{2,5},{3,4},{4,3},{5,2},{6,1},{7,0}} | collective-permute-start | bytes 786440 | tf_op jit(solution)/shard_map/ppermute | solution.py:491
  687.4 75.9 %collective-permute-start.12 = (bf16[384,1024]{1,0:T(8,128)(2,1)}, bf16[384,1024]{1,0:T(8,128)(2,1)S(1)}, u32[]{:S(2)}, u32[]{:S(2)}) collective-permute-start(bf16[384,1024]{1,0:T(8,128)(2,1)} %get-tuple-element.131), channel_id=1, source_target_pairs={{0,2},{1,3},{2,0},{3,1},{4,6},{5,7},{6,4},{7,5}} | collective-permute-start | bytes 2359304 | tf_op jit(solution)/shard_map/ppermute | solution.py:491
  739.5 62.3 %collective-permute-start.14 = (bf16[384,1024]{1,0:T(8,128)(2,1)}, bf16[384,1024]{1,0:T(8,128)(2,1)}, u32[]{:S(2)}, u32[]{:S(2)}) collective-permute-start(bf16[384,1024]{1,0:T(8,128)(2,1)} %get-tuple-element.133), channel_id=1, source_target_pairs={{0,4},{1,5},{2,6},{3,7},{4,0},{5,1},{6,2},{7,3}} | collective-permute-start | bytes 2359304 | tf_op jit(solution)/shard_map/ppermute | solution.py:491
  750.6 51.2 %collective-permute-start.16 = (bf16[384,1024]{1,0:T(8,128)(2,1)}, bf16[384,1024]{1,0:T(8,128)(2,1)}, u32[]{:S(2)}, u32[]{:S(2)}) collective-permute-start(bf16[384,1024]{1,0:T(8,128)(2,1)} %get-tuple-element.135), channel_id=1, source_target_pairs={{0,6},{1,7},{2,4},{3,5},{4,2},{5,3},{6,0},{7,1}} | collective-permute-start | bytes 2359304 | tf_op jit(solution)/shard_map/ppermute | solution.py:491
  752.6 60.9 %collective-permute-start.5 = (bf16[384,1024]{1,0:T(8,128)(2,1)}, bf16[384,1024]{1,0:T(8,128)(2,1)}, u32[]{:S(2)}, u32[]{:S(2)}) collective-permute-start(bf16[384,1024]{1,0:T(8,128)(2,1)} %get-tuple-element.123), channel_id=1, source_target_pairs={{0,2},{1,3},{2,0},{3,1},{4,6},{5,7},{6,4},{7,5}} | collective-permute-start | bytes 2359304 | tf_op jit(solution)/shard_map/ppermute | solution.py:491
  761.8 73.6 %collective-permute-start.7 = (bf16[384,1024]{1,0:T(8,128)(2,1)}, bf16[384,1024]{1,0:T(8,128)(2,1)}, u32[]{:S(2)}, u32[]{:S(2)}) collective-permute-start(bf16[384,1024]{1,0:T(8,128)(2,1)} %get-tuple-element.125), channel_id=1, source_target_pairs={{0,4},{1,5},{2,6},{3,7},{4,0},{5,1},{6,2},{7,3}} | collective-permute-start | bytes 2359304 | tf_op jit(solution)/shard_map/ppermute | solution.py:491
  763.3 72.1 %collective-permute-start.9 = (bf16[384,1024]{1,0:T(8,128)(2,1)}, bf16[384,1024]{1,0:T(8,128)(2,1)}, u32[]{:S(2)}, u32[]{:S(2)}) collective-permute-start(bf16[384,1024]{1,0:T(8,128)(2,1)} %get-tuple-element.127), channel_id=1, source_target_pairs={{0,6},{1,7},{2,4},{3,5},{4,2},{5,3},{6,0},{7,1}} | collective-permute-start | bytes 2359304 | tf_op jit(solution)/shard_map/ppermute | solution.py:491
  849.6 137.0 %all-gather.8.cloned.1.call-start = ((), (), s32[]{:S(2)}) async-start(), calls=%async_computation.1 | async-start | bytes 9437184 | tf_op jit(solution)/shard_map/all_gather | solution.py:494
  850.2 184.6 %all-gather.10.cloned.1.call-start = ((), (), s32[]{:S(2)}) async-start(), calls=%async_computation.2 | async-start | bytes 9437184 | tf_op jit(solution)/shard_map/all_gather | solution.py:494
  (53 other events, 1594.2 us)
Sparse Core Ops, SparseCore 0:
  577.8 84.1 all-gather.11
  663.8 134.7 all-gather.13
  849.7 84.1 all-gather.5
  935.6 48.6 all-gather.7
  986.0 48.6 all-gather.9
